TPU v7x, 32 devices: a whole 2x2x4 slice. The times are simulated.
32 devices in a mesh: grp: 2 (over y), hist: 4 (over z), chan: 2 (over x), seq: 2 (over core).
Axes of the slice: x: 2, y: 2, z: 4, core: 2. Of those that a mesh axis runs over, the one named last changes fastest.
Arguments:
- history: bfloat16 [16, 2048, 4096], P(('grp', 'seq'), 'hist', 'chan'), parts along dimension 0, may hold values from -6 to 6
- filter_taps: bfloat16 [4096, 4096], P(('grp', 'hist'), 'chan'), parts along dimension 0, may hold values from -0.125 to 0.125
- skip_gain: float32 [8192], P(('grp', 'chan')), parts along dimension 0, may hold values from -4 to 4
- gate_values: bfloat16 [16, 64, 4096], P(('grp', 'seq'), 'hist', 'chan'), parts along dimension 0, may hold values from -6 to 6
Outputs:
- output: bfloat16 [16, 64, 4096], P(('grp', 'seq'), 'hist', 'chan'), parts along dimension 0
There are 2 independent parts, one for each index of `grp`. A program takes and returns all parts, laid end to end along the dimension named above; each array names one. Nothing has to cross between parts.
All inputs are finite; a program needn't handle non-finite values.
Results may differ from a plain program's by a relative error of at most 0.0085.
Values may be sent and summed in bfloat16 or wider, within the bound.
No kernel may reach another device: no remote copies, remote signals or barrier semaphores. Data moves between devices by JAX's collectives and lax.ppermute only.
A program may use at most 192 MiB of HBM per device.

v0:
```python
import math

import jax
import jax.numpy as jnp
from jax import lax
from jax.sharding import PartitionSpec as P

NEW = 64


def from_behind(value, axis, steps):
    count = lax.axis_size(axis)
    first, last = (max(0, -steps), min(count, count - steps))
    return lax.ppermute(value, axis, [(source, source + steps) for source in range(first, last)])


def phase_table(rows, length):
    row_ids = lax.iota(jnp.int32, rows)[:, None]
    col_ids = lax.iota(jnp.int32, length)[None, :]
    phase = row_ids * col_ids % length
    angle = 2.0 * math.pi / length * phase.astype(jnp.float32)
    return (jnp.cos(angle), jnp.sin(angle))


def split_table(table):
    upper = table.astype(jnp.bfloat16)
    lower = (table - upper.astype(jnp.float32)).astype(jnp.bfloat16)
    return (upper, lower)


def forward(data, table, form):
    upper, lower = table
    first = jnp.einsum(form, data, upper, preferred_element_type=jnp.float32)
    return first + jnp.einsum(form, data, lower, preferred_element_type=jnp.float32)


def inverse(spectra, table):
    data_upper, data_lower = split_table(spectra)
    table_upper, table_lower = table
    value = jnp.einsum("kc,ki->ic", data_upper, table_upper, preferred_element_type=jnp.float32)
    value = value + jnp.einsum(
        "kc,ki->ic", data_upper, table_lower, preferred_element_type=jnp.float32
    )
    return value + jnp.einsum(
        "kc,ki->ic", data_lower, table_upper, preferred_element_type=jnp.float32
    )


def body(history, filter_taps, skip_gain, gate_values):
    hist_count = lax.axis_size("hist")
    hist_index = lax.axis_index("hist")
    block_rows = history.shape[1]
    channels = history.shape[2]
    seq_count = history.shape[0]
    length = 2 * NEW
    groups = block_rows // NEW
    tap_rim = from_behind(filter_taps[:NEW], "hist", -1)
    extended = jnp.concatenate([filter_taps, tap_rim], axis=0)
    tap_blocks = jnp.concatenate(
        [
            extended[:block_rows].reshape(groups, NEW, channels),
            extended[NEW:].reshape(groups, NEW, channels),
        ],
        axis=1,
    )
    long_cos, long_sin = phase_table(length, length)
    short_cos, short_sin = phase_table(NEW, length)
    taps_cos = forward(tap_blocks, split_table(long_cos), "qsc,sk->qkc")
    taps_sin = forward(tap_blocks, split_table(long_sin), "qsc,sk->qkc")
    short_cos_parts = split_table(short_cos)
    short_sin_parts = split_table(short_sin)
    freq_ids = lax.iota(jnp.int32, length)[:, None]
    lag_ids = (NEW - 1 - lax.iota(jnp.int32, NEW))[None, :]
    back_angle = 2.0 * math.pi / length * (freq_ids * lag_ids % length).astype(jnp.float32)
    back_table = jnp.concatenate(
        [jnp.cos(back_angle) / length, -jnp.sin(back_angle) / length], axis=0
    )
    back_parts = split_table(back_table)
    rows_out = []
    for seq_id in range(seq_count):
        blocks_in = history[seq_id].reshape(groups, NEW, channels)
        input_cos = forward(blocks_in, short_cos_parts, "qrc,rk->qkc")
        input_sin = forward(blocks_in, short_sin_parts, "qrc,rk->qkc")
        real_part = jnp.sum(input_cos * taps_cos + input_sin * taps_sin, axis=0)
        imag_part = jnp.sum(input_sin * taps_cos - input_cos * taps_sin, axis=0)
        spectra = jnp.concatenate([real_part, imag_part], axis=0)
        rows_out.append(inverse(spectra, back_parts))
    partial_value = jnp.stack(rows_out, axis=0)
    newest_rows = history[:, block_rows - NEW :, :]
    last_flag = (hist_index == hist_count - 1).astype(jnp.float32)
    partial_value = partial_value + last_flag * skip_gain[None, None, :] * newest_rows.astype(
        jnp.float32
    )
    result = lax.psum_scatter(partial_value, "hist", scatter_dimension=1, tiled=True)
    return (gate_values.astype(jnp.float32) * result).astype(jnp.bfloat16)


def solution(mesh):
    placed = (
        P(("grp", "seq"), "hist", "chan"),
        P(("grp", "hist"), "chan"),
        P(("grp", "chan")),
        P(("grp", "seq"), "hist", "chan"),
    )
    return jax.shard_map(
        body,
        mesh=mesh,
        in_specs=placed,
        out_specs=P(("grp", "seq"), "hist", "chan"),
        check_vma=False,
    )
```

profile of v0, /device:TPU:0, one launch (start us, length us, event | category | flops | bytes accessed | tf_op | source)
XLA Modules:
  0.0 205.9 jit_solution(13798787908328344978)
XLA Ops:
  6.5 1.0 slice.22
  7.5 1.3 collective-permute-start
  8.8 3.7 %fusion.192 = (bf16[1,512,2048]{2,1,0:T(8,128)(2,1)S(1)}, bf16[1,512,2048]{2,1,0:T(8,128)(2,1)S(1)}, bf16[1,512,2048]{2,1,0:T(8,128)(2,1)S(1)}, bf16[1,512,2048]{2,1,0:T(8,128)(2,1)S(1)}) fusion(bf16[4,512,2048]{2,1,0:T(8,128)(2,1)} %param.4), kind=kLoop, calls=%fused_computation.212 | loop fusion | bytes 16777216 | tf_op jit(solution)/shard_map/slice | solution.py:81
  12.6 4.7 %fusion.63 = f32[128,8,2048]{2,0,1:T(8,128)} fusion(bf16[8,64,2048]{2,1,0:T(8,128)(2,1)S(1)} %bitcast.106), kind=kOutput, calls=%fused_computation.98 | convolution fusion | flops 268558336 | bytes 10485760 | tf_op jit(solution)/shard_map/qrc,rk->qkc/dot_general | solution.py:33
  17.3 4.6 %fusion.71 = f32[128,8,2048]{2,0,1:T(8,128)} fusion(bf16[8,64,2048]{2,1,0:T(8,128)(2,1)S(1)} %bitcast.107), kind=kOutput, calls=%fused_computation.106 | convolution fusion | flops 268558336 | bytes 10485760 | tf_op jit(solution)/shard_map/qrc,rk->qkc/dot_general | solution.py:33
  21.9 4.6 %fusion.65 = f32[128,8,2048]{2,0,1:T(8,128)} fusion(bf16[8,64,2048]{2,1,0:T(8,128)(2,1)S(1)} %bitcast.102), kind=kOutput, calls=%fused_computation.100 | convolution fusion | flops 268558336 | bytes 10485760 | tf_op jit(solution)/shard_map/qrc,rk->qkc/dot_general | solution.py:33
  26.5 4.6 %fusion.73 = f32[128,8,2048]{2,0,1:T(8,128)} fusion(bf16[8,64,2048]{2,1,0:T(8,128)(2,1)S(1)} %bitcast.103), kind=kOutput, calls=%fused_computation.108 | convolution fusion | flops 268558336 | bytes 10485760 | tf_op jit(solution)/shard_map/qrc,rk->qkc/dot_general | solution.py:33
  31.1 4.6 %fusion.67 = f32[128,8,2048]{2,0,1:T(8,128)} fusion(bf16[8,64,2048]{2,1,0:T(8,128)(2,1)S(1)} %bitcast.94), kind=kOutput, calls=%fused_computation.102 | convolution fusion | flops 268558336 | bytes 10485760 | tf_op jit(solution)/shard_map/qrc,rk->qkc/dot_general | solution.py:33
  35.7 1.4 fusion.75
  37.1 1.4 fusion.77
  38.5 1.4 fusion.69
  39.9 8.1 %convolution_add_fusion = f32[128,8,2048]{2,0,1:T(8,128)} fusion(f32[128,8,2048]{2,0,1:T(8,128)} %fusion.63, bf16[8,64,2048]{2,1,0:T(8,128)(2,1)S(1)} %bitcast.108), kind=kOutput, calls=%fused_computation.8 | convolution fusion | flops 270680064 | bytes 18874368 | tf_op jit(solution)/shard_map/qrc,rk->qkc/dot_general | solution.py:34
  48.1 8.2 %convolution_add_fusion.1 = f32[128,8,2048]{2,0,1:T(8,128)} fusion(f32[128,8,2048]{2,0,1:T(8,128)} %fusion.71, bf16[8,64,2048]{2,1,0:T(8,128)(2,1)S(1)} %bitcast.109), kind=kOutput, calls=%fused_computation.9 | convolution fusion | flops 270680064 | bytes 18874368 | tf_op jit(solution)/shard_map/qrc,rk->qkc/dot_general | solution.py:34
  56.3 8.0 %convolution_add_fusion.2 = f32[128,8,2048]{2,0,1:T(8,128)} fusion(f32[128,8,2048]{2,0,1:T(8,128)} %fusion.65, bf16[8,64,2048]{2,1,0:T(8,128)(2,1)S(1)} %bitcast.104), kind=kOutput, calls=%fused_computation.10 | convolution fusion | flops 270680064 | bytes 18874368 | tf_op jit(solution)/shard_map/qrc,rk->qkc/dot_general | solution.py:34
  64.3 8.0 %convolution_add_fusion.3 = f32[128,8,2048]{2,0,1:T(8,128)} fusion(f32[128,8,2048]{2,0,1:T(8,128)} %fusion.73, bf16[8,64,2048]{2,1,0:T(8,128)(2,1)S(1)} %bitcast.105), kind=kOutput, calls=%fused_computation.11 | convolution fusion | flops 270680064 | bytes 18874368 | tf_op jit(solution)/shard_map/qrc,rk->qkc/dot_general | solution.py:34
  72.3 8.0 %convolution_add_fusion.4 = f32[128,8,2048]{2,0,1:T(8,128)} fusion(f32[128,8,2048]{2,0,1:T(8,128)} %fusion.67, bf16[8,64,2048]{2,1,0:T(8,128)(2,1)S(1)} %bitcast.96), kind=kOutput, calls=%fused_computation.12 | convolution fusion | flops 270680064 | bytes 18874368 | tf_op jit(solution)/shard_map/qrc,rk->qkc/dot_general | solution.py:34
  80.3 4.6 %convolution_add_fusion.5 = f32[128,8,2048]{2,0,1:T(8,128)} fusion(f32[128,8,2048]{2,0,1:T(8,128)S(1)} %fusion.75, bf16[8,64,2048]{2,1,0:T(8,128)(2,1)S(1)} %bitcast.97), kind=kOutput, calls=%fused_computation.13 | convolution fusion | flops 270680064 | bytes 18874368 | tf_op jit(solution)/shard_map/qrc,rk->qkc/dot_general | solution.py:34
  84.9 4.6 %convolution_add_fusion.7 = f32[128,8,2048]{2,0,1:T(8,128)} fusion(f32[128,8,2048]{2,0,1:T(8,128)S(1)} %fusion.77, bf16[8,64,2048]{2,1,0:T(8,128)(2,1)S(1)} %bitcast.92), kind=kOutput, calls=%fused_computation.15 | convolution fusion | flops 270680064 | bytes 18874368 | tf_op jit(solution)/shard_map/qrc,rk->qkc/dot_general | solution.py:34
  89.6 4.6 %convolution_add_fusion.6 = f32[128,8,2048]{2,0,1:T(8,128)} fusion(f32[128,8,2048]{2,0,1:T(8,128)S(1)} %fusion.69, bf16[8,64,2048]{2,1,0:T(8,128)(2,1)S(1)} %bitcast.93), kind=kOutput, calls=%fused_computation.14 | convolution fusion | flops 270680064 | bytes 18874368 | tf_op jit(solution)/shard_map/qrc,rk->qkc/dot_general | solution.py:34
  94.7 1.5 fusion.43
  96.2 4.7 %fusion.41 = f32[128,8,2048]{2,0,1:T(8,128)} fusion(bf16[8,64,2048]{2,1,0:T(8,128)(2,1)S(1)} %bitcast.99, bf16[8,64,2048]{2,1,0:T(8,128)(2,1)S(1)} %bitcast.87), kind=kOutput, calls=%fused_computation.78 | convolution fusion | flops 545505280 | bytes 12582912 | tf_op jit(solution)/shard_map/qsc,sk->qkc/dot_general | solution.py:33
  100.9 4.2 %convolution_add_fusion.9 = f32[128,8,2048]{2,0,1:T(8,128)} fusion(f32[128,8,2048]{2,0,1:T(8,128)S(1)} %fusion.43, bf16[8,64,2048]{2,1,0:T(8,128)(2,1)S(1)} %bitcast.100, bf16[8,64,2048]{2,1,0:T(8,128)(2,1)S(1)} %bitcast.88), kind=kOutput, calls=%fused_computation.17 | convolution fusion | flops 547651584 | bytes 20971520 | tf_op jit(solution)/shard_map/qsc,sk->qkc/dot_general | solution.py:34
  105.1 32.8 %add_reduce_fusion.3 = (f32[128,2048]{1,0:T(8,128)}, f32[128,2048]{1,0:T(8,128)}, f32[128,2048]{1,0:T(8,128)S(1)}, f32[128,2048]{1,0:T(8,128)}, f32[128,2048]{1,...) fusion(f32[128,8,2048]{2,0,1:T(8,128)} %convolution_add_fusion.6, ...), kind=kOutput, calls=%fused_computation.7 | convolution fusion | flops 612663296 | bytes 96468992 | tf_op jit(solution)/shard_map/qsc,sk->qkc/dot_general | solution.py:34
  137.8 2.0 fusion.10
  140.6 0.9 copy-done.5
  141.5 0.3 copy-done.6
  142.8 0.9 copy-done.3
  143.7 0.3 copy-done.4
  144.9 0.9 copy-done.2
  146.8 2.9 %maximum_add_fusion = f32[4,64,2048]{2,1,0:T(8,128)} fusion(f32[1,64,2048]{2,1,0:T(8,128)S(1)} %fusion.3, f32[1,64,2048]{2,1,0:T(8,128)S(1)} %fusion.2, f32[1,64,2048]{2,1,0:T(8,128)S(1)} %fusion.1, f32[1,64,2048]{2,1,0:T(8,128)S(1)} %fusion, bf16[4,512,2048]{2,1,0:T(8,128)(2,1)} %param.4, f32[2048]{0:T(1024)S(1)} %broadcast_multiply_fusion), kind=kLoop, calls=%fused_computation.36 | loop fusion | flops 3145728 | bytes 5251072 | tf_op jit(solution)/shard_map/add | solution.py:91
  149.7 47.6 %reduce-scatter.2.cloned.1.call-done = f32[4,16,2048]{2,1,0:T(8,128)} async-done(((f32[4,64,2048]{2,1,0:T(8,128)}), f32[4,16,2048]{2,1,0:T(8,128)}) %reduce-scatter.2.cloned.1.call-update) | async-done | bytes 524304 | tf_op jit(solution)/shard_map/reduce_scatter | solution.py:94
  197.3 1.8 multiply_convert_fusion
  (36 shorter events, 4.0 us)
Async XLA Ops:
  6.5 190.7 %reduce-scatter.2.cloned.1.call-start = ((), (), s32[]{:S(2)}) async-start(), calls=%async_computation.1 | async-start | bytes 2621440 | tf_op jit(solution)/shard_map/reduce_scatter | solution.py:94
  7.5 87.0 %collective-permute-start = (bf16[64,2048]{1,0:T(8,128)(2,1)S(1)}, bf16[64,2048]{1,0:T(8,128)(2,1)S(1)}, u32[]{:S(2)}, u32[]{:S(2)}) collective-permute-start(bf16[64,2048]{1,0:T(8,128)(2,1)S(1)} %slice.22), channel_id=1, source_target_pairs={{4,0},{8,4},{12,8},{5,1},{9,5},{13,9},{6,2},{10,6},{14,10},{7,3},{... | collective-permute-start | bytes 786440 | tf_op jit(solution)/shard_map/ppermute | solution.py:14
  89.6 4.9 %copy-start.10 = (f32[2048]{0:T(1024)S(1)}, f32[2048]{0:T(1024)}, u32[]{:S(2)}) copy-start(f32[2048]{0:T(1024)} %param.6) | copy-start | bytes 24580
  89.6 4.9 %copy-start = (bf16[512,2048]{1,0:T(8,128)(2,1)S(1)}, bf16[512,2048]{1,0:T(8,128)(2,1)}, u32[]{:S(2)}) copy-start(bf16[512,2048]{1,0:T(8,128)(2,1)} %param.5) | copy-start | bytes 6291460
  94.7 6.2 %copy-start.1 = (bf16[512,2048]{1,0:T(8,128)(2,1)}, bf16[512,2048]{1,0:T(8,128)(2,1)S(1)}, u32[]{:S(2)}) copy-start(bf16[512,2048]{1,0:T(8,128)(2,1)S(1)} %pad_maximum_fusion.1) | copy-start | bytes 6291460
  137.8 2.0 copy-start.7
  137.8 2.2 %copy-start.8 = (f32[128,2048]{1,0:T(8,128)S(1)}, f32[128,2048]{1,0:T(8,128)}, u32[]{:S(2)}) copy-start(f32[128,2048]{1,0:T(8,128)} %get-tuple-element.6) | copy-start | bytes 3145732
  140.3 1.2 copy-start.5
  140.3 1.5 copy-start.6
  142.5 1.2 copy-start.3
  142.5 1.5 copy-start.4
  144.6 1.2 copy-start.2
  149.7 47.6 %copy-start.9 = (bf16[4,16,2048]{2,1,0:T(8,128)(2,1)S(1)}, bf16[4,16,2048]{2,1,0:T(8,128)(2,1)}, u32[]{:S(2)}) copy-start(bf16[4,16,2048]{2,1,0:T(8,128)(2,1)} %param.7) | copy-start | bytes 786436
Sparse Core Ops, SparseCore 0:
  149.8 47.4 reduce-scatter.1
where the time goes:
time: 206 us
  matrix products  130 us (63%)
  waiting for transfers between devices  47.6 us (23%)
  between operations  13.6 us (7%)
  local copies, waits for them, and re-layouts  8.24 us (4%)
  other arithmetic  5.16 us (3%)
    dot_general x10, matrix products, forward(): jnp.einsum(form, data, lower, preferred_element_type=jnp.float32)  91.2 us
    reduce_scatter x1, waiting for transfers between devices, body(): lax.psum_scatter(partial_value, 'hist', scatter_dimension=1, tiled=True)  47.6 us
    dot_general x10, matrix products, forward(): first = jnp.einsum(form, data, upper, preferred_element_type=jnp.float32)  33.5 us
  transfers between devices with their start and end apart: 2, of which 1 were waited for; matrix products, arithmetic and copies ran while one was open for 42% of the time, Pallas kernels for 0%

commit v1 on v0

v1 whole, which is shorter than its diff:
```python
import functools

import jax
import jax.numpy as jnp
import numpy as np
from jax import lax
from jax.experimental import pallas as pl
from jax.experimental.pallas import tpu as pltpu
from jax.sharding import PartitionSpec as P

LANES = 256
BLOCK = 128


def tables(block, new):
    length = block + new
    bins = length // 2
    freq = np.arange(bins)[:, None] + 0.5
    step = 2.0 * np.pi / length

    def pair(positions):
        angle = step * freq * positions[None, :]
        return np.concatenate([np.cos(angle), np.sin(angle)], axis=0)

    taps = pair(np.arange(length))
    back = pair(new - 1 - np.arange(new)).T * (2.0 / length)
    back[:, bins:] *= -1.0
    return taps, back


def conv_body(meta, hist, taps, rim, gain, fwd, back, *outs):
    seqs, rows, lanes = hist.shape
    new = rim.shape[0]
    length = fwd.shape[1]
    block = length - new
    bins = length // 2
    count = rows // block
    share = new // len(outs)
    fwd_taps = fwd[...]
    fwd_hist = fwd[:, :block]
    back_table = back[0]
    flag = (meta[0] == len(outs) - 1).astype(jnp.float32)
    scale = gain[...] * flag
    spectra = []
    for q in range(count):
        if q + 1 < count:
            window = taps[q * block : q * block + length, :]
        else:
            window = jnp.concatenate([taps[q * block :, :], rim[...]], axis=0)
        spectra.append(jnp.dot(fwd_taps, window, preferred_element_type=jnp.float32))
    for b in range(seqs):
        real = jnp.zeros((bins, lanes), jnp.float32)
        imag = jnp.zeros((bins, lanes), jnp.float32)
        for q in range(count):
            data = jnp.dot(
                fwd_hist,
                hist[b, q * block : (q + 1) * block, :],
                preferred_element_type=jnp.float32,
            )
            dc, ds = data[:bins], data[bins:]
            tc, ts = spectra[q][:bins], spectra[q][bins:]
            real = real + (dc * tc + ds * ts)
            imag = imag + (ds * tc - dc * ts)
        both = jnp.concatenate([real, imag], axis=0).astype(jnp.bfloat16)
        part = jnp.dot(back_table, both, preferred_element_type=jnp.float32)
        newest = hist[b, rows - new :, :].astype(jnp.float32)
        for j, out in enumerate(outs):
            first = (j - 1) % len(outs) * share
            direct = scale * newest[first : first + share]
            piece = part[j * share : (j + 1) * share] + direct
            out[b] = piece.astype(out.dtype)


def conv_chunk(meta, history, taps, rim, gain, fwd, back, tiles, ranks):
    seqs, rows, _ = history.shape
    new = rim.shape[0]
    share = new // ranks
    width = tiles * LANES
    shapes = [
        jax.ShapeDtypeStruct((seqs, share, width), jnp.bfloat16 if j else jnp.float32)
        for j in range(ranks)
    ]
    flops = 2 * width * fwd.shape[0] * rows * (seqs + 1)
    spec = pltpu.PrefetchScalarGridSpec(
        num_scalar_prefetch=1,
        grid=(tiles,),
        in_specs=[
            pl.BlockSpec((seqs, rows, LANES), lambda t, m: (0, 0, m[1] + t)),
            pl.BlockSpec((rows, LANES), lambda t, m: (0, m[1] + t)),
            pl.BlockSpec((new, LANES), lambda t, m: (0, m[1] + t)),
            pl.BlockSpec((1, LANES), lambda t, m: (0, m[1] + t)),
            pl.BlockSpec(fwd.shape, lambda t, m: (0, 0)),
            pl.BlockSpec((1,) + back.shape[1:], lambda t, m: (m[0], 0, 0)),
        ],
        out_specs=[
            pl.BlockSpec((seqs, share, LANES), lambda t, m: (0, 0, t)) for _ in shapes
        ],
    )
    return pl.pallas_call(
        conv_body,
        grid_spec=spec,
        out_shape=shapes,
        cost_estimate=pl.CostEstimate(
            flops=flops,
            transcendentals=0,
            bytes_accessed=2 * width * rows * (seqs + 1),
        ),
        name="conv_chunk",
    )(meta, history, taps, rim, gain, fwd, back)


def chunk_tiles(total):
    sizes = []
    left = total
    while left:
        size = min(left, 1 if not sizes else 2)
        sizes.append(size)
        left -= size
    return sizes


def body(history, filter_taps, skip_gain, gate_values):
    ranks = lax.axis_size("hist")
    rank = lax.axis_index("hist").astype(jnp.int32)
    new = gate_values.shape[1] * ranks
    share = gate_values.shape[1]
    channels = history.shape[2]
    block = min(BLOCK, history.shape[1])
    taps_table, back_table = tables(block, new)
    fwd = jnp.asarray(taps_table, jnp.bfloat16)
    turned = np.stack([np.roll(back_table, -share * z, axis=0) for z in range(ranks)])
    back = jnp.asarray(turned, jnp.bfloat16)
    rim = lax.ppermute(
        filter_taps[:new], "hist", [(source, source - 1) for source in range(1, ranks)]
    )
    gain = skip_gain[None, :]
    pieces = []
    start = 0
    for tiles in chunk_tiles(channels // LANES):
        meta = jnp.stack([rank, jnp.int32(start)])
        parts = conv_chunk(meta, history, filter_taps, rim, gain, fwd, back, tiles, ranks)
        total = parts[0]
        for j in range(1, ranks):
            got = lax.ppermute(
                parts[j], "hist", [(source, (source + j) % ranks) for source in range(ranks)]
            )
            total = total + got.astype(jnp.float32)
        lo, hi = start * LANES, (start + tiles) * LANES
        gate = gate_values[:, :, lo:hi].astype(jnp.float32)
        pieces.append((gate * total).astype(jnp.bfloat16))
        start += tiles
    return jnp.concatenate(pieces, axis=2)


def solution(mesh):
    placed = (
        P(("grp", "seq"), "hist", "chan"),
        P(("grp", "hist"), "chan"),
        P(("grp", "chan")),
        P(("grp", "seq"), "hist", "chan"),
    )
    return jax.shard_map(
        body,
        mesh=mesh,
        in_specs=placed,
        out_specs=P(("grp", "seq"), "hist", "chan"),
        check_vma=False,
    )
```

time: 206 us -> 67.7 us (0.33)
  matrix products: 130 us -> 0 us
  waiting for transfers between devices: 47.6 us -> 11.2 us
  starting transfers between devices: 1.29 us -> 26 us
  Pallas kernels: 0 us -> 24.7 us
  between operations: 13.6 us -> 0.21 us
  local copies, waits for them, and re-layouts: 8.24 us -> 1.73 us
    dot_general x32 -> x0, matrix products: 130 us -> none  [the longest x10 91.2 us: forward(): jnp.einsum(form, data, lower, preferred_element_type=jnp.float32)]
    reduce_scatter x1 -> x0, waiting for transfers between devices: 47.6 us -> none  [body(): lax.psum_scatter(partial_value, 'hist', scatter_dimension=1, tiled=True)]
    ppermute x1 -> x16, starting transfers between devices: 1.29 us -> 26 us  [the longest x15 24.7 us: body(): lax.ppermute(parts[j], 'hist', [(source, (source + j) % ranks) for source...]
    pallas_call x0 -> x5, Pallas kernels: none -> 24.7 us  [conv_chunk(): pl.pallas_call(conv_body, grid_spec=spec, out_shape=shapes, cost_estimate...]
    ppermute x1 -> x16, waiting for transfers between devices: 0.01 us -> 11.2 us  [the longest x1 8.09 us: body(): lax.ppermute(filter_taps[:new], 'hist', [(source, source - 1) for source...]
    slice x2 -> x1, local copies, waits for them, and re-layouts: 4.71 us -> 0.97 us  [body(): filter_taps[:new]]
    add x1 -> x0, other arithmetic: 2.91 us -> none  [body(): partial_value + last_flag * skip_gain[None, None, :] * newest_rows.astype...]
    unnamed x22 -> x28, local copies, waits for them, and re-layouts: 3.53 us -> 0.76 us
  transfers between devices with their start and end apart: 2 -> 16, of which waited for: 1 -> 5; matrix products, arithmetic and copies ran while one was open for 42% -> 3% of each run, Pallas kernels for 0% -> 31%
where the time goes in v1:
time: 67.7 us; the launch traced here: 67.3 us
  starting transfers between devices  26 us (38%)
  Pallas kernels  24.7 us (36%)
  waiting for transfers between devices  11.2 us (17%)
  other arithmetic  3.51 us (5%)
  local copies, waits for them, and re-layouts  1.73 us (3%)
    ppermute x15, starting transfers between devices, body(): lax.ppermute(parts[j], 'hist', [(source, (source + j) % ranks) for source...  24.7 us
    pallas_call x5, Pallas kernels, conv_chunk(): pl.pallas_call(conv_body, grid_spec=spec, out_shape=shapes, cost_estimate...  24.7 us
    ppermute x1, waiting for transfers between devices, body(): lax.ppermute(filter_taps[:new], 'hist', [(source, source - 1) for source...  8.09 us
    ppermute x15, waiting for transfers between devices, body(): lax.ppermute(parts[j], 'hist', [(source, (source + j) % ranks) for source...  3.1 us
    another operation x3, other arithmetic, body(): meta = jnp.stack([rank, jnp.int32(start)])  1.86 us
    concatenate x1, other arithmetic, body(): return jnp.concatenate(pieces, axis=2)  1.48 us
  transfers between devices with their start and end apart: 16, of which 5 were waited for; matrix products, arithmetic and copies ran while one was open for 3% of the time, Pallas kernels for 31%

profile of v1, /device:TPU:0, one launch (start us, length us, event | category | flops | bytes accessed | tf_op | source)
XLA Modules:
  0.0 67.3 jit_solution(8683132692881994104)
XLA Ops:
  0.0 1.0 %slice.19 = bf16[64,2048]{1,0:T(8,128)(2,1)S(1)} slice(bf16[512,2048]{1,0:T(8,128)(2,1)} %taps.9), slice={[0:64], [0:2048]} | slice | bytes 524288 | tf_op jit(solution)/shard_map/slice | solution.py:134
  1.0 1.3 %collective-permute-start = (bf16[64,2048]{1,0:T(8,128)(2,1)S(1)}, bf16[64,2048]{1,0:T(8,128)(2,1)S(1)}, u32[]{:S(2)}, u32[]{:S(2)}) collective-permute-start(bf16[64,2048]{1,0:T(8,128)(2,1)S(1)} %slice.19), channel_id=1, source_target_pairs={{4,0},{8,4},{12,8},{5,1},{9,5},{13,9},{6,2},{10,6},{14,10},{7,3},{... | collective-permute-start | bytes 786440 | tf_op jit(solution)/shard_map/ppermute | solution.py:133
  2.3 0.6 pad_add_fusion.4.meta
  2.8 0.7 pad_add_fusion
  3.5 0.7 pad_add_fusion.2
  4.1 8.1 %collective-permute-done.rim = bf16[64,2048]{1,0:T(8,128)(2,1)S(1)} collective-permute-done((bf16[64,2048]{1,0:T(8,128)(2,1)S(1)}, bf16[64,2048]{1,0:T(8,128)(2,1)S(1)}, u32[]{:S(2)}, u32[]{:S(2)}) %collective-permute-start) | collective-permute-done | bytes 262176 | tf_op jit(solution)/shard_map/ppermute | solution.py:133
  12.2 0.7 %copy-done = bf16[64,2048]{1,0:T(8,128)(2,1)} copy-done((bf16[64,2048]{1,0:T(8,128)(2,1)}, bf16[64,2048]{1,0:T(8,128)(2,1)S(1)}, u32[]{:S(2)}) %copy-start) | copy-done | bytes 262168
  12.9 4.0 %conv_chunk.5 = (f32[4,16,256]{2,1,0:T(8,128)}, bf16[4,16,256]{2,1,0:T(8,128)(2,1)}, bf16[4,16,256]{2,1,0:T(8,128)(2,1)}, bf16[4,16,256]{2,1,0:T(8,128)(2,1)}) custom-call(s32[2]{0:T(128)} %get-tuple-element.45.meta, bf16[4,512,2048]{2,1,0:T(8,128)(2,1)} %hist.9, bf16[512,2048]{1,0:T(8,128)(2,1)} %taps.9, bf16[64,2048]{1,0:T(8,128)(2,1)} %copy-done, ...), custom_call_target="tpu_custom_call" | custom-call | flops 251658240 | bytes 1310720 | tf_op jit(solution)/shard_map/conv_chunk/pallas_call | solution.py:99
  16.9 1.7 %collective-permute-start.1 = (bf16[4,16,256]{2,1,0:T(8,128)(2,1)}, bf16[4,16,256]{2,1,0:T(8,128)(2,1)S(1)}, u32[]{:S(2)}, u32[]{:S(2)}) collective-permute-start(bf16[4,16,256]{2,1,0:T(8,128)(2,1)} %get-tuple-element.26), channel_id=1, source_target_pairs={{0,4},{4,8},{8,12},{12,0},{1,5},{5,9},{9,13},{13,1},{2,6},{6,10},{... | collective-permute-start | bytes 98312 | tf_op jit(solution)/shard_map/ppermute | solution.py:144
  18.6 1.1 %collective-permute-start.2 = (bf16[4,16,256]{2,1,0:T(8,128)(2,1)}, bf16[4,16,256]{2,1,0:T(8,128)(2,1)S(1)}, u32[]{:S(2)}, u32[]{:S(2)}) collective-permute-start(bf16[4,16,256]{2,1,0:T(8,128)(2,1)} %get-tuple-element.27), channel_id=1, source_target_pairs={{0,8},{4,12},{8,0},{12,4},{1,9},{5,13},{9,1},{13,5},{2,10},{6,14},... | collective-permute-start | bytes 98312 | tf_op jit(solution)/shard_map/ppermute | solution.py:144
  19.7 2.9 %collective-permute-start.3 = (bf16[4,16,256]{2,1,0:T(8,128)(2,1)}, bf16[4,16,256]{2,1,0:T(8,128)(2,1)S(1)}, u32[]{:S(2)}, u32[]{:S(2)}) collective-permute-start(bf16[4,16,256]{2,1,0:T(8,128)(2,1)} %get-tuple-element.28), channel_id=1, source_target_pairs={{0,12},{4,0},{8,4},{12,8},{1,13},{5,1},{9,5},{13,9},{2,14},{6,2},{... | collective-permute-start | bytes 98312 | tf_op jit(solution)/shard_map/ppermute | solution.py:144
  22.6 5.5 %conv_chunk.6 = (f32[4,16,512]{2,1,0:T(8,128)}, bf16[4,16,512]{2,1,0:T(8,128)(2,1)}, bf16[4,16,512]{2,1,0:T(8,128)(2,1)}, bf16[4,16,512]{2,1,0:T(8,128)(2,1)}) custom-call(s32[2]{0:T(128)} %get-tuple-element.46.meta, bf16[4,512,2048]{2,1,0:T(8,128)(2,1)} %hist.9, bf16[512,2048]{1,0:T(8,128)(2,1)} %taps.9, bf16[64,2048]{1,0:T(8,128)(2,1)} %copy-done, ...), custom_call_target="tpu_custom_call" | custom-call | flops 503316480 | bytes 2621440 | tf_op jit(solution)/shard_map/conv_chunk/pallas_call | solution.py:99
  28.1 1.0 %collective-permute-start.5 = (bf16[4,16,512]{2,1,0:T(8,128)(2,1)}, bf16[4,16,512]{2,1,0:T(8,128)(2,1)S(1)}, u32[]{:S(2)}, u32[]{:S(2)}) collective-permute-start(bf16[4,16,512]{2,1,0:T(8,128)(2,1)} %get-tuple-element.31), channel_id=1, source_target_pairs={{0,8},{4,12},{8,0},{12,4},{1,9},{5,13},{9,1},{13,5},{2,10},{6,14},... | collective-permute-start | bytes 196616 | tf_op jit(solution)/shard_map/ppermute | solution.py:144
  29.1 5.5 %conv_chunk.7 = (f32[4,16,512]{2,1,0:T(8,128)}, bf16[4,16,512]{2,1,0:T(8,128)(2,1)}, bf16[4,16,512]{2,1,0:T(8,128)(2,1)}, bf16[4,16,512]{2,1,0:T(8,128)(2,1)}) custom-call(s32[2]{0:T(128)} %get-tuple-element.47.meta, bf16[4,512,2048]{2,1,0:T(8,128)(2,1)} %hist.9, bf16[512,2048]{1,0:T(8,128)(2,1)} %taps.9, bf16[64,2048]{1,0:T(8,128)(2,1)} %copy-done, ...), custom_call_target="tpu_custom_call" | custom-call | flops 503316480 | bytes 2621440 | tf_op jit(solution)/shard_map/conv_chunk/pallas_call | solution.py:99
  34.7 5.6 %conv_chunk.8 = (f32[4,16,512]{2,1,0:T(8,128)}, bf16[4,16,512]{2,1,0:T(8,128)(2,1)}, bf16[4,16,512]{2,1,0:T(8,128)(2,1)}, bf16[4,16,512]{2,1,0:T(8,128)(2,1)}) custom-call(s32[2]{0:T(128)} %get-tuple-element.48.meta, bf16[4,512,2048]{2,1,0:T(8,128)(2,1)} %hist.9, bf16[512,2048]{1,0:T(8,128)(2,1)} %taps.9, bf16[64,2048]{1,0:T(8,128)(2,1)} %copy-done, ...), custom_call_target="tpu_custom_call" | custom-call | flops 503316480 | bytes 2621440 | tf_op jit(solution)/shard_map/conv_chunk/pallas_call | solution.py:99
  40.3 4.1 %conv_chunk.9 = (f32[4,16,256]{2,1,0:T(8,128)}, bf16[4,16,256]{2,1,0:T(8,128)(2,1)}, bf16[4,16,256]{2,1,0:T(8,128)(2,1)}, bf16[4,16,256]{2,1,0:T(8,128)(2,1)}) custom-call(s32[2]{0:T(128)} %pad_add_fusion.4.meta, bf16[4,512,2048]{2,1,0:T(8,128)(2,1)} %hist.9, bf16[512,2048]{1,0:T(8,128)(2,1)} %taps.9, bf16[64,2048]{1,0:T(8,128)(2,1)} %copy-done, ...), custom_call_target="tpu_custom_call" | custom-call | flops 251658240 | bytes 1310720 | tf_op jit(solution)/shard_map/conv_chunk/pallas_call | solution.py:99
  44.5 2.9 %collective-permute-start.6 = (bf16[4,16,512]{2,1,0:T(8,128)(2,1)S(1)}, bf16[4,16,512]{2,1,0:T(8,128)(2,1)S(1)}, u32[]{:S(2)}, u32[]{:S(2)}) collective-permute-start(bf16[4,16,512]{2,1,0:T(8,128)(2,1)S(1)} %copy-done.13), channel_id=1, source_target_pairs={{0,12},{4,0},{8,4},{12,8},{1,13},{5,1},{9,5},{13,9},{2,14},{6,2},{... | collective-permute-start | bytes 196616 | tf_op jit(solution)/shard_map/ppermute | solution.py:144
  47.3 0.6 collective-permute-start.7
  48.0 1.5 %collective-permute-start.8 = (bf16[4,16,512]{2,1,0:T(8,128)(2,1)S(1)}, bf16[4,16,512]{2,1,0:T(8,128)(2,1)S(1)}, u32[]{:S(2)}, u32[]{:S(2)}) collective-permute-start(bf16[4,16,512]{2,1,0:T(8,128)(2,1)S(1)} %copy-done.11), channel_id=1, source_target_pairs={{0,8},{4,12},{8,0},{12,4},{1,9},{5,13},{9,1},{13,5},{2,10},{6,14},... | collective-permute-start | bytes 196616 | tf_op jit(solution)/shard_map/ppermute | solution.py:144
  49.5 2.9 %collective-permute-start.9 = (bf16[4,16,512]{2,1,0:T(8,128)(2,1)S(1)}, bf16[4,16,512]{2,1,0:T(8,128)(2,1)S(1)}, u32[]{:S(2)}, u32[]{:S(2)}) collective-permute-start(bf16[4,16,512]{2,1,0:T(8,128)(2,1)S(1)} %copy-done.10), channel_id=1, source_target_pairs={{0,12},{4,0},{8,4},{12,8},{1,13},{5,1},{9,5},{13,9},{2,14},{6,2},{... | collective-permute-start | bytes 196616 | tf_op jit(solution)/shard_map/ppermute | solution.py:144
  52.4 1.0 %collective-permute-start.11 = (bf16[4,16,512]{2,1,0:T(8,128)(2,1)S(1)}, bf16[4,16,512]{2,1,0:T(8,128)(2,1)S(1)}, u32[]{:S(2)}, u32[]{:S(2)}) collective-permute-start(bf16[4,16,512]{2,1,0:T(8,128)(2,1)S(1)} %copy-done.8), channel_id=1, source_target_pairs={{0,8},{4,12},{8,0},{12,4},{1,9},{5,13},{9,1},{13,5},{2,10},{6,14},... | collective-permute-start | bytes 196616 | tf_op jit(solution)/shard_map/ppermute | solution.py:144
  53.4 0.2 collective-permute-done.7
  53.6 2.7 %collective-permute-start.12 = (bf16[4,16,512]{2,1,0:T(8,128)(2,1)S(1)}, bf16[4,16,512]{2,1,0:T(8,128)(2,1)S(1)}, u32[]{:S(2)}, u32[]{:S(2)}) collective-permute-start(bf16[4,16,512]{2,1,0:T(8,128)(2,1)S(1)} %copy-done.7), channel_id=1, source_target_pairs={{0,12},{4,0},{8,4},{12,8},{1,13},{5,1},{9,5},{13,9},{2,14},{6,2},{... | collective-permute-start | bytes 196616 | tf_op jit(solution)/shard_map/ppermute | solution.py:144
  56.4 0.7 collective-permute-done.8
  57.0 1.1 %collective-permute-start.13 = (bf16[4,16,256]{2,1,0:T(8,128)(2,1)}, bf16[4,16,256]{2,1,0:T(8,128)(2,1)S(1)}, u32[]{:S(2)}, u32[]{:S(2)}) collective-permute-start(bf16[4,16,256]{2,1,0:T(8,128)(2,1)} %get-tuple-element.42), channel_id=1, source_target_pairs={{0,4},{4,8},{8,12},{12,0},{1,5},{5,9},{9,13},{13,1},{2,6},{6,10},{... | collective-permute-start | bytes 98312 | tf_op jit(solution)/shard_map/ppermute | solution.py:144
  58.1 3.5 %collective-permute-start.14 = (bf16[4,16,256]{2,1,0:T(8,128)(2,1)}, bf16[4,16,256]{2,1,0:T(8,128)(2,1)S(1)}, u32[]{:S(2)}, u32[]{:S(2)}) collective-permute-start(bf16[4,16,256]{2,1,0:T(8,128)(2,1)} %get-tuple-element.43), channel_id=1, source_target_pairs={{0,8},{4,12},{8,0},{12,4},{1,9},{5,13},{9,1},{13,5},{2,10},{6,14},... | collective-permute-start | bytes 98312 | tf_op jit(solution)/shard_map/ppermute | solution.py:144
  61.6 0.1 fusion.1
  61.7 1.9 %collective-permute-start.15 = (bf16[4,16,256]{2,1,0:T(8,128)(2,1)}, bf16[4,16,256]{2,1,0:T(8,128)(2,1)S(1)}, u32[]{:S(2)}, u32[]{:S(2)}) collective-permute-start(bf16[4,16,256]{2,1,0:T(8,128)(2,1)} %get-tuple-element.44), channel_id=1, source_target_pairs={{0,12},{4,0},{8,4},{12,8},{1,13},{5,1},{9,5},{13,9},{2,14},{6,2},{... | collective-permute-start | bytes 98312 | tf_op jit(solution)/shard_map/ppermute | solution.py:144
  63.6 0.1 fusion.2
  63.6 0.1 collective-permute-done.14
  63.7 2.1 %collective-permute-done.15 = bf16[4,16,256]{2,1,0:T(8,128)(2,1)S(1)} collective-permute-done((bf16[4,16,256]{2,1,0:T(8,128)(2,1)}, bf16[4,16,256]{2,1,0:T(8,128)(2,1)S(1)}, u32[]{:S(2)}, u32[]{:S(2)}) %collective-permute-start.15) | collective-permute-done | bytes 32800 | tf_op jit(solution)/shard_map/ppermute | solution.py:144
  65.9 1.5 %fusion.4 = bf16[4,16,2048]{2,1,0:T(8,128)(2,1)} fusion(bf16[4,16,2048]{2,1,0:T(8,128)(2,1)} %copy-done.6, bf16[4,16,256]{2,1,0:T(8,128)(2,1)S(1)} %collective-permute-done.15, bf16[4,16,256]{2,1,0:T(8,128)(2,1)S(1)} %collective-permute-done.14, f32[4,16,256]{2,1,0:T(8,128)} %get-tuple-element.41, bf16[4,16,256]{2,1,0:T(8,128)(2,1)S(1)} %collective-permute-done.13, ...), kind=kLoop, calls=%fused_computation.9 | loop fusion | flops 147456 | bytes 229376 | tf_op jit(solution)/shard_map/concatenate | solution.py:152
  (42 shorter events, 0.2 us)
Async XLA Ops:
  1.0 11.3 %collective-permute-start = (bf16[64,2048]{1,0:T(8,128)(2,1)S(1)}, bf16[64,2048]{1,0:T(8,128)(2,1)S(1)}, u32[]{:S(2)}, u32[]{:S(2)}) collective-permute-start(bf16[64,2048]{1,0:T(8,128)(2,1)S(1)} %slice.19), channel_id=1, source_target_pairs={{4,0},{8,4},{12,8},{5,1},{9,5},{13,9},{6,2},{10,6},{14,10},{7,3},{... | collective-permute-start | bytes 786440 | tf_op jit(solution)/shard_map/ppermute | solution.py:133
  12.2 0.7 %copy-start = (bf16[64,2048]{1,0:T(8,128)(2,1)}, bf16[64,2048]{1,0:T(8,128)(2,1)S(1)}, u32[]{:S(2)}) copy-start(bf16[64,2048]{1,0:T(8,128)(2,1)S(1)} %collective-permute-done.rim) | copy-start | bytes 786436
  16.9 27.6 %collective-permute-start.1 = (bf16[4,16,256]{2,1,0:T(8,128)(2,1)}, bf16[4,16,256]{2,1,0:T(8,128)(2,1)S(1)}, u32[]{:S(2)}, u32[]{:S(2)}) collective-permute-start(bf16[4,16,256]{2,1,0:T(8,128)(2,1)} %get-tuple-element.26), channel_id=1, source_target_pairs={{0,4},{4,8},{8,12},{12,0},{1,5},{5,9},{9,13},{13,1},{2,6},{6,10},{... | collective-permute-start | bytes 98312 | tf_op jit(solution)/shard_map/ppermute | solution.py:144
  18.6 28.7 %collective-permute-start.2 = (bf16[4,16,256]{2,1,0:T(8,128)(2,1)}, bf16[4,16,256]{2,1,0:T(8,128)(2,1)S(1)}, u32[]{:S(2)}, u32[]{:S(2)}) collective-permute-start(bf16[4,16,256]{2,1,0:T(8,128)(2,1)} %get-tuple-element.27), channel_id=1, source_target_pairs={{0,8},{4,12},{8,0},{12,4},{1,9},{5,13},{9,1},{13,5},{2,10},{6,14},... | collective-permute-start | bytes 98312 | tf_op jit(solution)/shard_map/ppermute | solution.py:144
  19.7 28.3 %collective-permute-start.3 = (bf16[4,16,256]{2,1,0:T(8,128)(2,1)}, bf16[4,16,256]{2,1,0:T(8,128)(2,1)S(1)}, u32[]{:S(2)}, u32[]{:S(2)}) collective-permute-start(bf16[4,16,256]{2,1,0:T(8,128)(2,1)} %get-tuple-element.28), channel_id=1, source_target_pairs={{0,12},{4,0},{8,4},{12,8},{1,13},{5,1},{9,5},{13,9},{2,14},{6,2},{... | collective-permute-start | bytes 98312 | tf_op jit(solution)/shard_map/ppermute | solution.py:144
  28.1 21.4 %collective-permute-start.4 = (bf16[4,16,512]{2,1,0:T(8,128)(2,1)}, bf16[4,16,512]{2,1,0:T(8,128)(2,1)S(1)}, u32[]{:S(2)}, u32[]{:S(2)}) collective-permute-start(bf16[4,16,512]{2,1,0:T(8,128)(2,1)} %get-tuple-element.30), channel_id=1, source_target_pairs={{0,4},{4,8},{8,12},{12,0},{1,5},{5,9},{9,13},{13,1},{2,6},{6,10},{... | collective-permute-start | bytes 196616 | tf_op jit(solution)/shard_map/ppermute | solution.py:144
  28.1 24.3 %collective-permute-start.5 = (bf16[4,16,512]{2,1,0:T(8,128)(2,1)}, bf16[4,16,512]{2,1,0:T(8,128)(2,1)S(1)}, u32[]{:S(2)}, u32[]{:S(2)}) collective-permute-start(bf16[4,16,512]{2,1,0:T(8,128)(2,1)} %get-tuple-element.31), channel_id=1, source_target_pairs={{0,8},{4,12},{8,0},{12,4},{1,9},{5,13},{9,1},{13,5},{2,10},{6,14},... | collective-permute-start | bytes 196616 | tf_op jit(solution)/shard_map/ppermute | solution.py:144
  34.6 9.9 %copy-start.13 = (bf16[4,16,512]{2,1,0:T(8,128)(2,1)S(1)}, bf16[4,16,512]{2,1,0:T(8,128)(2,1)}, u32[]{:S(2)}) copy-start(bf16[4,16,512]{2,1,0:T(8,128)(2,1)} %get-tuple-element.32) | copy-start | bytes 196612
  34.6 12.7 %copy-start.12 = (bf16[4,16,512]{2,1,0:T(8,128)(2,1)S(1)}, bf16[4,16,512]{2,1,0:T(8,128)(2,1)}, u32[]{:S(2)}) copy-start(bf16[4,16,512]{2,1,0:T(8,128)(2,1)} %get-tuple-element.34) | copy-start | bytes 196612
  34.6 13.3 %copy-start.11 = (bf16[4,16,512]{2,1,0:T(8,128)(2,1)S(1)}, bf16[4,16,512]{2,1,0:T(8,128)(2,1)}, u32[]{:S(2)}) copy-start(bf16[4,16,512]{2,1,0:T(8,128)(2,1)} %get-tuple-element.35) | copy-start | bytes 196612
  34.6 14.8 %copy-start.1 = (bf16[4,16,2048]{2,1,0:T(8,128)(2,1)S(1)}, bf16[4,16,2048]{2,1,0:T(8,128)(2,1)}, u32[]{:S(2)}) copy-start(bf16[4,16,2048]{2,1,0:T(8,128)(2,1)} %param.9) | copy-start | bytes 786436
  34.6 14.8 %copy-start.5 = (f32[4,16,256]{2,1,0:T(8,128)S(1)}, f32[4,16,256]{2,1,0:T(8,128)}, u32[]{:S(2)}) copy-start(f32[4,16,256]{2,1,0:T(8,128)} %get-tuple-element.25) | copy-start | bytes 196612
  34.7 14.8 %copy-start.10 = (bf16[4,16,512]{2,1,0:T(8,128)(2,1)S(1)}, bf16[4,16,512]{2,1,0:T(8,128)(2,1)}, u32[]{:S(2)}) copy-start(bf16[4,16,512]{2,1,0:T(8,128)(2,1)} %get-tuple-element.36) | copy-start | bytes 196612
  34.7 18.7 %copy-start.4 = (f32[4,16,512]{2,1,0:T(8,128)S(1)}, f32[4,16,512]{2,1,0:T(8,128)}, u32[]{:S(2)}) copy-start(f32[4,16,512]{2,1,0:T(8,128)} %get-tuple-element.29) | copy-start | bytes 393220
  40.3 12.1 %copy-start.9 = (bf16[4,16,512]{2,1,0:T(8,128)(2,1)S(1)}, bf16[4,16,512]{2,1,0:T(8,128)(2,1)}, u32[]{:S(2)}) copy-start(bf16[4,16,512]{2,1,0:T(8,128)(2,1)} %get-tuple-element.38) | copy-start | bytes 196612
  40.3 12.1 %copy-start.8 = (bf16[4,16,512]{2,1,0:T(8,128)(2,1)S(1)}, bf16[4,16,512]{2,1,0:T(8,128)(2,1)}, u32[]{:S(2)}) copy-start(bf16[4,16,512]{2,1,0:T(8,128)(2,1)} %get-tuple-element.39) | copy-start | bytes 196612
  40.3 13.3 %copy-start.7 = (bf16[4,16,512]{2,1,0:T(8,128)(2,1)S(1)}, bf16[4,16,512]{2,1,0:T(8,128)(2,1)}, u32[]{:S(2)}) copy-start(bf16[4,16,512]{2,1,0:T(8,128)(2,1)} %get-tuple-element.40) | copy-start | bytes 196612
  40.3 21.3 %copy-start.3 = (f32[4,16,512]{2,1,0:T(8,128)S(1)}, f32[4,16,512]{2,1,0:T(8,128)}, u32[]{:S(2)}) copy-start(f32[4,16,512]{2,1,0:T(8,128)} %get-tuple-element.33) | copy-start | bytes 393220
  40.3 23.2 %copy-start.2 = (f32[4,16,512]{2,1,0:T(8,128)S(1)}, f32[4,16,512]{2,1,0:T(8,128)}, u32[]{:S(2)}) copy-start(f32[4,16,512]{2,1,0:T(8,128)} %get-tuple-element.37) | copy-start | bytes 393220
  44.5 7.9 %collective-permute-start.6 = (bf16[4,16,512]{2,1,0:T(8,128)(2,1)S(1)}, bf16[4,16,512]{2,1,0:T(8,128)(2,1)S(1)}, u32[]{:S(2)}, u32[]{:S(2)}) collective-permute-start(bf16[4,16,512]{2,1,0:T(8,128)(2,1)S(1)} %copy-done.13), channel_id=1, source_target_pairs={{0,12},{4,0},{8,4},{12,8},{1,13},{5,1},{9,5},{13,9},{2,14},{6,2},{... | collective-permute-start | bytes 196616 | tf_op jit(solution)/shard_map/ppermute | solution.py:144
  47.3 6.3 %collective-permute-start.7 = (bf16[4,16,512]{2,1,0:T(8,128)(2,1)S(1)}, bf16[4,16,512]{2,1,0:T(8,128)(2,1)S(1)}, u32[]{:S(2)}, u32[]{:S(2)}) collective-permute-start(bf16[4,16,512]{2,1,0:T(8,128)(2,1)S(1)} %copy-done.12), channel_id=1, source_target_pairs={{0,4},{4,8},{8,12},{12,0},{1,5},{5,9},{9,13},{13,1},{2,6},{6,10},{... | collective-permute-start | bytes 196616 | tf_op jit(solution)/shard_map/ppermute | solution.py:144
  48.0 9.1 %collective-permute-start.8 = (bf16[4,16,512]{2,1,0:T(8,128)(2,1)S(1)}, bf16[4,16,512]{2,1,0:T(8,128)(2,1)S(1)}, u32[]{:S(2)}, u32[]{:S(2)}) collective-permute-start(bf16[4,16,512]{2,1,0:T(8,128)(2,1)S(1)} %copy-done.11), channel_id=1, source_target_pairs={{0,8},{4,12},{8,0},{12,4},{1,9},{5,13},{9,1},{13,5},{2,10},{6,14},... | collective-permute-start | bytes 196616 | tf_op jit(solution)/shard_map/ppermute | solution.py:144
  49.5 8.6 %collective-permute-start.9 = (bf16[4,16,512]{2,1,0:T(8,128)(2,1)S(1)}, bf16[4,16,512]{2,1,0:T(8,128)(2,1)S(1)}, u32[]{:S(2)}, u32[]{:S(2)}) collective-permute-start(bf16[4,16,512]{2,1,0:T(8,128)(2,1)S(1)} %copy-done.10), channel_id=1, source_target_pairs={{0,12},{4,0},{8,4},{12,8},{1,13},{5,1},{9,5},{13,9},{2,14},{6,2},{... | collective-permute-start | bytes 196616 | tf_op jit(solution)/shard_map/ppermute | solution.py:144
  52.4 9.3 %collective-permute-start.10 = (bf16[4,16,512]{2,1,0:T(8,128)(2,1)S(1)}, bf16[4,16,512]{2,1,0:T(8,128)(2,1)S(1)}, u32[]{:S(2)}, u32[]{:S(2)}) collective-permute-start(bf16[4,16,512]{2,1,0:T(8,128)(2,1)S(1)} %copy-done.9), channel_id=1, source_target_pairs={{0,4},{4,8},{8,12},{12,0},{1,5},{5,9},{9,13},{13,1},{2,6},{6,10},{... | collective-permute-start | bytes 196616 | tf_op jit(solution)/shard_map/ppermute | solution.py:144
  52.4 11.2 %collective-permute-start.11 = (bf16[4,16,512]{2,1,0:T(8,128)(2,1)S(1)}, bf16[4,16,512]{2,1,0:T(8,128)(2,1)S(1)}, u32[]{:S(2)}, u32[]{:S(2)}) collective-permute-start(bf16[4,16,512]{2,1,0:T(8,128)(2,1)S(1)} %copy-done.8), channel_id=1, source_target_pairs={{0,8},{4,12},{8,0},{12,4},{1,9},{5,13},{9,1},{13,5},{2,10},{6,14},... | collective-permute-start | bytes 196616 | tf_op jit(solution)/shard_map/ppermute | solution.py:144
  53.6 9.9 %collective-permute-start.12 = (bf16[4,16,512]{2,1,0:T(8,128)(2,1)S(1)}, bf16[4,16,512]{2,1,0:T(8,128)(2,1)S(1)}, u32[]{:S(2)}, u32[]{:S(2)}) collective-permute-start(bf16[4,16,512]{2,1,0:T(8,128)(2,1)S(1)} %copy-done.7), channel_id=1, source_target_pairs={{0,12},{4,0},{8,4},{12,8},{1,13},{5,1},{9,5},{13,9},{2,14},{6,2},{... | collective-permute-start | bytes 196616 | tf_op jit(solution)/shard_map/ppermute | solution.py:144
  57.0 6.6 %collective-permute-start.13 = (bf16[4,16,256]{2,1,0:T(8,128)(2,1)}, bf16[4,16,256]{2,1,0:T(8,128)(2,1)S(1)}, u32[]{:S(2)}, u32[]{:S(2)}) collective-permute-start(bf16[4,16,256]{2,1,0:T(8,128)(2,1)} %get-tuple-element.42), channel_id=1, source_target_pairs={{0,4},{4,8},{8,12},{12,0},{1,5},{5,9},{9,13},{13,1},{2,6},{6,10},{... | collective-permute-start | bytes 98312 | tf_op jit(solution)/shard_map/ppermute | solution.py:144
  58.1 5.6 %collective-permute-start.14 = (bf16[4,16,256]{2,1,0:T(8,128)(2,1)}, bf16[4,16,256]{2,1,0:T(8,128)(2,1)S(1)}, u32[]{:S(2)}, u32[]{:S(2)}) collective-permute-start(bf16[4,16,256]{2,1,0:T(8,128)(2,1)} %get-tuple-element.43), channel_id=1, source_target_pairs={{0,8},{4,12},{8,0},{12,4},{1,9},{5,13},{9,1},{13,5},{2,10},{6,14},... | collective-permute-start | bytes 98312 | tf_op jit(solution)/shard_map/ppermute | solution.py:144
  61.7 4.2 %collective-permute-start.15 = (bf16[4,16,256]{2,1,0:T(8,128)(2,1)}, bf16[4,16,256]{2,1,0:T(8,128)(2,1)S(1)}, u32[]{:S(2)}, u32[]{:S(2)}) collective-permute-start(bf16[4,16,256]{2,1,0:T(8,128)(2,1)} %get-tuple-element.44), channel_id=1, source_target_pairs={{0,12},{4,0},{8,4},{12,8},{1,13},{5,1},{9,5},{13,9},{2,14},{6,2},{... | collective-permute-start | bytes 98312 | tf_op jit(solution)/shard_map/ppermute | solution.py:144
  63.6 2.2 %copy-start.6 = (bf16[4,16,2048]{2,1,0:T(8,128)(2,1)}, bf16[4,16,2048]{2,1,0:T(8,128)(2,1)S(1)}, u32[]{:S(2)}) copy-start(bf16[4,16,2048]{2,1,0:T(8,128)(2,1)S(1)} %fusion.2) | copy-start | bytes 786436

commit v2 on v1

v2 whole, which is shorter than its diff:
```python
import functools

import jax
import jax.numpy as jnp
import numpy as np
from jax import lax
from jax.experimental import pallas as pl
from jax.experimental.pallas import tpu as pltpu
from jax.sharding import PartitionSpec as P


LANES = 256
BLOCK = 128


def tables(block, new):
    length = block + new
    bins = length // 2
    freq = np.arange(bins)[:, None] + 0.5
    step = 2.0 * np.pi / length

    def pair(positions):
        angle = step * freq * positions[None, :]
        return np.concatenate([np.cos(angle), np.sin(angle)], axis=0)

    taps = pair(np.arange(length))
    back = pair(new - 1 - np.arange(new)).T * (2.0 / length)
    back[:, bins:] *= -1.0
    return taps, back


def conv_body(meta, hist, taps, gain, fwd, back, rim, keep, send, *, base, rim_base, owners):
    seqs, rows, _ = hist.shape
    new = rim.shape[0]
    length = fwd.shape[1]
    block = length - new
    bins = length // 2
    count = rows // block
    share = new // len(owners)
    flag = (meta[0] == len(owners) - 1).astype(jnp.float32)

    def tile(t, carry):
        here = pl.ds(pl.multiple_of((base + t) * LANES, LANES), LANES)
        there = pl.ds(pl.multiple_of(t * LANES, LANES), LANES)
        rim_at = pl.ds(pl.multiple_of((base - rim_base + t) * LANES, LANES), LANES)
        fwd_taps = fwd[...]
        fwd_hist = fwd[:, :block]
        back_table = back[meta[0]]
        scale = gain[:, here] * flag
        spectra = []
        for q in range(count):
            if q + 1 < count:
                window = taps[q * block : q * block + length, here]
            else:
                window = jnp.concatenate([taps[q * block :, here], rim[:, rim_at]], axis=0)
            spectra.append(jnp.dot(fwd_taps, window, preferred_element_type=jnp.float32))
        for b in range(seqs):
            real = jnp.zeros((bins, LANES), jnp.float32)
            imag = jnp.zeros((bins, LANES), jnp.float32)
            for q in range(count):
                data = jnp.dot(
                    fwd_hist,
                    hist[b, q * block : (q + 1) * block, here],
                    preferred_element_type=jnp.float32,
                )
                dc, ds = data[:bins], data[bins:]
                tc, ts = spectra[q][:bins], spectra[q][bins:]
                real = real + (dc * tc + ds * ts)
                imag = imag + (ds * tc - dc * ts)
            both = jnp.concatenate([real, imag], axis=0).astype(jnp.bfloat16)
            part = jnp.dot(back_table, both, preferred_element_type=jnp.float32)
            newest = hist[b, rows - new :, here].astype(jnp.float32)
            for k, owner in enumerate(owners):
                direct = scale * newest[owner * share : (owner + 1) * share]
                piece = part[k * share : (k + 1) * share] + direct
                out = keep if k < len(owners) // 2 else send
                at = k % max(1, len(owners) // 2) * share
                out[b, at : at + share, there] = piece.astype(out.dtype)
        return carry

    lax.fori_loop(0, keep.shape[2] // LANES, tile, 0)


def stage_body(*refs):
    count = len(refs) // 2
    arrays, copies, done = refs[:count], refs[count:-1], refs[-1]
    moves = [
        pltpu.make_async_copy(arrays[i], copies[i], done.at[i]) for i in range(count)
    ]
    for move in moves:
        move.start()
    for move in moves:
        move.wait()


def stage(*arrays):
    return pl.pallas_call(
        stage_body,
        in_specs=[pl.BlockSpec(memory_space=pltpu.HBM)] * len(arrays),
        out_specs=[pl.BlockSpec(memory_space=pltpu.VMEM)] * len(arrays),
        out_shape=[pltpu.VMEM(a.shape, a.dtype) for a in arrays],
        scratch_shapes=[pltpu.SemaphoreType.DMA((len(arrays),))],
        compiler_params=pltpu.CompilerParams(vmem_limit_bytes=16 << 20),
        name="stage",
    )(*[pltpu.with_memory_space_constraint(a, pltpu.HBM) for a in arrays])


def conv_chunk(meta, staged, rim, base, rim_base, tiles, owners):
    history, _, _, fwd, _ = staged
    seqs, rows, _ = history.shape
    half = rim.shape[0] // 2
    width = tiles * LANES
    vmem = pl.BlockSpec(memory_space=pltpu.VMEM)
    return pl.pallas_call(
        functools.partial(conv_body, base=base, rim_base=rim_base, owners=owners),
        in_specs=[pl.BlockSpec(memory_space=pltpu.SMEM)] + [vmem] * 6,
        out_specs=[vmem] * 2,
        out_shape=[
            jax.ShapeDtypeStruct((seqs, half, width), jnp.float32),
            jax.ShapeDtypeStruct((seqs, half, width), jnp.bfloat16),
        ],
        cost_estimate=pl.CostEstimate(
            flops=2 * width * fwd.shape[0] * rows * (seqs + 1),
            transcendentals=0,
            bytes_accessed=2 * width * rows * (seqs + 1),
        ),
        compiler_params=pltpu.CompilerParams(vmem_limit_bytes=16 << 20),
        name="conv_chunk",
    )(meta, *staged, rim)


def chunk_tiles(total):
    sizes = []
    left = total
    while left:
        size = min(left, 1 if not sizes else 2)
        sizes.append(size)
        left -= size
    return sizes


def swapped(ranks):
    order = [0]
    step = ranks // 2
    while step:
        order += [step ^ value for value in order]
        step //= 2
    return order


def exchange(value, bit, ranks):
    return lax.ppermute(value, "hist", [(z, z ^ bit) for z in range(ranks)])


def body(history, filter_taps, skip_gain, gate_values):
    ranks = lax.axis_size("hist")
    rank = lax.axis_index("hist").astype(jnp.int32)
    share = gate_values.shape[1]
    new = share * ranks
    channels = history.shape[2]
    block = min(BLOCK, history.shape[1])
    taps_table, back_table = tables(block, new)
    fwd = jnp.asarray(taps_table, jnp.bfloat16)
    order = swapped(ranks)
    by_owner = back_table.reshape(ranks, share, -1)
    turned = np.stack(
        [np.concatenate([by_owner[z ^ j] for j in order]) for z in range(ranks)]
    )
    back = jnp.asarray(turned, jnp.bfloat16)
    owners = [(ranks - 1) ^ j for j in order]
    meta = rank[None]
    sizes = chunk_tiles(channels // LANES)
    toward = [(source, source - 1) for source in range(1, ranks)]
    split = sizes[0] * LANES
    rims = []
    for part in (slice(0, split), slice(split, None)):
        rims.append(lax.ppermute(filter_taps[:new, part], "hist", toward))
    staged = stage(history, filter_taps, skip_gain[None, :], fwd, back)
    pieces = []
    start = 0
    for index, tiles in enumerate(sizes):
        keep, send = conv_chunk(
            meta,
            staged,
            rims[min(index, 1)],
            start,
            sizes[0] if index else 0,
            tiles,
            owners,
        )
        bit = 1
        while bit < ranks:
            got = exchange(send, bit, ranks)
            total = keep + got.astype(jnp.float32)
            half = total.shape[1] // 2
            keep, send = total[:, :half], total[:, half:].astype(jnp.bfloat16)
            bit *= 2
        lo, hi = start * LANES, (start + tiles) * LANES
        gate = gate_values[:, :, lo:hi].astype(jnp.float32)
        pieces.append((gate * total).astype(jnp.bfloat16))
        start += tiles
    return jnp.concatenate(pieces, axis=2)


def solution(mesh):
    placed = (
        P(("grp", "seq"), "hist", "chan"),
        P(("grp", "hist"), "chan"),
        P(("grp", "chan")),
        P(("grp", "seq"), "hist", "chan"),
    )
    return jax.shard_map(
        body,
        mesh=mesh,
        in_specs=placed,
        out_specs=P(("grp", "seq"), "hist", "chan"),
        check_vma=False,
    )
```

time: 67.7 us -> 52.1 us (0.77)
  Pallas kernels: 24.7 us -> 14.8 us
  starting transfers between devices: 26 us -> 18.1 us
  waiting for transfers between devices: 11.2 us -> 15.5 us
  other arithmetic: 3.51 us -> 0.83 us
  local copies, waits for them, and re-layouts: 1.73 us -> 2.46 us
    pallas_call x5 -> x6, Pallas kernels: 24.7 us -> 14.8 us  [the longest x5 10.8 us: conv_chunk(): pl.pallas_call(functools.partial(conv_body, base=base, rim_base=rim_base,...]
    ppermute x16 -> x12, starting transfers between devices: 26 us -> 18.1 us  [the longest x10 15.5 us: exchange(): return lax.ppermute(value, 'hist', [(z, z ^ bit) for z in range(ranks)])]
    ppermute x16 -> x12, waiting for transfers between devices: 11.2 us -> 15.5 us  [the longest x2 8.06 us: body(): rims.append(lax.ppermute(filter_taps[:new, part], 'hist', toward))]
    another operation x3 -> x0, other arithmetic: 1.86 us -> none  [body(): meta = jnp.stack([rank, jnp.int32(start)])]
    concatenate x1, other arithmetic: 1.48 us -> 0.63 us  [body(): return jnp.concatenate(pieces, axis=2)]
    slice x1 -> x7, local copies, waits for them, and re-layouts: 0.97 us -> 1.76 us  [the longest x2 1.71 us: body(): rims.append(lax.ppermute(filter_taps[:new, part], 'hist', toward))]
  transfers between devices with their start and end apart: 16 -> 12, of which waited for: 5 -> 7; matrix products, arithmetic and copies ran while one was open for 3% -> 2% of each run, Pallas kernels for 31% -> 21%
where the time goes in v2:
time: 52.1 us; the launch traced here: 51.9 us
  starting transfers between devices  18.1 us (35%)
  waiting for transfers between devices  15.5 us (30%)
  Pallas kernels  14.8 us (28%)
  local copies, waits for them, and re-layouts  2.46 us (5%)
  other arithmetic  0.83 us (2%)
    ppermute x10, starting transfers between devices, exchange(): return lax.ppermute(value, 'hist', [(z, z ^ bit) for z in range(ranks)])  15.5 us
    pallas_call x5, Pallas kernels, conv_chunk(): pl.pallas_call(functools.partial(conv_body, base=base, rim_base=rim_base,...  10.8 us
    ppermute x2, waiting for transfers between devices, body(): rims.append(lax.ppermute(filter_taps[:new, part], 'hist', toward))  8.06 us
    ppermute x10, waiting for transfers between devices, exchange(): return lax.ppermute(value, 'hist', [(z, z ^ bit) for z in range(ranks)])  7.42 us
    pallas_call x1, Pallas kernels, stage(): pl.pallas_call(stage_body, in_specs=[pl.BlockSpec(memory_space=pltpu.HBM)...  4.03 us
    ppermute x2, starting transfers between devices, body(): rims.append(lax.ppermute(filter_taps[:new, part], 'hist', toward))  2.57 us
    slice x2, local copies, waits for them, and re-layouts, body(): rims.append(lax.ppermute(filter_taps[:new, part], 'hist', toward))  1.71 us
  transfers between devices with their start and end apart: 12, of which 7 were waited for; matrix products, arithmetic and copies ran while one was open for 2% of the time, Pallas kernels for 21%

profile of v2, /device:TPU:0, one launch (start us, length us, event | category | flops | bytes accessed | tf_op | source)
XLA Modules:
  0.0 51.9 jit_solution(17327261927933773431)
XLA Ops:
  0.0 0.8 %slice.57 = bf16[64,256]{1,0:T(8,128)(2,1)S(1)} slice(bf16[512,2048]{1,0:T(8,128)(2,1)} %refs_1_.1), slice={[0:64], [0:256]} | slice | bytes 65536 | tf_op jit(solution)/shard_map/slice | solution.py:177
  0.8 1.3 %collective-permute-start = (bf16[64,256]{1,0:T(8,128)(2,1)S(1)}, bf16[64,256]{1,0:T(8,128)(2,1)S(1)}, u32[]{:S(2)}, u32[]{:S(2)}) collective-permute-start(bf16[64,256]{1,0:T(8,128)(2,1)S(1)} %slice.57), channel_id=1, source_target_pairs={{4,0},{8,4},{12,8},{5,1},{9,5},{13,9},{6,2},{10,6},{14,10},{7,3},{... | collective-permute-start | bytes 98312 | tf_op jit(solution)/shard_map/ppermute | solution.py:177
  2.1 4.0 %stage.1 = (bf16[4,512,2048]{2,1,0:T(8,128)(2,1)S(1)}, bf16[512,2048]{1,0:T(8,128)(2,1)S(1)}, f32[1,2048]{1,0:T(1,128)S(1)}, bf16[192,192]{1,0:T(8,128)(2,1)S(1)}, bf16[4,64,192]{2,1,0:T(8,128)(2,1)S(1)}) custom-call(bf16[4,512,2048]{2,1,0:T(8,128)(2,1)} %refs_0_.1, bf16[512,2048]{1,0:T(8,128)(2,1)} %refs_1_.1, f32[1,2048]{1,0:T(1,128)} %bitcast.2, ...), custom_call_target="tpu_custom_call" | custom-call | tf_op jit(solution)/shard_map/stage/pallas_call | solution.py:97
  6.1 0.0 copy-start
  6.1 1.5 %collective-permute-done.rim = bf16[64,256]{1,0:T(8,128)(2,1)S(1)} collective-permute-done((bf16[64,256]{1,0:T(8,128)(2,1)S(1)}, bf16[64,256]{1,0:T(8,128)(2,1)S(1)}, u32[]{:S(2)}, u32[]{:S(2)}) %collective-permute-start) | collective-permute-done | bytes 32800 | tf_op jit(solution)/shard_map/ppermute | solution.py:177
  7.6 1.4 %conv_chunk.5 = (f32[4,32,256]{2,1,0:T(8,128)S(1)}, bf16[4,32,256]{2,1,0:T(8,128)(2,1)S(1)}) custom-call(s32[1]{0:T(128)} %bitcast.meta, bf16[4,512,2048]{2,1,0:T(8,128)(2,1)S(1)} %get-tuple-element.20.hist, bf16[512,2048]{1,0:T(8,128)(2,1)S(1)} %get-tuple-element.21.taps, f32[1,2048]{1,0:T(1,128)S(1)} %get-tuple-element.22.gain, ...), custom_call_target="tpu_custom_call" | custom-call | flops 251658240 | bytes 1310720 | tf_op jit(solution)/shard_map/conv_chunk/pallas_call | solution.py:114
  9.0 2.3 %collective-permute-start.1 = (bf16[4,32,256]{2,1,0:T(8,128)(2,1)S(1)}, bf16[4,32,256]{2,1,0:T(8,128)(2,1)S(1)}, u32[]{:S(2)}, u32[]{:S(2)}) collective-permute-start(bf16[4,32,256]{2,1,0:T(8,128)(2,1)S(1)} %get-tuple-element.26), channel_id=1, source_target_pairs={{0,4},{4,0},{8,12},{12,8},{1,5},{5,1},{9,13},{13,9},{2,6},{6,2},{1... | collective-permute-start | bytes 196616 | tf_op jit(solution)/shard_map/ppermute | solution.py:152
  11.2 2.2 %collective-permute-done.1 = bf16[4,32,256]{2,1,0:T(8,128)(2,1)S(1)} collective-permute-done((bf16[4,32,256]{2,1,0:T(8,128)(2,1)S(1)}, bf16[4,32,256]{2,1,0:T(8,128)(2,1)S(1)}, u32[]{:S(2)}, u32[]{:S(2)}) %collective-permute-start.1) | collective-permute-done | bytes 65568 | tf_op jit(solution)/shard_map/ppermute | solution.py:152
  13.5 3.5 %collective-permute-start.2 = (bf16[4,16,256]{2,1,0:T(8,128)(2,1)S(1)}, bf16[4,16,256]{2,1,0:T(8,128)(2,1)S(1)}, u32[]{:S(2)}, u32[]{:S(2)}) collective-permute-start(bf16[4,16,256]{2,1,0:T(8,128)(2,1)S(1)} %slice.132), channel_id=1, source_target_pairs={{0,8},{4,12},{8,0},{12,4},{1,9},{5,13},{9,1},{13,5},{2,10},{6,14},... | collective-permute-start | bytes 98312 | tf_op jit(solution)/shard_map/ppermute | solution.py:152
  17.0 1.0 %slice.61 = bf16[64,1792]{1,0:T(8,128)(2,1)S(1)} slice(bf16[512,2048]{1,0:T(8,128)(2,1)} %refs_1_.1), slice={[0:64], [256:2048]} | slice | bytes 458752 | tf_op jit(solution)/shard_map/slice | solution.py:177
  18.0 1.3 %collective-permute-start.3 = (bf16[64,1792]{1,0:T(8,128)(2,1)S(1)}, bf16[64,1792]{1,0:T(8,128)(2,1)S(1)}, u32[]{:S(2)}, u32[]{:S(2)}) collective-permute-start(bf16[64,1792]{1,0:T(8,128)(2,1)S(1)} %slice.61), channel_id=1, source_target_pairs={{4,0},{8,4},{12,8},{5,1},{9,5},{13,9},{6,2},{10,6},{14,10},{7,3},{... | collective-permute-start | bytes 688136 | tf_op jit(solution)/shard_map/ppermute | solution.py:177
  19.3 6.6 %collective-permute-done.3.rim = bf16[64,1792]{1,0:T(8,128)(2,1)S(1)} collective-permute-done((bf16[64,1792]{1,0:T(8,128)(2,1)S(1)}, bf16[64,1792]{1,0:T(8,128)(2,1)S(1)}, u32[]{:S(2)}, u32[]{:S(2)}) %collective-permute-start.3) | collective-permute-done | bytes 229408 | tf_op jit(solution)/shard_map/ppermute | solution.py:177
  25.9 2.7 %conv_chunk.6 = (f32[4,32,512]{2,1,0:T(8,128)S(1)}, bf16[4,32,512]{2,1,0:T(8,128)(2,1)S(1)}) custom-call(s32[1]{0:T(128)} %bitcast.meta, bf16[4,512,2048]{2,1,0:T(8,128)(2,1)S(1)} %get-tuple-element.20.hist, bf16[512,2048]{1,0:T(8,128)(2,1)S(1)} %get-tuple-element.21.taps, f32[1,2048]{1,0:T(1,128)S(1)} %get-tuple-element.22.gain, ...), custom_call_target="tpu_custom_call" | custom-call | flops 503316480 | bytes 2621440 | tf_op jit(solution)/shard_map/conv_chunk/pallas_call | solution.py:114
  28.6 1.6 %collective-permute-start.4 = (bf16[4,32,512]{2,1,0:T(8,128)(2,1)S(1)}, bf16[4,32,512]{2,1,0:T(8,128)(2,1)S(1)}, u32[]{:S(2)}, u32[]{:S(2)}) collective-permute-start(bf16[4,32,512]{2,1,0:T(8,128)(2,1)S(1)} %get-tuple-element.28), channel_id=1, source_target_pairs={{0,4},{4,0},{8,12},{12,8},{1,5},{5,1},{9,13},{13,9},{2,6},{6,2},{1... | collective-permute-start | bytes 393224 | tf_op jit(solution)/shard_map/ppermute | solution.py:152
  30.3 1.3 %conv_chunk.9 = (f32[4,32,256]{2,1,0:T(8,128)S(1)}, bf16[4,32,256]{2,1,0:T(8,128)(2,1)S(1)}) custom-call(s32[1]{0:T(128)} %bitcast.meta, bf16[4,512,2048]{2,1,0:T(8,128)(2,1)S(1)} %get-tuple-element.20.hist, bf16[512,2048]{1,0:T(8,128)(2,1)S(1)} %get-tuple-element.21.taps, f32[1,2048]{1,0:T(1,128)S(1)} %get-tuple-element.22.gain, ...), custom_call_target="tpu_custom_call" | custom-call | flops 251658240 | bytes 1310720 | tf_op jit(solution)/shard_map/conv_chunk/pallas_call | solution.py:114
  31.6 0.5 collective-permute-start.10
  32.1 2.7 %conv_chunk.7 = (f32[4,32,512]{2,1,0:T(8,128)S(1)}, bf16[4,32,512]{2,1,0:T(8,128)(2,1)S(1)}) custom-call(s32[1]{0:T(128)} %bitcast.meta, bf16[4,512,2048]{2,1,0:T(8,128)(2,1)S(1)} %get-tuple-element.20.hist, bf16[512,2048]{1,0:T(8,128)(2,1)S(1)} %get-tuple-element.21.taps, f32[1,2048]{1,0:T(1,128)S(1)} %get-tuple-element.22.gain, ...), custom_call_target="tpu_custom_call" | custom-call | flops 503316480 | bytes 2621440 | tf_op jit(solution)/shard_map/conv_chunk/pallas_call | solution.py:114
  34.8 1.6 %collective-permute-start.6 = (bf16[4,32,512]{2,1,0:T(8,128)(2,1)S(1)}, bf16[4,32,512]{2,1,0:T(8,128)(2,1)S(1)}, u32[]{:S(2)}, u32[]{:S(2)}) collective-permute-start(bf16[4,32,512]{2,1,0:T(8,128)(2,1)S(1)} %get-tuple-element.30), channel_id=1, source_target_pairs={{0,4},{4,0},{8,12},{12,8},{1,5},{5,1},{9,13},{13,9},{2,6},{6,2},{1... | collective-permute-start | bytes 393224 | tf_op jit(solution)/shard_map/ppermute | solution.py:152
  36.5 2.7 %conv_chunk.8 = (f32[4,32,512]{2,1,0:T(8,128)S(1)}, bf16[4,32,512]{2,1,0:T(8,128)(2,1)S(1)}) custom-call(s32[1]{0:T(128)} %bitcast.meta, bf16[4,512,2048]{2,1,0:T(8,128)(2,1)S(1)} %get-tuple-element.20.hist, bf16[512,2048]{1,0:T(8,128)(2,1)S(1)} %get-tuple-element.21.taps, f32[1,2048]{1,0:T(1,128)S(1)} %get-tuple-element.22.gain, ...), custom_call_target="tpu_custom_call" | custom-call | flops 503316480 | bytes 2621440 | tf_op jit(solution)/shard_map/conv_chunk/pallas_call | solution.py:114
  39.2 0.5 collective-permute-start.8
  39.7 0.0 collective-permute-done.10
  39.7 0.6 %collective-permute-start.11 = (bf16[4,16,256]{2,1,0:T(8,128)(2,1)S(1)}, bf16[4,16,256]{2,1,0:T(8,128)(2,1)S(1)}, u32[]{:S(2)}, u32[]{:S(2)}) collective-permute-start(bf16[4,16,256]{2,1,0:T(8,128)(2,1)S(1)} %slice.131), channel_id=1, source_target_pairs={{0,8},{4,12},{8,0},{12,4},{1,9},{5,13},{9,1},{13,5},{2,10},{6,14},... | collective-permute-start | bytes 98312 | tf_op jit(solution)/shard_map/ppermute | solution.py:152
  40.4 2.4 %collective-permute-start.5 = (bf16[4,16,512]{2,1,0:T(8,128)(2,1)S(1)}, bf16[4,16,512]{2,1,0:T(8,128)(2,1)S(1)}, u32[]{:S(2)}, u32[]{:S(2)}) collective-permute-start(bf16[4,16,512]{2,1,0:T(8,128)(2,1)S(1)} %slice.130), channel_id=1, source_target_pairs={{0,8},{4,12},{8,0},{12,4},{1,9},{5,13},{9,1},{13,5},{2,10},{6,14},... | collective-permute-start | bytes 196616 | tf_op jit(solution)/shard_map/ppermute | solution.py:152
  42.9 0.6 %collective-permute-start.7 = (bf16[4,16,512]{2,1,0:T(8,128)(2,1)S(1)}, bf16[4,16,512]{2,1,0:T(8,128)(2,1)S(1)}, u32[]{:S(2)}, u32[]{:S(2)}) collective-permute-start(bf16[4,16,512]{2,1,0:T(8,128)(2,1)S(1)} %slice.129), channel_id=1, source_target_pairs={{0,8},{4,12},{8,0},{12,4},{1,9},{5,13},{9,1},{13,5},{2,10},{6,14},... | collective-permute-start | bytes 196616 | tf_op jit(solution)/shard_map/ppermute | solution.py:152
  43.5 0.7 %collective-permute-done.8 = bf16[4,32,512]{2,1,0:T(8,128)(2,1)S(1)} collective-permute-done((bf16[4,32,512]{2,1,0:T(8,128)(2,1)S(1)}, bf16[4,32,512]{2,1,0:T(8,128)(2,1)S(1)}, u32[]{:S(2)}, u32[]{:S(2)}) %collective-permute-start.8) | collective-permute-done | bytes 131104 | tf_op jit(solution)/shard_map/ppermute | solution.py:152
  44.3 1.8 %collective-permute-start.9 = (bf16[4,16,512]{2,1,0:T(8,128)(2,1)S(1)}, bf16[4,16,512]{2,1,0:T(8,128)(2,1)S(1)}, u32[]{:S(2)}, u32[]{:S(2)}) collective-permute-start(bf16[4,16,512]{2,1,0:T(8,128)(2,1)S(1)} %slice.128), channel_id=1, source_target_pairs={{0,8},{4,12},{8,0},{12,4},{1,9},{5,13},{9,1},{13,5},{2,10},{6,14},... | collective-permute-start | bytes 196616 | tf_op jit(solution)/shard_map/ppermute | solution.py:152
  46.0 1.2 %collective-permute-done.5 = bf16[4,16,512]{2,1,0:T(8,128)(2,1)S(1)} collective-permute-done((bf16[4,16,512]{2,1,0:T(8,128)(2,1)S(1)}, bf16[4,16,512]{2,1,0:T(8,128)(2,1)S(1)}, u32[]{:S(2)}, u32[]{:S(2)}) %collective-permute-start.5) | collective-permute-done | bytes 65568 | tf_op jit(solution)/shard_map/ppermute | solution.py:152
  47.3 0.9 %collective-permute-done.7 = bf16[4,16,512]{2,1,0:T(8,128)(2,1)S(1)} collective-permute-done((bf16[4,16,512]{2,1,0:T(8,128)(2,1)S(1)}, bf16[4,16,512]{2,1,0:T(8,128)(2,1)S(1)}, u32[]{:S(2)}, u32[]{:S(2)}) %collective-permute-start.7) | collective-permute-done | bytes 65568 | tf_op jit(solution)/shard_map/ppermute | solution.py:152
  48.2 2.4 %collective-permute-done.9 = bf16[4,16,512]{2,1,0:T(8,128)(2,1)S(1)} collective-permute-done((bf16[4,16,512]{2,1,0:T(8,128)(2,1)S(1)}, bf16[4,16,512]{2,1,0:T(8,128)(2,1)S(1)}, u32[]{:S(2)}, u32[]{:S(2)}) %collective-permute-start.9) | collective-permute-done | bytes 65568 | tf_op jit(solution)/shard_map/ppermute | solution.py:152
  50.6 0.0 copy-start.1
  50.6 0.7 %copy-done.1 = bf16[4,16,2048]{2,1,0:T(8,128)(2,1)} copy-done((bf16[4,16,2048]{2,1,0:T(8,128)(2,1)}, bf16[4,16,2048]{2,1,0:T(8,128)(2,1)S(1)}, u32[]{:S(2)}) %copy-start.1) | copy-done | bytes 262168
  51.3 0.6 %fusion.14 = bf16[4,16,2048]{2,1,0:T(8,128)(2,1)} fusion(bf16[4,16,2048]{2,1,0:T(8,128)(2,1)} %copy-done.1, bf16[4,16,256]{2,1,0:T(8,128)(2,1)S(1)} %collective-permute-done.11, f32[4,32,256]{2,1,0:T(8,128)S(1)} %convert_add_fusion.3, bf16[4,16,2048]{2,1,0:T(8,128)(2,1)S(1)} %copy-done), kind=kLoop, calls=%fused_computation.29 | loop fusion | flops 81920 | bytes 163840 | tf_op jit(solution)/shard_map/concatenate | solution.py:202
  (19 shorter events, 0.3 us)
Async XLA Ops:
  0.8 6.8 %collective-permute-start = (bf16[64,256]{1,0:T(8,128)(2,1)S(1)}, bf16[64,256]{1,0:T(8,128)(2,1)S(1)}, u32[]{:S(2)}, u32[]{:S(2)}) collective-permute-start(bf16[64,256]{1,0:T(8,128)(2,1)S(1)} %slice.57), channel_id=1, source_target_pairs={{4,0},{8,4},{12,8},{5,1},{9,5},{13,9},{6,2},{10,6},{14,10},{7,3},{... | collective-permute-start | bytes 98312 | tf_op jit(solution)/shard_map/ppermute | solution.py:177
  6.1 13.2 %copy-start = (bf16[4,16,2048]{2,1,0:T(8,128)(2,1)S(1)}, bf16[4,16,2048]{2,1,0:T(8,128)(2,1)}, u32[]{:S(2)}) copy-start(bf16[4,16,2048]{2,1,0:T(8,128)(2,1)} %param.9) | copy-start | bytes 786436
  9.0 4.5 %collective-permute-start.1 = (bf16[4,32,256]{2,1,0:T(8,128)(2,1)S(1)}, bf16[4,32,256]{2,1,0:T(8,128)(2,1)S(1)}, u32[]{:S(2)}, u32[]{:S(2)}) collective-permute-start(bf16[4,32,256]{2,1,0:T(8,128)(2,1)S(1)} %get-tuple-element.26), channel_id=1, source_target_pairs={{0,4},{4,0},{8,12},{12,8},{1,5},{5,1},{9,13},{13,9},{2,6},{6,2},{1... | collective-permute-start | bytes 196616 | tf_op jit(solution)/shard_map/ppermute | solution.py:152
  13.5 5.8 %collective-permute-start.2 = (bf16[4,16,256]{2,1,0:T(8,128)(2,1)S(1)}, bf16[4,16,256]{2,1,0:T(8,128)(2,1)S(1)}, u32[]{:S(2)}, u32[]{:S(2)}) collective-permute-start(bf16[4,16,256]{2,1,0:T(8,128)(2,1)S(1)} %slice.132), channel_id=1, source_target_pairs={{0,8},{4,12},{8,0},{12,4},{1,9},{5,13},{9,1},{13,5},{2,10},{6,14},... | collective-permute-start | bytes 98312 | tf_op jit(solution)/shard_map/ppermute | solution.py:152
  18.0 7.9 %collective-permute-start.3 = (bf16[64,1792]{1,0:T(8,128)(2,1)S(1)}, bf16[64,1792]{1,0:T(8,128)(2,1)S(1)}, u32[]{:S(2)}, u32[]{:S(2)}) collective-permute-start(bf16[64,1792]{1,0:T(8,128)(2,1)S(1)} %slice.61), channel_id=1, source_target_pairs={{4,0},{8,4},{12,8},{5,1},{9,5},{13,9},{6,2},{10,6},{14,10},{7,3},{... | collective-permute-start | bytes 688136 | tf_op jit(solution)/shard_map/ppermute | solution.py:177
  28.6 11.7 %collective-permute-start.4 = (bf16[4,32,512]{2,1,0:T(8,128)(2,1)S(1)}, bf16[4,32,512]{2,1,0:T(8,128)(2,1)S(1)}, u32[]{:S(2)}, u32[]{:S(2)}) collective-permute-start(bf16[4,32,512]{2,1,0:T(8,128)(2,1)S(1)} %get-tuple-element.28), channel_id=1, source_target_pairs={{0,4},{4,0},{8,12},{12,8},{1,5},{5,1},{9,13},{13,9},{2,6},{6,2},{1... | collective-permute-start | bytes 393224 | tf_op jit(solution)/shard_map/ppermute | solution.py:152
  31.6 8.1 %collective-permute-start.10 = (bf16[4,32,256]{2,1,0:T(8,128)(2,1)S(1)}, bf16[4,32,256]{2,1,0:T(8,128)(2,1)S(1)}, u32[]{:S(2)}, u32[]{:S(2)}) collective-permute-start(bf16[4,32,256]{2,1,0:T(8,128)(2,1)S(1)} %get-tuple-element.34), channel_id=1, source_target_pairs={{0,4},{4,0},{8,12},{12,8},{1,5},{5,1},{9,13},{13,9},{2,6},{6,2},{1... | collective-permute-start | bytes 196616 | tf_op jit(solution)/shard_map/ppermute | solution.py:152
  34.8 8.0 %collective-permute-start.6 = (bf16[4,32,512]{2,1,0:T(8,128)(2,1)S(1)}, bf16[4,32,512]{2,1,0:T(8,128)(2,1)S(1)}, u32[]{:S(2)}, u32[]{:S(2)}) collective-permute-start(bf16[4,32,512]{2,1,0:T(8,128)(2,1)S(1)} %get-tuple-element.30), channel_id=1, source_target_pairs={{0,4},{4,0},{8,12},{12,8},{1,5},{5,1},{9,13},{13,9},{2,6},{6,2},{1... | collective-permute-start | bytes 393224 | tf_op jit(solution)/shard_map/ppermute | solution.py:152
  39.2 5.0 %collective-permute-start.8 = (bf16[4,32,512]{2,1,0:T(8,128)(2,1)S(1)}, bf16[4,32,512]{2,1,0:T(8,128)(2,1)S(1)}, u32[]{:S(2)}, u32[]{:S(2)}) collective-permute-start(bf16[4,32,512]{2,1,0:T(8,128)(2,1)S(1)} %get-tuple-element.32), channel_id=1, source_target_pairs={{0,4},{4,0},{8,12},{12,8},{1,5},{5,1},{9,13},{13,9},{2,6},{6,2},{1... | collective-permute-start | bytes 393224 | tf_op jit(solution)/shard_map/ppermute | solution.py:152
  39.7 10.9 %collective-permute-start.11 = (bf16[4,16,256]{2,1,0:T(8,128)(2,1)S(1)}, bf16[4,16,256]{2,1,0:T(8,128)(2,1)S(1)}, u32[]{:S(2)}, u32[]{:S(2)}) collective-permute-start(bf16[4,16,256]{2,1,0:T(8,128)(2,1)S(1)} %slice.131), channel_id=1, source_target_pairs={{0,8},{4,12},{8,0},{12,4},{1,9},{5,13},{9,1},{13,5},{2,10},{6,14},... | collective-permute-start | bytes 98312 | tf_op jit(solution)/shard_map/ppermute | solution.py:152
  40.4 6.8 %collective-permute-start.5 = (bf16[4,16,512]{2,1,0:T(8,128)(2,1)S(1)}, bf16[4,16,512]{2,1,0:T(8,128)(2,1)S(1)}, u32[]{:S(2)}, u32[]{:S(2)}) collective-permute-start(bf16[4,16,512]{2,1,0:T(8,128)(2,1)S(1)} %slice.130), channel_id=1, source_target_pairs={{0,8},{4,12},{8,0},{12,4},{1,9},{5,13},{9,1},{13,5},{2,10},{6,14},... | collective-permute-start | bytes 196616 | tf_op jit(solution)/shard_map/ppermute | solution.py:152
  42.9 5.2 %collective-permute-start.7 = (bf16[4,16,512]{2,1,0:T(8,128)(2,1)S(1)}, bf16[4,16,512]{2,1,0:T(8,128)(2,1)S(1)}, u32[]{:S(2)}, u32[]{:S(2)}) collective-permute-start(bf16[4,16,512]{2,1,0:T(8,128)(2,1)S(1)} %slice.129), channel_id=1, source_target_pairs={{0,8},{4,12},{8,0},{12,4},{1,9},{5,13},{9,1},{13,5},{2,10},{6,14},... | collective-permute-start | bytes 196616 | tf_op jit(solution)/shard_map/ppermute | solution.py:152
  44.3 6.3 %collective-permute-start.9 = (bf16[4,16,512]{2,1,0:T(8,128)(2,1)S(1)}, bf16[4,16,512]{2,1,0:T(8,128)(2,1)S(1)}, u32[]{:S(2)}, u32[]{:S(2)}) collective-permute-start(bf16[4,16,512]{2,1,0:T(8,128)(2,1)S(1)} %slice.128), channel_id=1, source_target_pairs={{0,8},{4,12},{8,0},{12,4},{1,9},{5,13},{9,1},{13,5},{2,10},{6,14},... | collective-permute-start | bytes 196616 | tf_op jit(solution)/shard_map/ppermute | solution.py:152
  50.6 0.7 %copy-start.1 = (bf16[4,16,2048]{2,1,0:T(8,128)(2,1)}, bf16[4,16,2048]{2,1,0:T(8,128)(2,1)S(1)}, u32[]{:S(2)}) copy-start(bf16[4,16,2048]{2,1,0:T(8,128)(2,1)S(1)} %fusion.8) | copy-start | bytes 786436

commit v3 on v2

--- a/solution.py
+++ b/solution.py
@@ -11,6 +11,8 @@
 
 LANES = 256
 BLOCK = 128
+CHUNKS = 3
+GROUP = 16
 
 
 def tables(block, new):
@@ -29,7 +31,9 @@
     return taps, back
 
 
-def conv_body(meta, hist, taps, gain, fwd, back, rim, keep, send, *, base, rim_base, owners):
+def conv_body(
+    meta, hist, taps, gain, fwd, back, rim, keep, send, spectra, *, base, rim_base, owners
+):
     seqs, rows, _ = hist.shape
     new = rim.shape[0]
     length = fwd.shape[1]
@@ -47,28 +51,34 @@
         fwd_hist = fwd[:, :block]
         back_table = back[meta[0]]
         scale = gain[:, here] * flag
-        spectra = []
-        for q in range(count):
-            if q + 1 < count:
-                window = taps[q * block : q * block + length, here]
-            else:
-                window = jnp.concatenate([taps[q * block :, here], rim[:, rim_at]], axis=0)
-            spectra.append(jnp.dot(fwd_taps, window, preferred_element_type=jnp.float32))
-        for b in range(seqs):
-            real = jnp.zeros((bins, LANES), jnp.float32)
-            imag = jnp.zeros((bins, LANES), jnp.float32)
-            for q in range(count):
-                data = jnp.dot(
+
+        def forward(b):
+            return [
+                jnp.dot(
                     fwd_hist,
                     hist[b, q * block : (q + 1) * block, here],
                     preferred_element_type=jnp.float32,
                 )
-                dc, ds = data[:bins], data[bins:]
-                tc, ts = spectra[q][:bins], spectra[q][bins:]
-                real = real + (dc * tc + ds * ts)
-                imag = imag + (ds * tc - dc * ts)
-            both = jnp.concatenate([real, imag], axis=0).astype(jnp.bfloat16)
-            part = jnp.dot(back_table, both, preferred_element_type=jnp.float32)
+                for q in range(count)
+            ]
+
+        def combine(data):
+            real, imag = [], []
+            for f in range(0, bins, GROUP):
+                re = im = None
+                for q in range(count):
+                    dc, ds = data[q][f : f + GROUP], data[q][bins + f : bins + f + GROUP]
+                    tc = spectra[q, f : f + GROUP, :]
+                    ts = spectra[q, bins + f : bins + f + GROUP, :]
+                    now_re, now_im = dc * tc + ds * ts, ds * tc - dc * ts
+                    re = now_re if re is None else re + now_re
+                    im = now_im if im is None else im + now_im
+                real.append(re.astype(jnp.bfloat16))
+                imag.append(im.astype(jnp.bfloat16))
+            both = jnp.concatenate(real + imag, axis=0)
+            return jnp.dot(back_table, both, preferred_element_type=jnp.float32)
+
+        def finish(b, part):
             newest = hist[b, rows - new :, here].astype(jnp.float32)
             for k, owner in enumerate(owners):
                 direct = scale * newest[owner * share : (owner + 1) * share]
@@ -76,6 +86,22 @@
                 out = keep if k < len(owners) // 2 else send
                 at = k % max(1, len(owners) // 2) * share
                 out[b, at : at + share, there] = piece.astype(out.dtype)
+
+        for q in range(count):
+            if q + 1 < count:
+                window = taps[q * block : q * block + length, here]
+            else:
+                window = jnp.concatenate([taps[q * block :, here], rim[:, rim_at]], axis=0)
+            spectra[q] = jnp.dot(fwd_taps, window, preferred_element_type=jnp.float32)
+        data = forward(0)
+        part = None
+        for b in range(seqs):
+            after = forward(b + 1) if b + 1 < seqs else None
+            now = combine(data)
+            if part is not None:
+                finish(b - 1, part)
+            part, data = now, after
+        finish(seqs - 1, part)
         return carry
 
     lax.fori_loop(0, keep.shape[2] // LANES, tile, 0)
@@ -115,6 +141,9 @@
         functools.partial(conv_body, base=base, rim_base=rim_base, owners=owners),
         in_specs=[pl.BlockSpec(memory_space=pltpu.SMEM)] + [vmem] * 6,
         out_specs=[vmem] * 2,
+        scratch_shapes=[
+            pltpu.VMEM((rows // (fwd.shape[1] - rim.shape[0]), fwd.shape[0], LANES), jnp.float32)
+        ],
         out_shape=[
             jax.ShapeDtypeStruct((seqs, half, width), jnp.float32),
             jax.ShapeDtypeStruct((seqs, half, width), jnp.bfloat16),
@@ -130,13 +159,8 @@
 
 
 def chunk_tiles(total):
-    sizes = []
-    left = total
-    while left:
-        size = min(left, 1 if not sizes else 2)
-        sizes.append(size)
-        left -= size
-    return sizes
+    parts = min(CHUNKS, total)
+    return [total // parts + (index < total % parts) for index in range(parts)]
 
 
 def swapped(ranks):

time: 52.1 us -> 40.8 us (0.78)
  starting transfers between devices: 18.1 us -> 13.2 us
  waiting for transfers between devices: 15.5 us -> 11.8 us
  Pallas kernels: 14.8 us -> 12.6 us
  local copies, waits for them, and re-layouts: 2.46 us -> 1.87 us
    ppermute x2, waiting for transfers between devices: 8.06 us -> 2.31 us  [body(): rims.append(lax.ppermute(filter_taps[:new, part], 'hist', toward))]
    ppermute x10 -> x6, starting transfers between devices: 15.5 us -> 10.6 us  [exchange(): return lax.ppermute(value, 'hist', [(z, z ^ bit) for z in range(ranks)])]
    pallas_call x5 -> x3, Pallas kernels: 10.8 us -> 8.6 us  [conv_chunk(): pl.pallas_call(functools.partial(conv_body, base=base, rim_base=rim_base,...]
    ppermute x10 -> x6, waiting for transfers between devices: 7.42 us -> 9.49 us  [exchange(): return lax.ppermute(value, 'hist', [(z, z ^ bit) for z in range(ranks)])]
    unnamed x4 -> x2, local copies, waits for them, and re-layouts: 0.69 us -> 0.01 us
  transfers between devices with their start and end apart: 12 -> 8, of which waited for: 7 -> 4; matrix products, arithmetic and copies ran while one was open for 2% -> 3% of each run, Pallas kernels for 21% -> 31%
where the time goes in v3:
time: 40.8 us; the launch traced here: 40.6 us
  starting transfers between devices  13.2 us (32%)
  Pallas kernels  12.6 us (31%)
  waiting for transfers between devices  11.8 us (29%)
  local copies, waits for them, and re-layouts  1.87 us (5%)
  other arithmetic  0.93 us (2%)
    ppermute x6, starting transfers between devices, exchange(): return lax.ppermute(value, 'hist', [(z, z ^ bit) for z in range(ranks)])  10.6 us
    ppermute x6, waiting for transfers between devices, exchange(): return lax.ppermute(value, 'hist', [(z, z ^ bit) for z in range(ranks)])  9.49 us
    pallas_call x3, Pallas kernels, conv_chunk(): pl.pallas_call(functools.partial(conv_body, base=base, rim_base=rim_base,...  8.6 us
    pallas_call x1, Pallas kernels, stage(): pl.pallas_call(stage_body, in_specs=[pl.BlockSpec(memory_space=pltpu.HBM)...  4.03 us
    ppermute x2, starting transfers between devices, body(): rims.append(lax.ppermute(filter_taps[:new, part], 'hist', toward))  2.57 us
    ppermute x2, waiting for transfers between devices, body(): rims.append(lax.ppermute(filter_taps[:new, part], 'hist', toward))  2.31 us
    slice x2, local copies, waits for them, and re-layouts, body(): rims.append(lax.ppermute(filter_taps[:new, part], 'hist', toward))  1.83 us
  transfers between devices with their start and end apart: 8, of which 4 were waited for; matrix products, arithmetic and copies ran while one was open for 3% of the time, Pallas kernels for 31%

profile of v3, /device:TPU:0, one launch (start us, length us, event | category | flops | bytes accessed | tf_op | source)
XLA Modules:
  0.0 40.6 jit_solution(16096898287195428394)
XLA Ops:
  0.0 0.9 %slice.41 = bf16[64,1280]{1,0:T(8,128)(2,1)S(1)} slice(bf16[512,2048]{1,0:T(8,128)(2,1)} %refs_1_.1), slice={[0:64], [768:2048]} | slice | bytes 327680 | tf_op jit(solution)/shard_map/slice | solution.py:201
  0.9 1.3 %collective-permute-start.3 = (bf16[64,1280]{1,0:T(8,128)(2,1)S(1)}, bf16[64,1280]{1,0:T(8,128)(2,1)S(1)}, u32[]{:S(2)}, u32[]{:S(2)}) collective-permute-start(bf16[64,1280]{1,0:T(8,128)(2,1)S(1)} %slice.41), channel_id=1, source_target_pairs={{4,0},{8,4},{12,8},{5,1},{9,5},{13,9},{6,2},{10,6},{14,10},{7,3},{... | collective-permute-start | bytes 491528 | tf_op jit(solution)/shard_map/ppermute | solution.py:201
  2.2 0.9 %slice.37 = bf16[64,768]{1,0:T(8,128)(2,1)S(1)} slice(bf16[512,2048]{1,0:T(8,128)(2,1)} %refs_1_.1), slice={[0:64], [0:768]} | slice | bytes 196608 | tf_op jit(solution)/shard_map/slice | solution.py:201
  3.1 1.3 %collective-permute-start = (bf16[64,768]{1,0:T(8,128)(2,1)S(1)}, bf16[64,768]{1,0:T(8,128)(2,1)S(1)}, u32[]{:S(2)}, u32[]{:S(2)}) collective-permute-start(bf16[64,768]{1,0:T(8,128)(2,1)S(1)} %slice.37), channel_id=1, source_target_pairs={{4,0},{8,4},{12,8},{5,1},{9,5},{13,9},{6,2},{10,6},{14,10},{7,3},{... | collective-permute-start | bytes 294920 | tf_op jit(solution)/shard_map/ppermute | solution.py:201
  4.4 4.0 %stage.1 = (bf16[4,512,2048]{2,1,0:T(8,128)(2,1)S(1)}, bf16[512,2048]{1,0:T(8,128)(2,1)S(1)}, f32[1,2048]{1,0:T(1,128)S(1)}, bf16[192,192]{1,0:T(8,128)(2,1)S(1)}, bf16[4,64,192]{2,1,0:T(8,128)(2,1)S(1)}) custom-call(bf16[4,512,2048]{2,1,0:T(8,128)(2,1)} %refs_0_.1, bf16[512,2048]{1,0:T(8,128)(2,1)} %refs_1_.1, f32[1,2048]{1,0:T(1,128)} %bitcast.2, ...), custom_call_target="tpu_custom_call" | custom-call | tf_op jit(solution)/shard_map/stage/pallas_call | solution.py:123
  8.5 2.3 %collective-permute-done.3.rim = bf16[64,1280]{1,0:T(8,128)(2,1)S(1)} collective-permute-done((bf16[64,1280]{1,0:T(8,128)(2,1)S(1)}, bf16[64,1280]{1,0:T(8,128)(2,1)S(1)}, u32[]{:S(2)}, u32[]{:S(2)}) %collective-permute-start.3) | collective-permute-done | bytes 163872 | tf_op jit(solution)/shard_map/ppermute | solution.py:201
  10.8 2.2 %conv_chunk.5 = (f32[4,32,512]{2,1,0:T(8,128)S(1)}, bf16[4,32,512]{2,1,0:T(8,128)(2,1)S(1)}) custom-call(s32[1]{0:T(128)} %bitcast.meta, bf16[4,512,2048]{2,1,0:T(8,128)(2,1)S(1)} %get-tuple-element.16.hist, bf16[512,2048]{1,0:T(8,128)(2,1)S(1)} %get-tuple-element.17.taps, f32[1,2048]{1,0:T(1,128)S(1)} %get-tuple-element.18.gain, ...), custom_call_target="tpu_custom_call" | custom-call | flops 503316480 | bytes 2621440 | tf_op jit(solution)/shard_map/conv_chunk/pallas_call | solution.py:140
  12.9 2.1 %collective-permute-start.6 = (bf16[4,32,512]{2,1,0:T(8,128)(2,1)S(1)}, bf16[4,32,512]{2,1,0:T(8,128)(2,1)S(1)}, u32[]{:S(2)}, u32[]{:S(2)}) collective-permute-start(bf16[4,32,512]{2,1,0:T(8,128)(2,1)S(1)} %get-tuple-element.26), channel_id=1, source_target_pairs={{0,4},{4,0},{8,12},{12,8},{1,5},{5,1},{9,13},{13,9},{2,6},{6,2},{1... | collective-permute-start | bytes 393224 | tf_op jit(solution)/shard_map/ppermute | solution.py:176
  15.0 0.0 collective-permute-done.rim
  15.0 3.2 %conv_chunk.3 = (f32[4,32,768]{2,1,0:T(8,128)S(1)}, bf16[4,32,768]{2,1,0:T(8,128)(2,1)S(1)}) custom-call(s32[1]{0:T(128)} %bitcast.meta, bf16[4,512,2048]{2,1,0:T(8,128)(2,1)S(1)} %get-tuple-element.16.hist, bf16[512,2048]{1,0:T(8,128)(2,1)S(1)} %get-tuple-element.17.taps, f32[1,2048]{1,0:T(1,128)S(1)} %get-tuple-element.18.gain, ...), custom_call_target="tpu_custom_call" | custom-call | flops 754974720 | bytes 3932160 | tf_op jit(solution)/shard_map/conv_chunk/pallas_call | solution.py:140
  18.3 0.0 copy-start
  18.3 0.1 collective-permute-start.1
  18.4 3.2 %conv_chunk.4 = (f32[4,32,768]{2,1,0:T(8,128)S(1)}, bf16[4,32,768]{2,1,0:T(8,128)(2,1)S(1)}) custom-call(s32[1]{0:T(128)} %bitcast.meta, bf16[4,512,2048]{2,1,0:T(8,128)(2,1)S(1)} %get-tuple-element.16.hist, bf16[512,2048]{1,0:T(8,128)(2,1)S(1)} %get-tuple-element.17.taps, f32[1,2048]{1,0:T(1,128)S(1)} %get-tuple-element.18.gain, ...), custom_call_target="tpu_custom_call" | custom-call | flops 754974720 | bytes 3932160 | tf_op jit(solution)/shard_map/conv_chunk/pallas_call | solution.py:140
  21.6 2.1 %collective-permute-start.4 = (bf16[4,32,768]{2,1,0:T(8,128)(2,1)S(1)}, bf16[4,32,768]{2,1,0:T(8,128)(2,1)S(1)}, u32[]{:S(2)}, u32[]{:S(2)}) collective-permute-start(bf16[4,32,768]{2,1,0:T(8,128)(2,1)S(1)} %get-tuple-element.24), channel_id=1, source_target_pairs={{0,4},{4,0},{8,12},{12,8},{1,5},{5,1},{9,13},{13,9},{2,6},{6,2},{1... | collective-permute-start | bytes 589832 | tf_op jit(solution)/shard_map/ppermute | solution.py:176
  23.7 0.0 collective-permute-done.6
  23.7 3.5 %collective-permute-start.7 = (bf16[4,16,512]{2,1,0:T(8,128)(2,1)S(1)}, bf16[4,16,512]{2,1,0:T(8,128)(2,1)S(1)}, u32[]{:S(2)}, u32[]{:S(2)}) collective-permute-start(bf16[4,16,512]{2,1,0:T(8,128)(2,1)S(1)} %slice.76), channel_id=1, source_target_pairs={{0,8},{4,12},{8,0},{12,4},{1,9},{5,13},{9,1},{13,5},{2,10},{6,14},... | collective-permute-start | bytes 196616 | tf_op jit(solution)/shard_map/ppermute | solution.py:176
  27.2 0.0 collective-permute-done.1
  27.3 1.3 %collective-permute-start.2 = (bf16[4,16,768]{2,1,0:T(8,128)(2,1)S(1)}, bf16[4,16,768]{2,1,0:T(8,128)(2,1)S(1)}, u32[]{:S(2)}, u32[]{:S(2)}) collective-permute-start(bf16[4,16,768]{2,1,0:T(8,128)(2,1)S(1)} %slice.75), channel_id=1, source_target_pairs={{0,8},{4,12},{8,0},{12,4},{1,9},{5,13},{9,1},{13,5},{2,10},{6,14},... | collective-permute-start | bytes 294920 | tf_op jit(solution)/shard_map/ppermute | solution.py:176
  28.6 2.8 %collective-permute-done.4 = bf16[4,32,768]{2,1,0:T(8,128)(2,1)S(1)} collective-permute-done((bf16[4,32,768]{2,1,0:T(8,128)(2,1)S(1)}, bf16[4,32,768]{2,1,0:T(8,128)(2,1)S(1)}, u32[]{:S(2)}, u32[]{:S(2)}) %collective-permute-start.4) | collective-permute-done | bytes 196640 | tf_op jit(solution)/shard_map/ppermute | solution.py:176
  31.4 1.6 %collective-permute-start.5 = (bf16[4,16,768]{2,1,0:T(8,128)(2,1)S(1)}, bf16[4,16,768]{2,1,0:T(8,128)(2,1)S(1)}, u32[]{:S(2)}, u32[]{:S(2)}) collective-permute-start(bf16[4,16,768]{2,1,0:T(8,128)(2,1)S(1)} %slice.74), channel_id=1, source_target_pairs={{0,8},{4,12},{8,0},{12,4},{1,9},{5,13},{9,1},{13,5},{2,10},{6,14},... | collective-permute-start | bytes 294920 | tf_op jit(solution)/shard_map/ppermute | solution.py:176
  33.0 0.0 collective-permute-done.7
  33.0 0.0 copy-done
  33.1 5.3 %collective-permute-done.2 = bf16[4,16,768]{2,1,0:T(8,128)(2,1)S(1)} collective-permute-done((bf16[4,16,768]{2,1,0:T(8,128)(2,1)S(1)}, bf16[4,16,768]{2,1,0:T(8,128)(2,1)S(1)}, u32[]{:S(2)}, u32[]{:S(2)}) %collective-permute-start.2) | collective-permute-done | bytes 98336 | tf_op jit(solution)/shard_map/ppermute | solution.py:176
  38.4 1.4 %collective-permute-done.5 = bf16[4,16,768]{2,1,0:T(8,128)(2,1)S(1)} collective-permute-done((bf16[4,16,768]{2,1,0:T(8,128)(2,1)S(1)}, bf16[4,16,768]{2,1,0:T(8,128)(2,1)S(1)}, u32[]{:S(2)}, u32[]{:S(2)}) %collective-permute-start.5) | collective-permute-done | bytes 98336 | tf_op jit(solution)/shard_map/ppermute | solution.py:176
  39.8 0.1 fusion.3
  39.8 0.7 %pad_maximum_fusion = bf16[4,16,2048]{2,1,0:T(8,128)(2,1)} fusion(bf16[4,16,512]{2,1,0:T(8,128)(2,1)S(1)} %fusion.5, bf16[4,16,768]{2,1,0:T(8,128)(2,1)S(1)} %get-tuple-element.28, bf16[4,16,768]{2,1,0:T(8,128)(2,1)S(1)} %get-tuple-element.27), kind=kLoop, calls=%fused_computation.2 | loop fusion | flops 786432 | bytes 524288 | tf_op jit(solution)/shard_map/concatenate | solution.py:226
  (7 shorter events, 0.2 us)
Async XLA Ops:
  0.9 9.8 %collective-permute-start.3 = (bf16[64,1280]{1,0:T(8,128)(2,1)S(1)}, bf16[64,1280]{1,0:T(8,128)(2,1)S(1)}, u32[]{:S(2)}, u32[]{:S(2)}) collective-permute-start(bf16[64,1280]{1,0:T(8,128)(2,1)S(1)} %slice.41), channel_id=1, source_target_pairs={{4,0},{8,4},{12,8},{5,1},{9,5},{13,9},{6,2},{10,6},{14,10},{7,3},{... | collective-permute-start | bytes 491528 | tf_op jit(solution)/shard_map/ppermute | solution.py:201
  3.1 11.9 %collective-permute-start = (bf16[64,768]{1,0:T(8,128)(2,1)S(1)}, bf16[64,768]{1,0:T(8,128)(2,1)S(1)}, u32[]{:S(2)}, u32[]{:S(2)}) collective-permute-start(bf16[64,768]{1,0:T(8,128)(2,1)S(1)} %slice.37), channel_id=1, source_target_pairs={{4,0},{8,4},{12,8},{5,1},{9,5},{13,9},{6,2},{10,6},{14,10},{7,3},{... | collective-permute-start | bytes 294920 | tf_op jit(solution)/shard_map/ppermute | solution.py:201
  12.9 10.7 %collective-permute-start.6 = (bf16[4,32,512]{2,1,0:T(8,128)(2,1)S(1)}, bf16[4,32,512]{2,1,0:T(8,128)(2,1)S(1)}, u32[]{:S(2)}, u32[]{:S(2)}) collective-permute-start(bf16[4,32,512]{2,1,0:T(8,128)(2,1)S(1)} %get-tuple-element.26), channel_id=1, source_target_pairs={{0,4},{4,0},{8,12},{12,8},{1,5},{5,1},{9,13},{13,9},{2,6},{6,2},{1... | collective-permute-start | bytes 393224 | tf_op jit(solution)/shard_map/ppermute | solution.py:176
  18.3 14.8 %copy-start = (bf16[4,16,2048]{2,1,0:T(8,128)(2,1)S(1)}, bf16[4,16,2048]{2,1,0:T(8,128)(2,1)}, u32[]{:S(2)}) copy-start(bf16[4,16,2048]{2,1,0:T(8,128)(2,1)} %param.9) | copy-start | bytes 786436
  18.3 9.0 %collective-permute-start.1 = (bf16[4,32,768]{2,1,0:T(8,128)(2,1)S(1)}, bf16[4,32,768]{2,1,0:T(8,128)(2,1)S(1)}, u32[]{:S(2)}, u32[]{:S(2)}) collective-permute-start(bf16[4,32,768]{2,1,0:T(8,128)(2,1)S(1)} %get-tuple-element.22), channel_id=1, source_target_pairs={{0,4},{4,0},{8,12},{12,8},{1,5},{5,1},{9,13},{13,9},{2,6},{6,2},{1... | collective-permute-start | bytes 589832 | tf_op jit(solution)/shard_map/ppermute | solution.py:176
  21.6 9.8 %collective-permute-start.4 = (bf16[4,32,768]{2,1,0:T(8,128)(2,1)S(1)}, bf16[4,32,768]{2,1,0:T(8,128)(2,1)S(1)}, u32[]{:S(2)}, u32[]{:S(2)}) collective-permute-start(bf16[4,32,768]{2,1,0:T(8,128)(2,1)S(1)} %get-tuple-element.24), channel_id=1, source_target_pairs={{0,4},{4,0},{8,12},{12,8},{1,5},{5,1},{9,13},{13,9},{2,6},{6,2},{1... | collective-permute-start | bytes 589832 | tf_op jit(solution)/shard_map/ppermute | solution.py:176
  23.7 9.3 %collective-permute-start.7 = (bf16[4,16,512]{2,1,0:T(8,128)(2,1)S(1)}, bf16[4,16,512]{2,1,0:T(8,128)(2,1)S(1)}, u32[]{:S(2)}, u32[]{:S(2)}) collective-permute-start(bf16[4,16,512]{2,1,0:T(8,128)(2,1)S(1)} %slice.76), channel_id=1, source_target_pairs={{0,8},{4,12},{8,0},{12,4},{1,9},{5,13},{9,1},{13,5},{2,10},{6,14},... | collective-permute-start | bytes 196616 | tf_op jit(solution)/shard_map/ppermute | solution.py:176
  27.3 11.1 %collective-permute-start.2 = (bf16[4,16,768]{2,1,0:T(8,128)(2,1)S(1)}, bf16[4,16,768]{2,1,0:T(8,128)(2,1)S(1)}, u32[]{:S(2)}, u32[]{:S(2)}) collective-permute-start(bf16[4,16,768]{2,1,0:T(8,128)(2,1)S(1)} %slice.75), channel_id=1, source_target_pairs={{0,8},{4,12},{8,0},{12,4},{1,9},{5,13},{9,1},{13,5},{2,10},{6,14},... | collective-permute-start | bytes 294920 | tf_op jit(solution)/shard_map/ppermute | solution.py:176
  31.4 8.3 %collective-permute-start.5 = (bf16[4,16,768]{2,1,0:T(8,128)(2,1)S(1)}, bf16[4,16,768]{2,1,0:T(8,128)(2,1)S(1)}, u32[]{:S(2)}, u32[]{:S(2)}) collective-permute-start(bf16[4,16,768]{2,1,0:T(8,128)(2,1)S(1)} %slice.74), channel_id=1, source_target_pairs={{0,8},{4,12},{8,0},{12,4},{1,9},{5,13},{9,1},{13,5},{2,10},{6,14},... | collective-permute-start | bytes 294920 | tf_op jit(solution)/shard_map/ppermute | solution.py:176

commit v4 on v3

--- a/solution.py
+++ b/solution.py
@@ -12,6 +12,8 @@
 LANES = 256
 BLOCK = 128
 CHUNKS = 3
+STRAIGHT = 4
+DIRECT = ()
 GROUP = 16
 
 
@@ -31,9 +33,29 @@
     return taps, back
 
 
-def conv_body(
-    meta, hist, taps, gain, fwd, back, rim, keep, send, spectra, *, base, rim_base, owners
-):
+def moves_in(sources, targets, done, first, count):
+    moves = []
+    for source, target in zip(sources, targets):
+        for t in range(count):
+            lead = (slice(None),) * (len(source.shape) - 1)
+            there = lead + (pl.ds((first + t) * LANES, LANES),)
+            here = lead + (pl.ds(t * LANES, LANES),)
+            moves.append(
+                pltpu.make_async_copy(source.at[there], target.at[here], done.at[len(moves)])
+            )
+    return moves
+
+
+def conv_body(meta, hist, taps, gain, fwd, back, rim, *refs, first, tiles, base, owners):
+    if base is None:
+        sources, refs = (), refs
+        outs, (spectra,) = refs[:-1], refs[-1:]
+    else:
+        sources, refs = refs[:2], refs[2:]
+        outs, targets, (spectra, done) = refs[:-4], refs[-4:-2], refs[-2:]
+        later = moves_in(sources, targets, done, base, targets[0].shape[2] // LANES)
+        for move in later:
+            move.start()
     seqs, rows, _ = hist.shape
     new = rim.shape[0]
     length = fwd.shape[1]
@@ -42,15 +64,16 @@
     count = rows // block
     share = new // len(owners)
     flag = (meta[0] == len(owners) - 1).astype(jnp.float32)
+    hist_at, rim_at, gain_at = first
 
     def tile(t, carry):
-        here = pl.ds(pl.multiple_of((base + t) * LANES, LANES), LANES)
+        here = pl.ds(pl.multiple_of((hist_at + t) * LANES, LANES), LANES)
+        near = pl.ds(pl.multiple_of((rim_at + t) * LANES, LANES), LANES)
         there = pl.ds(pl.multiple_of(t * LANES, LANES), LANES)
-        rim_at = pl.ds(pl.multiple_of((base - rim_base + t) * LANES, LANES), LANES)
         fwd_taps = fwd[...]
         fwd_hist = fwd[:, :block]
         back_table = back[meta[0]]
-        scale = gain[:, here] * flag
+        scale = gain[:, pl.ds(pl.multiple_of((gain_at + t) * LANES, LANES), LANES)] * flag
 
         def forward(b):
             return [
@@ -83,15 +106,15 @@
             for k, owner in enumerate(owners):
                 direct = scale * newest[owner * share : (owner + 1) * share]
                 piece = part[k * share : (k + 1) * share] + direct
-                out = keep if k < len(owners) // 2 else send
-                at = k % max(1, len(owners) // 2) * share
+                out = outs[k * len(outs) // len(owners)]
+                at = k % (len(owners) // len(outs)) * share
                 out[b, at : at + share, there] = piece.astype(out.dtype)
 
         for q in range(count):
             if q + 1 < count:
                 window = taps[q * block : q * block + length, here]
             else:
-                window = jnp.concatenate([taps[q * block :, here], rim[:, rim_at]], axis=0)
+                window = jnp.concatenate([taps[q * block :, here], rim[:, near]], axis=0)
             spectra[q] = jnp.dot(fwd_taps, window, preferred_element_type=jnp.float32)
         data = forward(0)
         part = None
@@ -104,50 +127,81 @@
         finish(seqs - 1, part)
         return carry
 
-    lax.fori_loop(0, keep.shape[2] // LANES, tile, 0)
-
-
-def stage_body(*refs):
-    count = len(refs) // 2
-    arrays, copies, done = refs[:count], refs[count:-1], refs[-1]
-    moves = [
-        pltpu.make_async_copy(arrays[i], copies[i], done.at[i]) for i in range(count)
-    ]
+    lax.fori_loop(0, tiles, tile, 0)
+    if base is not None:
+        for move in later:
+            move.wait()
+
+
+def stage_body(meta, *refs, tiles):
+    del meta
+    count = len(refs) // 2 - 1
+    arrays, copies, (done, whole) = refs[:count], refs[count:-2], refs[-2:]
+    moves = moves_in(arrays[:2], copies[:2], done, 0, tiles)
+    for i in range(2, count):
+        moves.append(pltpu.make_async_copy(arrays[i], copies[i], whole.at[i]))
     for move in moves:
         move.start()
     for move in moves:
         move.wait()
 
 
-def stage(*arrays):
+def in_hbm(*arrays):
+    return [pltpu.with_memory_space_constraint(a, pltpu.HBM) for a in arrays]
+
+
+def stage(meta, history, taps, *rest, tiles):
+    width = tiles * LANES
+    arrays = (history, taps) + rest
+    shapes = [a.shape[:-1] + (width,) for a in arrays[:2]] + [a.shape for a in rest]
     return pl.pallas_call(
-        stage_body,
-        in_specs=[pl.BlockSpec(memory_space=pltpu.HBM)] * len(arrays),
+        functools.partial(stage_body, tiles=tiles),
+        in_specs=[pl.BlockSpec(memory_space=pltpu.SMEM)]
+        + [pl.BlockSpec(memory_space=pltpu.HBM)] * len(arrays),
         out_specs=[pl.BlockSpec(memory_space=pltpu.VMEM)] * len(arrays),
-        out_shape=[pltpu.VMEM(a.shape, a.dtype) for a in arrays],
-        scratch_shapes=[pltpu.SemaphoreType.DMA((len(arrays),))],
+        out_shape=[pltpu.VMEM(d, a.dtype) for d, a in zip(shapes, arrays)],
+        scratch_shapes=[
+            pltpu.SemaphoreType.DMA((2 * tiles,)),
+            pltpu.SemaphoreType.DMA((len(arrays),)),
+        ],
         compiler_params=pltpu.CompilerParams(vmem_limit_bytes=16 << 20),
         name="stage",
-    )(*[pltpu.with_memory_space_constraint(a, pltpu.HBM) for a in arrays])
-
-
-def conv_chunk(meta, staged, rim, base, rim_base, tiles, owners):
+    )(meta, *in_hbm(*arrays))
+
+
+def conv_chunk(meta, staged, rim, first, tiles, owners, splits, later=None):
     history, _, _, fwd, _ = staged
     seqs, rows, _ = history.shape
-    half = rim.shape[0] // 2
+    new = rim.shape[0]
     width = tiles * LANES
     vmem = pl.BlockSpec(memory_space=pltpu.VMEM)
+    operands = [meta, *staged, rim]
+    in_specs = [pl.BlockSpec(memory_space=pltpu.SMEM)] + [vmem] * 6
+    out_shape = [
+        jax.ShapeDtypeStruct(
+            (seqs, new // splits, width), jnp.bfloat16 if k else jnp.float32
+        )
+        for k in range(splits)
+    ]
+    scratch = [
+        pltpu.VMEM((rows // (fwd.shape[1] - new), fwd.shape[0], LANES), jnp.float32)
+    ]
+    base = None
+    if later is not None:
+        base = tiles
+        left = later[0].shape[-1] // LANES - tiles
+        operands += in_hbm(*later)
+        in_specs += [pl.BlockSpec(memory_space=pltpu.HBM)] * 2
+        out_shape += [
+            pltpu.VMEM(a.shape[:-1] + (left * LANES,), a.dtype) for a in later
+        ]
+        scratch.append(pltpu.SemaphoreType.DMA((2 * left,)))
     return pl.pallas_call(
-        functools.partial(conv_body, base=base, rim_base=rim_base, owners=owners),
-        in_specs=[pl.BlockSpec(memory_space=pltpu.SMEM)] + [vmem] * 6,
-        out_specs=[vmem] * 2,
-        scratch_shapes=[
-            pltpu.VMEM((rows // (fwd.shape[1] - rim.shape[0]), fwd.shape[0], LANES), jnp.float32)
-        ],
-        out_shape=[
-            jax.ShapeDtypeStruct((seqs, half, width), jnp.float32),
-            jax.ShapeDtypeStruct((seqs, half, width), jnp.bfloat16),
-        ],
+        functools.partial(conv_body, first=first, tiles=tiles, base=base, owners=owners),
+        in_specs=in_specs,
+        out_specs=[vmem] * len(out_shape),
+        out_shape=out_shape,
+        scratch_shapes=scratch,
         cost_estimate=pl.CostEstimate(
             flops=2 * width * fwd.shape[0] * rows * (seqs + 1),
             transcendentals=0,
@@ -155,7 +209,37 @@
         ),
         compiler_params=pltpu.CompilerParams(vmem_limit_bytes=16 << 20),
         name="conv_chunk",
-    )(meta, *staged, rim)
+    )(*operands)
+
+
+def gate_body(gate, *refs, counts):
+    *pieces, out = refs
+    place = 0
+    for count in counts:
+        (keep, *got), pieces = pieces[:count], pieces[count:]
+        for t in range(keep.shape[2] // LANES):
+            here = slice(place * LANES, (place + 1) * LANES)
+            there = slice(t * LANES, (t + 1) * LANES)
+            value = keep[:, :, there]
+            for piece in got:
+                value = value + piece[:, :, there].astype(jnp.float32)
+            scaled = gate[:, :, here].astype(jnp.float32) * value
+            out[:, :, here] = scaled.astype(out.dtype)
+            place = place + 1
+
+
+def gated(gate, chunks):
+    vmem = pl.BlockSpec(memory_space=pltpu.VMEM)
+    pieces = [piece for chunk in chunks for piece in chunk]
+    counts = [len(chunk) for chunk in chunks]
+    return pl.pallas_call(
+        functools.partial(gate_body, counts=counts),
+        in_specs=[vmem] * (1 + len(pieces)),
+        out_specs=vmem,
+        out_shape=jax.ShapeDtypeStruct(gate.shape, gate.dtype),
+        compiler_params=pltpu.CompilerParams(vmem_limit_bytes=16 << 20),
+        name="gated",
+    )(gate, *pieces)
 
 
 def chunk_tiles(total):
@@ -182,6 +266,7 @@
     share = gate_values.shape[1]
     new = share * ranks
     channels = history.shape[2]
+    total = channels // LANES
     block = min(BLOCK, history.shape[1])
     taps_table, back_table = tables(block, new)
     fwd = jnp.asarray(taps_table, jnp.bfloat16)
@@ -193,37 +278,52 @@
     back = jnp.asarray(turned, jnp.bfloat16)
     owners = [(ranks - 1) ^ j for j in order]
     meta = rank[None]
-    sizes = chunk_tiles(channels // LANES)
+    sizes = chunk_tiles(total)
     toward = [(source, source - 1) for source in range(1, ranks)]
     split = sizes[0] * LANES
     rims = []
     for part in (slice(0, split), slice(split, None)):
         rims.append(lax.ppermute(filter_taps[:new, part], "hist", toward))
-    staged = stage(history, filter_taps, skip_gain[None, :], fwd, back)
-    pieces = []
+    gain = skip_gain[None, :]
+    staged = stage(meta, history, filter_taps, gain, fwd, back, tiles=sizes[0])
+    chunks = []
     start = 0
     for index, tiles in enumerate(sizes):
-        keep, send = conv_chunk(
+        straight = 2 < ranks <= STRAIGHT and index in DIRECT
+        splits = ranks if straight else 2
+        at = start - sizes[0] if index else 0
+        later = None if index or len(sizes) == 1 else (history, filter_taps)
+        keep, *sends = conv_chunk(
             meta,
             staged,
             rims[min(index, 1)],
-            start,
-            sizes[0] if index else 0,
+            (at, at, start),
             tiles,
             owners,
+            splits,
+            later,
         )
-        bit = 1
-        while bit < ranks:
-            got = exchange(send, bit, ranks)
-            total = keep + got.astype(jnp.float32)
-            half = total.shape[1] // 2
-            keep, send = total[:, :half], total[:, half:].astype(jnp.bfloat16)
-            bit *= 2
-        lo, hi = start * LANES, (start + tiles) * LANES
-        gate = gate_values[:, :, lo:hi].astype(jnp.float32)
-        pieces.append((gate * total).astype(jnp.bfloat16))
+        if later is not None:
+            staged = [sends[-2], sends[-1], *staged[2:]]
+            sends = sends[:-2]
+        got = []
+        if straight:
+            for k, send in enumerate(sends):
+                got.append(exchange(send, order[k + 1], ranks))
+        else:
+            bit = 1
+            while True:
+                came = exchange(sends[0], bit, ranks)
+                bit *= 2
+                if bit >= ranks:
+                    break
+                summed = keep + came.astype(jnp.float32)
+                half = summed.shape[1] // 2
+                keep, sends = summed[:, :half], [summed[:, half:].astype(jnp.bfloat16)]
+            got.append(came)
+        chunks.append([keep, *got])
         start += tiles
-    return jnp.concatenate(pieces, axis=2)
+    return gated(gate_values, chunks)
 
 
 def solution(mesh):

time: 40.8 us -> 39.4 us (0.966)
  Pallas kernels: 12.6 us -> 11.6 us
  other arithmetic: 0.93 us -> 0.12 us
  starting transfers between devices: 13.2 us -> 13.8 us
    pallas_call x4 -> x5, Pallas kernels: 12.6 us -> 11.6 us  [the longest x3 8.53 us: conv_chunk(): pl.pallas_call(functools.partial(conv_body, first=first, tiles=tiles, bas...]
    concatenate x1 -> x0, other arithmetic: 0.72 us -> none  [body(): return jnp.concatenate(pieces, axis=2)]
    ppermute x6, starting transfers between devices: 10.6 us -> 11.2 us  [exchange(): return lax.ppermute(value, 'hist', [(z, z ^ bit) for z in range(ranks)])]
  transfers between devices with their start and end apart: 8 -> 8, of which waited for: 4 -> 3; matrix products, arithmetic and copies ran while one was open for 3% -> 3% of each run, Pallas kernels for 31% -> 28%
where the time goes in v4:
time: 39.4 us; the launch traced here: 39.2 us
  starting transfers between devices  13.8 us (35%)
  Pallas kernels  11.6 us (29%)
  waiting for transfers between devices  11.6 us (29%)
  local copies, waits for them, and re-layouts  1.91 us (5%)
    ppermute x6, starting transfers between devices, exchange(): return lax.ppermute(value, 'hist', [(z, z ^ bit) for z in range(ranks)])  11.2 us
    ppermute x6, waiting for transfers between devices, exchange(): return lax.ppermute(value, 'hist', [(z, z ^ bit) for z in range(ranks)])  9.67 us
    pallas_call x3, Pallas kernels, conv_chunk(): pl.pallas_call(functools.partial(conv_body, first=first, tiles=tiles, bas...  8.53 us
    ppermute x2, starting transfers between devices, body(): rims.append(lax.ppermute(filter_taps[:new, part], 'hist', toward))  2.57 us
    pallas_call x1, Pallas kernels, stage(): pl.pallas_call(functools.partial(stage_body, tiles=tiles), in_specs=[pl.B...  2.3 us
    ppermute x2, waiting for transfers between devices, body(): rims.append(lax.ppermute(filter_taps[:new, part], 'hist', toward))  1.91 us
    slice x2, local copies, waits for them, and re-layouts, body(): rims.append(lax.ppermute(filter_taps[:new, part], 'hist', toward))  1.83 us
  transfers between devices with their start and end apart: 8, of which 3 were waited for; matrix products, arithmetic and copies ran while one was open for 3% of the time, Pallas kernels for 28%

profile of v4, /device:TPU:0, one launch (start us, length us, event | category | flops | bytes accessed | tf_op | source)
XLA Modules:
  0.0 39.2 jit_solution(1951610388631481978)
XLA Ops:
  0.0 0.9 %slice.27 = bf16[64,768]{1,0:T(8,128)(2,1)S(1)} slice(bf16[512,2048]{1,0:T(8,128)(2,1)} %refs_1_.3), slice={[0:64], [0:768]} | slice | bytes 196608 | tf_op jit(solution)/shard_map/slice | solution.py:286
  0.9 1.3 %collective-permute-start = (bf16[64,768]{1,0:T(8,128)(2,1)S(1)}, bf16[64,768]{1,0:T(8,128)(2,1)S(1)}, u32[]{:S(2)}, u32[]{:S(2)}) collective-permute-start(bf16[64,768]{1,0:T(8,128)(2,1)S(1)} %slice.27), channel_id=1, source_target_pairs={{4,0},{8,4},{12,8},{5,1},{9,5},{13,9},{6,2},{10,6},{14,10},{7,3},{... | collective-permute-start | bytes 294920 | tf_op jit(solution)/shard_map/ppermute | solution.py:286
  2.2 0.9 %slice.30 = bf16[64,1280]{1,0:T(8,128)(2,1)S(1)} slice(bf16[512,2048]{1,0:T(8,128)(2,1)} %refs_1_.3), slice={[0:64], [768:2048]} | slice | bytes 327680 | tf_op jit(solution)/shard_map/slice | solution.py:286
  3.1 1.3 %collective-permute-start.3 = (bf16[64,1280]{1,0:T(8,128)(2,1)S(1)}, bf16[64,1280]{1,0:T(8,128)(2,1)S(1)}, u32[]{:S(2)}, u32[]{:S(2)}) collective-permute-start(bf16[64,1280]{1,0:T(8,128)(2,1)S(1)} %slice.30), channel_id=1, source_target_pairs={{4,0},{8,4},{12,8},{5,1},{9,5},{13,9},{6,2},{10,6},{14,10},{7,3},{... | collective-permute-start | bytes 491528 | tf_op jit(solution)/shard_map/ppermute | solution.py:286
  4.4 2.3 %stage.1 = (bf16[4,512,768]{2,1,0:T(8,128)(2,1)S(1)}, bf16[512,768]{1,0:T(8,128)(2,1)S(1)}, f32[1,2048]{1,0:T(1,128)S(1)}, bf16[192,192]{1,0:T(8,128)(2,1)S(1)}, bf16[4,64,192]{2,1,0:T(8,128)(2,1)S(1)}) custom-call(s32[1]{0:T(128)} %bitcast.meta, bf16[4,512,2048]{2,1,0:T(8,128)(2,1)} %refs_0_.3, bf16[512,2048]{1,0:T(8,128)(2,1)} %refs_1_.3, ...), custom_call_target="tpu_custom_call" | custom-call | tf_op jit(solution)/shard_map/stage/pallas_call | solution.py:157
  6.7 1.9 %collective-permute-done.rim = bf16[64,768]{1,0:T(8,128)(2,1)S(1)} collective-permute-done((bf16[64,768]{1,0:T(8,128)(2,1)S(1)}, bf16[64,768]{1,0:T(8,128)(2,1)S(1)}, u32[]{:S(2)}, u32[]{:S(2)}) %collective-permute-start) | collective-permute-done | bytes 98336 | tf_op jit(solution)/shard_map/ppermute | solution.py:286
  8.6 3.3 %conv_chunk.3 = (f32[4,32,768]{2,1,0:T(8,128)S(1)}, bf16[4,32,768]{2,1,0:T(8,128)(2,1)S(1)}, bf16[4,512,1280]{2,1,0:T(8,128)(2,1)S(1)}, bf16[512,1280]{1,0:T(8,128)(2,1)S(1)}) custom-call(s32[1]{0:T(128)} %bitcast.meta, bf16[4,512,768]{2,1,0:T(8,128)(2,1)S(1)} %get-tuple-element.18.hist, bf16[512,768]{1,0:T(8,128)(2,1)S(1)} %get-tuple-element.19.taps, ...), custom_call_target="tpu_custom_call" | custom-call | flops 754974720 | bytes 3932160 | tf_op jit(solution)/shard_map/conv_chunk/pallas_call | solution.py:199
  11.9 2.5 %collective-permute-start.1 = (bf16[4,32,768]{2,1,0:T(8,128)(2,1)S(1)}, bf16[4,32,768]{2,1,0:T(8,128)(2,1)S(1)}, u32[]{:S(2)}, u32[]{:S(2)}) collective-permute-start(bf16[4,32,768]{2,1,0:T(8,128)(2,1)S(1)} %get-tuple-element.24), channel_id=1, source_target_pairs={{0,4},{4,0},{8,12},{12,8},{1,5},{5,1},{9,13},{13,9},{2,6},{6,2},{1... | collective-permute-start | bytes 589832 | tf_op jit(solution)/shard_map/ppermute | solution.py:260
  14.4 0.0 collective-permute-done.3.rim
  14.4 2.1 %conv_chunk.5 = (f32[4,32,512]{2,1,0:T(8,128)S(1)}, bf16[4,32,512]{2,1,0:T(8,128)(2,1)S(1)}) custom-call(s32[1]{0:T(128)} %bitcast.meta, bf16[4,512,1280]{2,1,0:T(8,128)(2,1)S(1)} %get-tuple-element.25.hist, bf16[512,1280]{1,0:T(8,128)(2,1)S(1)} %get-tuple-element.26.taps, f32[1,2048]{1,0:T(1,128)S(1)} %get-tuple-element.20.gain, ...), custom_call_target="tpu_custom_call" | custom-call | flops 503316480 | bytes 2621440 | tf_op jit(solution)/shard_map/conv_chunk/pallas_call | solution.py:199
  16.6 0.3 collective-permute-start.6
  16.8 3.1 %conv_chunk.4 = (f32[4,32,768]{2,1,0:T(8,128)S(1)}, bf16[4,32,768]{2,1,0:T(8,128)(2,1)S(1)}) custom-call(s32[1]{0:T(128)} %bitcast.meta, bf16[4,512,1280]{2,1,0:T(8,128)(2,1)S(1)} %get-tuple-element.25.hist, bf16[512,1280]{1,0:T(8,128)(2,1)S(1)} %get-tuple-element.26.taps, f32[1,2048]{1,0:T(1,128)S(1)} %get-tuple-element.20.gain, ...), custom_call_target="tpu_custom_call" | custom-call | flops 754974720 | bytes 3932160 | tf_op jit(solution)/shard_map/conv_chunk/pallas_call | solution.py:199
  20.0 0.0 copy-start
  20.0 1.9 %collective-permute-start.4 = (bf16[4,32,768]{2,1,0:T(8,128)(2,1)S(1)}, bf16[4,32,768]{2,1,0:T(8,128)(2,1)S(1)}, u32[]{:S(2)}, u32[]{:S(2)}) collective-permute-start(bf16[4,32,768]{2,1,0:T(8,128)(2,1)S(1)} %get-tuple-element.28), channel_id=1, source_target_pairs={{0,4},{4,0},{8,12},{12,8},{1,5},{5,1},{9,13},{13,9},{2,6},{6,2},{1... | collective-permute-start | bytes 589832 | tf_op jit(solution)/shard_map/ppermute | solution.py:260
  21.9 0.0 collective-permute-done.1
  21.9 3.5 %collective-permute-start.2 = (bf16[4,16,768]{2,1,0:T(8,128)(2,1)S(1)}, bf16[4,16,768]{2,1,0:T(8,128)(2,1)S(1)}, u32[]{:S(2)}, u32[]{:S(2)}) collective-permute-start(bf16[4,16,768]{2,1,0:T(8,128)(2,1)S(1)} %slice.45), channel_id=1, source_target_pairs={{0,8},{4,12},{8,0},{12,4},{1,9},{5,13},{9,1},{13,5},{2,10},{6,14},... | collective-permute-start | bytes 294920 | tf_op jit(solution)/shard_map/ppermute | solution.py:260
  25.5 2.3 %collective-permute-done.4 = bf16[4,32,768]{2,1,0:T(8,128)(2,1)S(1)} collective-permute-done((bf16[4,32,768]{2,1,0:T(8,128)(2,1)S(1)}, bf16[4,32,768]{2,1,0:T(8,128)(2,1)S(1)}, u32[]{:S(2)}, u32[]{:S(2)}) %collective-permute-start.4) | collective-permute-done | bytes 196640 | tf_op jit(solution)/shard_map/ppermute | solution.py:260
  27.9 2.9 %collective-permute-start.5 = (bf16[4,16,768]{2,1,0:T(8,128)(2,1)S(1)}, bf16[4,16,768]{2,1,0:T(8,128)(2,1)S(1)}, u32[]{:S(2)}, u32[]{:S(2)}) collective-permute-start(bf16[4,16,768]{2,1,0:T(8,128)(2,1)S(1)} %slice.44), channel_id=1, source_target_pairs={{0,8},{4,12},{8,0},{12,4},{1,9},{5,13},{9,1},{13,5},{2,10},{6,14},... | collective-permute-start | bytes 294920 | tf_op jit(solution)/shard_map/ppermute | solution.py:260
  30.8 0.0 collective-permute-done.6
  30.8 0.2 collective-permute-start.7
  31.1 7.3 %collective-permute-done.7.refs_5_ = bf16[4,16,512]{2,1,0:T(8,128)(2,1)S(1)} collective-permute-done((bf16[4,16,512]{2,1,0:T(8,128)(2,1)S(1)}, bf16[4,16,512]{2,1,0:T(8,128)(2,1)S(1)}, u32[]{:S(2)}, u32[]{:S(2)}) %collective-permute-start.7) | collective-permute-done | bytes 65568 | tf_op jit(solution)/shard_map/ppermute | solution.py:260
  38.4 0.0 collective-permute-done.2.refs_1_
  38.4 0.0 collective-permute-done.5.refs_3_
  38.4 0.0 copy-done
  38.4 0.8 %gated.1 = bf16[4,16,2048]{2,1,0:T(8,128)(2,1)} custom-call(bf16[4,16,2048]{2,1,0:T(8,128)(2,1)S(1)} %copy-done, f32[4,16,768]{2,1,0:T(8,128)S(1)} %slice.35.refs_0_, bf16[4,16,768]{2,1,0:T(8,128)(2,1)S(1)} %collective-permute-done.2.refs_1_, f32[4,16,768]{2,1,0:T(8,128)S(1)} %slice.37.refs_2_, bf16[4,16,768]{2,1,0:T(8,128)(2,1)S(1)} %collective-permute-done.5.refs_3_, ...), custom_call_target="tpu_custom_call" | custom-call | tf_op jit(solution)/shard_map/gated/pallas_call | solution.py:235
  (9 shorter events, 0.2 us)
Async XLA Ops:
  0.9 7.7 %collective-permute-start = (bf16[64,768]{1,0:T(8,128)(2,1)S(1)}, bf16[64,768]{1,0:T(8,128)(2,1)S(1)}, u32[]{:S(2)}, u32[]{:S(2)}) collective-permute-start(bf16[64,768]{1,0:T(8,128)(2,1)S(1)} %slice.27), channel_id=1, source_target_pairs={{4,0},{8,4},{12,8},{5,1},{9,5},{13,9},{6,2},{10,6},{14,10},{7,3},{... | collective-permute-start | bytes 294920 | tf_op jit(solution)/shard_map/ppermute | solution.py:286
  3.1 11.3 %collective-permute-start.3 = (bf16[64,1280]{1,0:T(8,128)(2,1)S(1)}, bf16[64,1280]{1,0:T(8,128)(2,1)S(1)}, u32[]{:S(2)}, u32[]{:S(2)}) collective-permute-start(bf16[64,1280]{1,0:T(8,128)(2,1)S(1)} %slice.30), channel_id=1, source_target_pairs={{4,0},{8,4},{12,8},{5,1},{9,5},{13,9},{6,2},{10,6},{14,10},{7,3},{... | collective-permute-start | bytes 491528 | tf_op jit(solution)/shard_map/ppermute | solution.py:286
  11.9 9.9 %collective-permute-start.1 = (bf16[4,32,768]{2,1,0:T(8,128)(2,1)S(1)}, bf16[4,32,768]{2,1,0:T(8,128)(2,1)S(1)}, u32[]{:S(2)}, u32[]{:S(2)}) collective-permute-start(bf16[4,32,768]{2,1,0:T(8,128)(2,1)S(1)} %get-tuple-element.24), channel_id=1, source_target_pairs={{0,4},{4,0},{8,12},{12,8},{1,5},{5,1},{9,13},{13,9},{2,6},{6,2},{1... | collective-permute-start | bytes 589832 | tf_op jit(solution)/shard_map/ppermute | solution.py:260
  16.6 14.2 %collective-permute-start.6 = (bf16[4,32,512]{2,1,0:T(8,128)(2,1)S(1)}, bf16[4,32,512]{2,1,0:T(8,128)(2,1)S(1)}, u32[]{:S(2)}, u32[]{:S(2)}) collective-permute-start(bf16[4,32,512]{2,1,0:T(8,128)(2,1)S(1)} %get-tuple-element.30), channel_id=1, source_target_pairs={{0,4},{4,0},{8,12},{12,8},{1,5},{5,1},{9,13},{13,9},{2,6},{6,2},{1... | collective-permute-start | bytes 393224 | tf_op jit(solution)/shard_map/ppermute | solution.py:260
  20.0 18.4 %copy-start = (bf16[4,16,2048]{2,1,0:T(8,128)(2,1)S(1)}, bf16[4,16,2048]{2,1,0:T(8,128)(2,1)}, u32[]{:S(2)}) copy-start(bf16[4,16,2048]{2,1,0:T(8,128)(2,1)} %gate.1) | copy-start | bytes 786436
  20.0 7.8 %collective-permute-start.4 = (bf16[4,32,768]{2,1,0:T(8,128)(2,1)S(1)}, bf16[4,32,768]{2,1,0:T(8,128)(2,1)S(1)}, u32[]{:S(2)}, u32[]{:S(2)}) collective-permute-start(bf16[4,32,768]{2,1,0:T(8,128)(2,1)S(1)} %get-tuple-element.28), channel_id=1, source_target_pairs={{0,4},{4,0},{8,12},{12,8},{1,5},{5,1},{9,13},{13,9},{2,6},{6,2},{1... | collective-permute-start | bytes 589832 | tf_op jit(solution)/shard_map/ppermute | solution.py:260
  21.9 16.4 %collective-permute-start.2 = (bf16[4,16,768]{2,1,0:T(8,128)(2,1)S(1)}, bf16[4,16,768]{2,1,0:T(8,128)(2,1)S(1)}, u32[]{:S(2)}, u32[]{:S(2)}) collective-permute-start(bf16[4,16,768]{2,1,0:T(8,128)(2,1)S(1)} %slice.45), channel_id=1, source_target_pairs={{0,8},{4,12},{8,0},{12,4},{1,9},{5,13},{9,1},{13,5},{2,10},{6,14},... | collective-permute-start | bytes 294920 | tf_op jit(solution)/shard_map/ppermute | solution.py:260
  27.9 10.5 %collective-permute-start.5 = (bf16[4,16,768]{2,1,0:T(8,128)(2,1)S(1)}, bf16[4,16,768]{2,1,0:T(8,128)(2,1)S(1)}, u32[]{:S(2)}, u32[]{:S(2)}) collective-permute-start(bf16[4,16,768]{2,1,0:T(8,128)(2,1)S(1)} %slice.44), channel_id=1, source_target_pairs={{0,8},{4,12},{8,0},{12,4},{1,9},{5,13},{9,1},{13,5},{2,10},{6,14},... | collective-permute-start | bytes 294920 | tf_op jit(solution)/shard_map/ppermute | solution.py:260
  30.8 7.5 %collective-permute-start.7 = (bf16[4,16,512]{2,1,0:T(8,128)(2,1)S(1)}, bf16[4,16,512]{2,1,0:T(8,128)(2,1)S(1)}, u32[]{:S(2)}, u32[]{:S(2)}) collective-permute-start(bf16[4,16,512]{2,1,0:T(8,128)(2,1)S(1)} %slice.46), channel_id=1, source_target_pairs={{0,8},{4,12},{8,0},{12,4},{1,9},{5,13},{9,1},{13,5},{2,10},{6,14},... | collective-permute-start | bytes 196616 | tf_op jit(solution)/shard_map/ppermute | solution.py:260

commit v5 on v4

--- a/solution.py
+++ b/solution.py
@@ -12,8 +12,6 @@
 LANES = 256
 BLOCK = 128
 CHUNKS = 3
-STRAIGHT = 4
-DIRECT = ()
 GROUP = 16
 
 
@@ -66,71 +64,85 @@
     flag = (meta[0] == len(owners) - 1).astype(jnp.float32)
     hist_at, rim_at, gain_at = first
 
-    def tile(t, carry):
-        here = pl.ds(pl.multiple_of((hist_at + t) * LANES, LANES), LANES)
-        near = pl.ds(pl.multiple_of((rim_at + t) * LANES, LANES), LANES)
-        there = pl.ds(pl.multiple_of(t * LANES, LANES), LANES)
-        fwd_taps = fwd[...]
-        fwd_hist = fwd[:, :block]
-        back_table = back[meta[0]]
-        scale = gain[:, pl.ds(pl.multiple_of((gain_at + t) * LANES, LANES), LANES)] * flag
-
-        def forward(b):
-            return [
-                jnp.dot(
-                    fwd_hist,
-                    hist[b, q * block : (q + 1) * block, here],
-                    preferred_element_type=jnp.float32,
-                )
-                for q in range(count)
-            ]
-
-        def combine(data):
-            real, imag = [], []
-            for f in range(0, bins, GROUP):
-                re = im = None
-                for q in range(count):
-                    dc, ds = data[q][f : f + GROUP], data[q][bins + f : bins + f + GROUP]
-                    tc = spectra[q, f : f + GROUP, :]
-                    ts = spectra[q, bins + f : bins + f + GROUP, :]
-                    now_re, now_im = dc * tc + ds * ts, ds * tc - dc * ts
-                    re = now_re if re is None else re + now_re
-                    im = now_im if im is None else im + now_im
-                real.append(re.astype(jnp.bfloat16))
-                imag.append(im.astype(jnp.bfloat16))
-            both = jnp.concatenate(real + imag, axis=0)
-            return jnp.dot(back_table, both, preferred_element_type=jnp.float32)
-
-        def finish(b, part):
-            newest = hist[b, rows - new :, here].astype(jnp.float32)
-            for k, owner in enumerate(owners):
-                direct = scale * newest[owner * share : (owner + 1) * share]
-                piece = part[k * share : (k + 1) * share] + direct
-                out = outs[k * len(outs) // len(owners)]
-                at = k % (len(owners) // len(outs)) * share
-                out[b, at : at + share, there] = piece.astype(out.dtype)
-
+    fwd_taps = fwd[...]
+    fwd_hist = fwd[:, :block]
+    back_table = back[meta[0]]
+
+    def lanes(tile):
+        return slice(tile * LANES, (tile + 1) * LANES)
+
+    def transform(t):
         for q in range(count):
+            here = lanes(hist_at + t)
             if q + 1 < count:
                 window = taps[q * block : q * block + length, here]
             else:
-                window = jnp.concatenate([taps[q * block :, here], rim[:, near]], axis=0)
-            spectra[q] = jnp.dot(fwd_taps, window, preferred_element_type=jnp.float32)
-        data = forward(0)
-        part = None
-        for b in range(seqs):
-            after = forward(b + 1) if b + 1 < seqs else None
-            now = combine(data)
-            if part is not None:
-                finish(b - 1, part)
-            part, data = now, after
-        finish(seqs - 1, part)
-        return carry
-
-    lax.fori_loop(0, tiles, tile, 0)
-    if base is not None:
-        for move in later:
-            move.wait()
+                window = jnp.concatenate(
+                    [taps[q * block :, here], rim[:, lanes(rim_at + t)]], axis=0
+                )
+            spectra[t % 2, q] = jnp.dot(
+                fwd_taps, window, preferred_element_type=jnp.float32
+            )
+
+    def forward(t, b):
+        return [
+            jnp.dot(
+                fwd_hist,
+                hist[b, q * block : (q + 1) * block, lanes(hist_at + t)],
+                preferred_element_type=jnp.float32,
+            )
+            for q in range(count)
+        ]
+
+    def combine(t, data):
+        real, imag = [], []
+        for f in range(0, bins, GROUP):
+            re = im = None
+            for q in range(count):
+                dc, ds = data[q][f : f + GROUP], data[q][bins + f : bins + f + GROUP]
+                tc = spectra[t % 2, q, f : f + GROUP, :]
+                ts = spectra[t % 2, q, bins + f : bins + f + GROUP, :]
+                now_re, now_im = dc * tc + ds * ts, ds * tc - dc * ts
+                re = now_re if re is None else re + now_re
+                im = now_im if im is None else im + now_im
+            real.append(re.astype(jnp.bfloat16))
+            imag.append(im.astype(jnp.bfloat16))
+        both = jnp.concatenate(real + imag, axis=0)
+        return jnp.dot(back_table, both, preferred_element_type=jnp.float32)
+
+    def finish(t, b, part):
+        scale = gain[:, lanes(gain_at + t)] * flag
+        newest = hist[b, rows - new :, lanes(hist_at + t)].astype(jnp.float32)
+        for k, owner in enumerate(owners):
+            direct = scale * newest[owner * share : (owner + 1) * share]
+            piece = part[k * share : (k + 1) * share] + direct
+            out = outs[k * len(outs) // len(owners)]
+            at = k % (len(owners) // len(outs)) * share
+            out[b, at : at + share, lanes(t)] = piece.astype(out.dtype)
+
+    def compute():
+        steps = [(t, b) for t in range(tiles) for b in range(seqs)]
+        transform(0)
+        data = forward(*steps[0])
+        last = None
+        for index, (t, b) in enumerate(steps):
+            after = None
+            if index + 1 < len(steps):
+                if b == seqs // 2 and t + 1 < tiles:
+                    transform(t + 1)
+                after = forward(*steps[index + 1])
+            now = combine(t, data)
+            if last is not None:
+                finish(*last)
+            last, data = (t, b, now), after
+        finish(*last)
+
+    if base is None:
+        compute()
+        return
+    pl.when(meta[0] >= 0)(compute)
+    for move in later:
+        move.wait()
 
 
 def stage_body(meta, *refs, tiles):
@@ -169,7 +181,7 @@
     )(meta, *in_hbm(*arrays))
 
 
-def conv_chunk(meta, staged, rim, first, tiles, owners, splits, later=None):
+def conv_chunk(meta, staged, rim, first, tiles, owners, later=None):
     history, _, _, fwd, _ = staged
     seqs, rows, _ = history.shape
     new = rim.shape[0]
@@ -179,12 +191,14 @@
     in_specs = [pl.BlockSpec(memory_space=pltpu.SMEM)] + [vmem] * 6
     out_shape = [
         jax.ShapeDtypeStruct(
-            (seqs, new // splits, width), jnp.bfloat16 if k else jnp.float32
+            (seqs, new // 2, width), jnp.bfloat16 if k else jnp.float32
         )
-        for k in range(splits)
+        for k in range(2)
     ]
     scratch = [
-        pltpu.VMEM((rows // (fwd.shape[1] - new), fwd.shape[0], LANES), jnp.float32)
+        pltpu.VMEM(
+            (2, rows // (fwd.shape[1] - new), fwd.shape[0], LANES), jnp.float32
+        )
     ]
     base = None
     if later is not None:
@@ -289,8 +303,6 @@
     chunks = []
     start = 0
     for index, tiles in enumerate(sizes):
-        straight = 2 < ranks <= STRAIGHT and index in DIRECT
-        splits = ranks if straight else 2
         at = start - sizes[0] if index else 0
         later = None if index or len(sizes) == 1 else (history, filter_taps)
         keep, *sends = conv_chunk(
@@ -300,28 +312,21 @@
             (at, at, start),
             tiles,
             owners,
-            splits,
             later,
         )
         if later is not None:
             staged = [sends[-2], sends[-1], *staged[2:]]
             sends = sends[:-2]
-        got = []
-        if straight:
-            for k, send in enumerate(sends):
-                got.append(exchange(send, order[k + 1], ranks))
-        else:
-            bit = 1
-            while True:
-                came = exchange(sends[0], bit, ranks)
-                bit *= 2
-                if bit >= ranks:
-                    break
-                summed = keep + came.astype(jnp.float32)
-                half = summed.shape[1] // 2
-                keep, sends = summed[:, :half], [summed[:, half:].astype(jnp.bfloat16)]
-            got.append(came)
-        chunks.append([keep, *got])
+        bit = 1
+        while True:
+            got = exchange(sends[0], bit, ranks)
+            bit *= 2
+            if bit >= ranks:
+                break
+            summed = keep + got.astype(jnp.float32)
+            half = summed.shape[1] // 2
+            keep, sends = summed[:, :half], [summed[:, half:].astype(jnp.bfloat16)]
+        chunks.append([keep, got])
         start += tiles
     return gated(gate_values, chunks)
 

time: 39.4 us -> 39.4 us (level)
  waiting for transfers between devices: 11.6 us -> 12.4 us
  Pallas kernels: 11.6 us -> 10.8 us
    ppermute x6, waiting for transfers between devices: 9.67 us -> 10.5 us  [exchange(): return lax.ppermute(value, 'hist', [(z, z ^ bit) for z in range(ranks)])]
    pallas_call x3, Pallas kernels: 8.53 us -> 7.72 us  [conv_chunk(): pl.pallas_call(functools.partial(conv_body, first=first, tiles=tiles, bas...]
  transfers between devices with their start and end apart: 8 -> 8, of which waited for: 3 -> 3; matrix products, arithmetic and copies ran while one was open for 3% -> 3% of each run, Pallas kernels for 28% -> 26%
where the time goes in v5:
time: 39.4 us; the launch traced here: 39.2 us
  starting transfers between devices  13.8 us (35%)
  waiting for transfers between devices  12.4 us (31%)
  Pallas kernels  10.8 us (27%)
  local copies, waits for them, and re-layouts  1.91 us (5%)
    ppermute x6, starting transfers between devices, exchange(): return lax.ppermute(value, 'hist', [(z, z ^ bit) for z in range(ranks)])  11.2 us
    ppermute x6, waiting for transfers between devices, exchange(): return lax.ppermute(value, 'hist', [(z, z ^ bit) for z in range(ranks)])  10.5 us
    pallas_call x3, Pallas kernels, conv_chunk(): pl.pallas_call(functools.partial(conv_body, first=first, tiles=tiles, bas...  7.72 us
    ppermute x2, starting transfers between devices, body(): rims.append(lax.ppermute(filter_taps[:new, part], 'hist', toward))  2.57 us
    pallas_call x1, Pallas kernels, stage(): pl.pallas_call(functools.partial(stage_body, tiles=tiles), in_specs=[pl.B...  2.3 us
    ppermute x2, waiting for transfers between devices, body(): rims.append(lax.ppermute(filter_taps[:new, part], 'hist', toward))  1.91 us
    slice x2, local copies, waits for them, and re-layouts, body(): rims.append(lax.ppermute(filter_taps[:new, part], 'hist', toward))  1.83 us
  transfers between devices with their start and end apart: 8, of which 3 were waited for; matrix products, arithmetic and copies ran while one was open for 3% of the time, Pallas kernels for 26%

profile of v5, /device:TPU:0, one launch (start us, length us, event | category | flops | bytes accessed | tf_op | source)
XLA Modules:
  0.0 39.2 jit_solution(13313303758285469879)
XLA Ops:
  0.0 0.9 %slice.27 = bf16[64,768]{1,0:T(8,128)(2,1)S(1)} slice(bf16[512,2048]{1,0:T(8,128)(2,1)} %refs_1_.3), slice={[0:64], [0:768]} | slice | bytes 196608 | tf_op jit(solution)/shard_map/slice | solution.py:300
  0.9 1.3 %collective-permute-start = (bf16[64,768]{1,0:T(8,128)(2,1)S(1)}, bf16[64,768]{1,0:T(8,128)(2,1)S(1)}, u32[]{:S(2)}, u32[]{:S(2)}) collective-permute-start(bf16[64,768]{1,0:T(8,128)(2,1)S(1)} %slice.27), channel_id=1, source_target_pairs={{4,0},{8,4},{12,8},{5,1},{9,5},{13,9},{6,2},{10,6},{14,10},{7,3},{... | collective-permute-start | bytes 294920 | tf_op jit(solution)/shard_map/ppermute | solution.py:300
  2.2 0.9 %slice.30 = bf16[64,1280]{1,0:T(8,128)(2,1)S(1)} slice(bf16[512,2048]{1,0:T(8,128)(2,1)} %refs_1_.3), slice={[0:64], [768:2048]} | slice | bytes 327680 | tf_op jit(solution)/shard_map/slice | solution.py:300
  3.1 1.3 %collective-permute-start.3 = (bf16[64,1280]{1,0:T(8,128)(2,1)S(1)}, bf16[64,1280]{1,0:T(8,128)(2,1)S(1)}, u32[]{:S(2)}, u32[]{:S(2)}) collective-permute-start(bf16[64,1280]{1,0:T(8,128)(2,1)S(1)} %slice.30), channel_id=1, source_target_pairs={{4,0},{8,4},{12,8},{5,1},{9,5},{13,9},{6,2},{10,6},{14,10},{7,3},{... | collective-permute-start | bytes 491528 | tf_op jit(solution)/shard_map/ppermute | solution.py:300
  4.4 2.3 %stage.1 = (bf16[4,512,768]{2,1,0:T(8,128)(2,1)S(1)}, bf16[512,768]{1,0:T(8,128)(2,1)S(1)}, f32[1,2048]{1,0:T(1,128)S(1)}, bf16[192,192]{1,0:T(8,128)(2,1)S(1)}, bf16[4,64,192]{2,1,0:T(8,128)(2,1)S(1)}) custom-call(s32[1]{0:T(128)} %bitcast.meta, bf16[4,512,2048]{2,1,0:T(8,128)(2,1)} %refs_0_.3, bf16[512,2048]{1,0:T(8,128)(2,1)} %refs_1_.3, ...), custom_call_target="tpu_custom_call" | custom-call | tf_op jit(solution)/shard_map/stage/pallas_call | solution.py:169
  6.7 1.9 %collective-permute-done.rim = bf16[64,768]{1,0:T(8,128)(2,1)S(1)} collective-permute-done((bf16[64,768]{1,0:T(8,128)(2,1)S(1)}, bf16[64,768]{1,0:T(8,128)(2,1)S(1)}, u32[]{:S(2)}, u32[]{:S(2)}) %collective-permute-start) | collective-permute-done | bytes 98336 | tf_op jit(solution)/shard_map/ppermute | solution.py:300
  8.6 3.0 %conv_chunk.3 = (f32[4,32,768]{2,1,0:T(8,128)S(1)}, bf16[4,32,768]{2,1,0:T(8,128)(2,1)S(1)}, bf16[4,512,1280]{2,1,0:T(8,128)(2,1)S(1)}, bf16[512,1280]{1,0:T(8,128)(2,1)S(1)}) custom-call(s32[1]{0:T(128)} %bitcast.meta, bf16[4,512,768]{2,1,0:T(8,128)(2,1)S(1)} %get-tuple-element.18.hist, bf16[512,768]{1,0:T(8,128)(2,1)S(1)} %get-tuple-element.19.taps, ...), custom_call_target="tpu_custom_call" | custom-call | flops 754974720 | bytes 3932160 | tf_op jit(solution)/shard_map/conv_chunk/pallas_call | solution.py:213
  11.7 2.5 %collective-permute-start.1 = (bf16[4,32,768]{2,1,0:T(8,128)(2,1)S(1)}, bf16[4,32,768]{2,1,0:T(8,128)(2,1)S(1)}, u32[]{:S(2)}, u32[]{:S(2)}) collective-permute-start(bf16[4,32,768]{2,1,0:T(8,128)(2,1)S(1)} %get-tuple-element.24), channel_id=1, source_target_pairs={{0,4},{4,0},{8,12},{12,8},{1,5},{5,1},{9,13},{13,9},{2,6},{6,2},{1... | collective-permute-start | bytes 589832 | tf_op jit(solution)/shard_map/ppermute | solution.py:274
  14.1 0.0 collective-permute-done.3.rim
  14.2 1.9 %conv_chunk.5 = (f32[4,32,512]{2,1,0:T(8,128)S(1)}, bf16[4,32,512]{2,1,0:T(8,128)(2,1)S(1)}) custom-call(s32[1]{0:T(128)} %bitcast.meta, bf16[4,512,1280]{2,1,0:T(8,128)(2,1)S(1)} %get-tuple-element.25.hist, bf16[512,1280]{1,0:T(8,128)(2,1)S(1)} %get-tuple-element.26.taps, f32[1,2048]{1,0:T(1,128)S(1)} %get-tuple-element.20.gain, ...), custom_call_target="tpu_custom_call" | custom-call | flops 503316480 | bytes 2621440 | tf_op jit(solution)/shard_map/conv_chunk/pallas_call | solution.py:213
  16.1 0.5 %collective-permute-start.6 = (bf16[4,32,512]{2,1,0:T(8,128)(2,1)S(1)}, bf16[4,32,512]{2,1,0:T(8,128)(2,1)S(1)}, u32[]{:S(2)}, u32[]{:S(2)}) collective-permute-start(bf16[4,32,512]{2,1,0:T(8,128)(2,1)S(1)} %get-tuple-element.30), channel_id=1, source_target_pairs={{0,4},{4,0},{8,12},{12,8},{1,5},{5,1},{9,13},{13,9},{2,6},{6,2},{1... | collective-permute-start | bytes 393224 | tf_op jit(solution)/shard_map/ppermute | solution.py:274
  16.6 2.8 %conv_chunk.4 = (f32[4,32,768]{2,1,0:T(8,128)S(1)}, bf16[4,32,768]{2,1,0:T(8,128)(2,1)S(1)}) custom-call(s32[1]{0:T(128)} %bitcast.meta, bf16[4,512,1280]{2,1,0:T(8,128)(2,1)S(1)} %get-tuple-element.25.hist, bf16[512,1280]{1,0:T(8,128)(2,1)S(1)} %get-tuple-element.26.taps, f32[1,2048]{1,0:T(1,128)S(1)} %get-tuple-element.20.gain, ...), custom_call_target="tpu_custom_call" | custom-call | flops 754974720 | bytes 3932160 | tf_op jit(solution)/shard_map/conv_chunk/pallas_call | solution.py:213
  19.4 0.0 copy-start
  19.4 1.6 %collective-permute-start.4 = (bf16[4,32,768]{2,1,0:T(8,128)(2,1)S(1)}, bf16[4,32,768]{2,1,0:T(8,128)(2,1)S(1)}, u32[]{:S(2)}, u32[]{:S(2)}) collective-permute-start(bf16[4,32,768]{2,1,0:T(8,128)(2,1)S(1)} %get-tuple-element.28), channel_id=1, source_target_pairs={{0,4},{4,0},{8,12},{12,8},{1,5},{5,1},{9,13},{13,9},{2,6},{6,2},{1... | collective-permute-start | bytes 589832 | tf_op jit(solution)/shard_map/ppermute | solution.py:274
  21.0 0.0 collective-permute-done.1
  21.1 3.5 %collective-permute-start.2 = (bf16[4,16,768]{2,1,0:T(8,128)(2,1)S(1)}, bf16[4,16,768]{2,1,0:T(8,128)(2,1)S(1)}, u32[]{:S(2)}, u32[]{:S(2)}) collective-permute-start(bf16[4,16,768]{2,1,0:T(8,128)(2,1)S(1)} %slice.45), channel_id=1, source_target_pairs={{0,8},{4,12},{8,0},{12,4},{1,9},{5,13},{9,1},{13,5},{2,10},{6,14},... | collective-permute-start | bytes 294920 | tf_op jit(solution)/shard_map/ppermute | solution.py:274
  24.6 3.5 %collective-permute-done.4 = bf16[4,32,768]{2,1,0:T(8,128)(2,1)S(1)} collective-permute-done((bf16[4,32,768]{2,1,0:T(8,128)(2,1)S(1)}, bf16[4,32,768]{2,1,0:T(8,128)(2,1)S(1)}, u32[]{:S(2)}, u32[]{:S(2)}) %collective-permute-start.4) | collective-permute-done | bytes 196640 | tf_op jit(solution)/shard_map/ppermute | solution.py:274
  28.2 2.1 %collective-permute-start.5 = (bf16[4,16,768]{2,1,0:T(8,128)(2,1)S(1)}, bf16[4,16,768]{2,1,0:T(8,128)(2,1)S(1)}, u32[]{:S(2)}, u32[]{:S(2)}) collective-permute-start(bf16[4,16,768]{2,1,0:T(8,128)(2,1)S(1)} %slice.44), channel_id=1, source_target_pairs={{0,8},{4,12},{8,0},{12,4},{1,9},{5,13},{9,1},{13,5},{2,10},{6,14},... | collective-permute-start | bytes 294920 | tf_op jit(solution)/shard_map/ppermute | solution.py:274
  30.3 0.0 collective-permute-done.6
  30.4 1.0 %collective-permute-start.7 = (bf16[4,16,512]{2,1,0:T(8,128)(2,1)S(1)}, bf16[4,16,512]{2,1,0:T(8,128)(2,1)S(1)}, u32[]{:S(2)}, u32[]{:S(2)}) collective-permute-start(bf16[4,16,512]{2,1,0:T(8,128)(2,1)S(1)} %slice.46), channel_id=1, source_target_pairs={{0,8},{4,12},{8,0},{12,4},{1,9},{5,13},{9,1},{13,5},{2,10},{6,14},... | collective-permute-start | bytes 196616 | tf_op jit(solution)/shard_map/ppermute | solution.py:274
  31.4 7.0 %collective-permute-done.7.refs_5_ = bf16[4,16,512]{2,1,0:T(8,128)(2,1)S(1)} collective-permute-done((bf16[4,16,512]{2,1,0:T(8,128)(2,1)S(1)}, bf16[4,16,512]{2,1,0:T(8,128)(2,1)S(1)}, u32[]{:S(2)}, u32[]{:S(2)}) %collective-permute-start.7) | collective-permute-done | bytes 65568 | tf_op jit(solution)/shard_map/ppermute | solution.py:274
  38.4 0.0 collective-permute-done.2.refs_1_
  38.4 0.0 collective-permute-done.5.refs_3_
  38.4 0.0 copy-done
  38.4 0.8 %gated.1 = bf16[4,16,2048]{2,1,0:T(8,128)(2,1)} custom-call(bf16[4,16,2048]{2,1,0:T(8,128)(2,1)S(1)} %copy-done, f32[4,16,768]{2,1,0:T(8,128)S(1)} %slice.35.refs_0_, bf16[4,16,768]{2,1,0:T(8,128)(2,1)S(1)} %collective-permute-done.2.refs_1_, f32[4,16,768]{2,1,0:T(8,128)S(1)} %slice.37.refs_2_, bf16[4,16,768]{2,1,0:T(8,128)(2,1)S(1)} %collective-permute-done.5.refs_3_, ...), custom_call_target="tpu_custom_call" | custom-call | tf_op jit(solution)/shard_map/gated/pallas_call | solution.py:249
  (9 shorter events, 0.2 us)
Async XLA Ops:
  0.9 7.7 %collective-permute-start = (bf16[64,768]{1,0:T(8,128)(2,1)S(1)}, bf16[64,768]{1,0:T(8,128)(2,1)S(1)}, u32[]{:S(2)}, u32[]{:S(2)}) collective-permute-start(bf16[64,768]{1,0:T(8,128)(2,1)S(1)} %slice.27), channel_id=1, source_target_pairs={{4,0},{8,4},{12,8},{5,1},{9,5},{13,9},{6,2},{10,6},{14,10},{7,3},{... | collective-permute-start | bytes 294920 | tf_op jit(solution)/shard_map/ppermute | solution.py:300
  3.1 11.0 %collective-permute-start.3 = (bf16[64,1280]{1,0:T(8,128)(2,1)S(1)}, bf16[64,1280]{1,0:T(8,128)(2,1)S(1)}, u32[]{:S(2)}, u32[]{:S(2)}) collective-permute-start(bf16[64,1280]{1,0:T(8,128)(2,1)S(1)} %slice.30), channel_id=1, source_target_pairs={{4,0},{8,4},{12,8},{5,1},{9,5},{13,9},{6,2},{10,6},{14,10},{7,3},{... | collective-permute-start | bytes 491528 | tf_op jit(solution)/shard_map/ppermute | solution.py:300
  11.7 9.4 %collective-permute-start.1 = (bf16[4,32,768]{2,1,0:T(8,128)(2,1)S(1)}, bf16[4,32,768]{2,1,0:T(8,128)(2,1)S(1)}, u32[]{:S(2)}, u32[]{:S(2)}) collective-permute-start(bf16[4,32,768]{2,1,0:T(8,128)(2,1)S(1)} %get-tuple-element.24), channel_id=1, source_target_pairs={{0,4},{4,0},{8,12},{12,8},{1,5},{5,1},{9,13},{13,9},{2,6},{6,2},{1... | collective-permute-start | bytes 589832 | tf_op jit(solution)/shard_map/ppermute | solution.py:274
  16.1 14.2 %collective-permute-start.6 = (bf16[4,32,512]{2,1,0:T(8,128)(2,1)S(1)}, bf16[4,32,512]{2,1,0:T(8,128)(2,1)S(1)}, u32[]{:S(2)}, u32[]{:S(2)}) collective-permute-start(bf16[4,32,512]{2,1,0:T(8,128)(2,1)S(1)} %get-tuple-element.30), channel_id=1, source_target_pairs={{0,4},{4,0},{8,12},{12,8},{1,5},{5,1},{9,13},{13,9},{2,6},{6,2},{1... | collective-permute-start | bytes 393224 | tf_op jit(solution)/shard_map/ppermute | solution.py:274
  19.4 19.0 %copy-start = (bf16[4,16,2048]{2,1,0:T(8,128)(2,1)S(1)}, bf16[4,16,2048]{2,1,0:T(8,128)(2,1)}, u32[]{:S(2)}) copy-start(bf16[4,16,2048]{2,1,0:T(8,128)(2,1)} %gate.1) | copy-start | bytes 786436
  19.4 8.8 %collective-permute-start.4 = (bf16[4,32,768]{2,1,0:T(8,128)(2,1)S(1)}, bf16[4,32,768]{2,1,0:T(8,128)(2,1)S(1)}, u32[]{:S(2)}, u32[]{:S(2)}) collective-permute-start(bf16[4,32,768]{2,1,0:T(8,128)(2,1)S(1)} %get-tuple-element.28), channel_id=1, source_target_pairs={{0,4},{4,0},{8,12},{12,8},{1,5},{5,1},{9,13},{13,9},{2,6},{6,2},{1... | collective-permute-start | bytes 589832 | tf_op jit(solution)/shard_map/ppermute | solution.py:274
  21.1 17.3 %collective-permute-start.2 = (bf16[4,16,768]{2,1,0:T(8,128)(2,1)S(1)}, bf16[4,16,768]{2,1,0:T(8,128)(2,1)S(1)}, u32[]{:S(2)}, u32[]{:S(2)}) collective-permute-start(bf16[4,16,768]{2,1,0:T(8,128)(2,1)S(1)} %slice.45), channel_id=1, source_target_pairs={{0,8},{4,12},{8,0},{12,4},{1,9},{5,13},{9,1},{13,5},{2,10},{6,14},... | collective-permute-start | bytes 294920 | tf_op jit(solution)/shard_map/ppermute | solution.py:274
  28.2 10.2 %collective-permute-start.5 = (bf16[4,16,768]{2,1,0:T(8,128)(2,1)S(1)}, bf16[4,16,768]{2,1,0:T(8,128)(2,1)S(1)}, u32[]{:S(2)}, u32[]{:S(2)}) collective-permute-start(bf16[4,16,768]{2,1,0:T(8,128)(2,1)S(1)} %slice.44), channel_id=1, source_target_pairs={{0,8},{4,12},{8,0},{12,4},{1,9},{5,13},{9,1},{13,5},{2,10},{6,14},... | collective-permute-start | bytes 294920 | tf_op jit(solution)/shard_map/ppermute | solution.py:274
  30.4 8.0 %collective-permute-start.7 = (bf16[4,16,512]{2,1,0:T(8,128)(2,1)S(1)}, bf16[4,16,512]{2,1,0:T(8,128)(2,1)S(1)}, u32[]{:S(2)}, u32[]{:S(2)}) collective-permute-start(bf16[4,16,512]{2,1,0:T(8,128)(2,1)S(1)} %slice.46), channel_id=1, source_target_pairs={{0,8},{4,12},{8,0},{12,4},{1,9},{5,13},{9,1},{13,5},{2,10},{6,14},... | collective-permute-start | bytes 196616 | tf_op jit(solution)/shard_map/ppermute | solution.py:274

commit v6 on v5

--- a/solution.py
+++ b/solution.py
@@ -12,7 +12,7 @@
 LANES = 256
 BLOCK = 128
 CHUNKS = 3
-GROUP = 16
+GROUP = 32
 
 
 def tables(block, new):
@@ -160,6 +160,33 @@
 
 def in_hbm(*arrays):
     return [pltpu.with_memory_space_constraint(a, pltpu.HBM) for a in arrays]
+
+
+def cut_body(taps, *refs):
+    pieces, done = refs[:-1], refs[-1]
+    moves = []
+    start = 0
+    for piece in pieces:
+        rows, width = piece.shape
+        source = taps.at[pl.ds(0, rows), pl.ds(start, width)]
+        moves.append(pltpu.make_async_copy(source, piece, done.at[len(moves)]))
+        start += width
+    for move in moves:
+        move.start()
+    for move in moves:
+        move.wait()
+
+
+def cut(taps, rows, widths):
+    return pl.pallas_call(
+        cut_body,
+        in_specs=[pl.BlockSpec(memory_space=pltpu.HBM)],
+        out_specs=[pl.BlockSpec(memory_space=pltpu.VMEM)] * len(widths),
+        out_shape=[pltpu.VMEM((rows, width), taps.dtype) for width in widths],
+        scratch_shapes=[pltpu.SemaphoreType.DMA((len(widths),))],
+        compiler_params=pltpu.CompilerParams(vmem_limit_bytes=16 << 20),
+        name="cut",
+    )(*in_hbm(taps))
 
 
 def stage(meta, history, taps, *rest, tiles):
@@ -295,9 +322,10 @@
     sizes = chunk_tiles(total)
     toward = [(source, source - 1) for source in range(1, ranks)]
     split = sizes[0] * LANES
+    widths = [split, channels - split] if split < channels else [split]
     rims = []
-    for part in (slice(0, split), slice(split, None)):
-        rims.append(lax.ppermute(filter_taps[:new, part], "hist", toward))
+    for part in cut(filter_taps, new, widths):
+        rims.append(lax.ppermute(part, "hist", toward))
     gain = skip_gain[None, :]
     staged = stage(meta, history, filter_taps, gain, fwd, back, tiles=sizes[0])
     chunks = []

time: 39.4 us -> 38.8 us (0.985)
  local copies, waits for them, and re-layouts: 1.91 us -> 0.08 us
  waiting for transfers between devices: 12.4 us -> 13.8 us
  starting transfers between devices: 13.8 us -> 12.7 us
  Pallas kernels: 10.8 us -> 11.8 us
    slice x2 -> x0, local copies, waits for them, and re-layouts: 1.83 us -> none  [body(): rims.append(lax.ppermute(filter_taps[:new, part], 'hist', toward))]
    ppermute x2, waiting for transfers between devices: 1.91 us -> 3.01 us  [body(): rims.append(lax.ppermute(part, 'hist', toward))]
    ppermute x6, starting transfers between devices: 11.2 us -> 10.1 us  [exchange(): return lax.ppermute(value, 'hist', [(z, z ^ bit) for z in range(ranks)])]
    pallas_call x0 -> x1, Pallas kernels: none -> 0.98 us  [cut(): pl.pallas_call(cut_body, in_specs=[pl.BlockSpec(memory_space=pltpu.HBM)],...]
  transfers between devices with their start and end apart: 8 -> 8, of which waited for: 3 -> 3; matrix products, arithmetic and copies ran while one was open for 3% -> 1% of each run, Pallas kernels for 26% -> 26%
where the time goes in v6:
time: 38.8 us; the launch traced here: 38.6 us
  waiting for transfers between devices  13.8 us (36%)
  starting transfers between devices  12.7 us (33%)
  Pallas kernels  11.8 us (30%)
    ppermute x6, waiting for transfers between devices, exchange(): return lax.ppermute(value, 'hist', [(z, z ^ bit) for z in range(ranks)])  10.8 us
    ppermute x6, starting transfers between devices, exchange(): return lax.ppermute(value, 'hist', [(z, z ^ bit) for z in range(ranks)])  10.1 us
    pallas_call x3, Pallas kernels, conv_chunk(): pl.pallas_call(functools.partial(conv_body, first=first, tiles=tiles, bas...  7.71 us
    ppermute x2, waiting for transfers between devices, body(): rims.append(lax.ppermute(part, 'hist', toward))  3.01 us
    ppermute x2, starting transfers between devices, body(): rims.append(lax.ppermute(part, 'hist', toward))  2.58 us
    pallas_call x1, Pallas kernels, stage(): pl.pallas_call(functools.partial(stage_body, tiles=tiles), in_specs=[pl.B...  2.3 us
    pallas_call x1, Pallas kernels, cut(): pl.pallas_call(cut_body, in_specs=[pl.BlockSpec(memory_space=pltpu.HBM)],...  0.98 us
    pallas_call x1, Pallas kernels, gated(): pl.pallas_call(functools.partial(gate_body, counts=counts), in_specs=[vme...  0.79 us
  transfers between devices with their start and end apart: 8, of which 3 were waited for; matrix products, arithmetic and copies ran while one was open for 1% of the time, Pallas kernels for 26%

profile of v6, /device:TPU:0, one launch (start us, length us, event | category | flops | bytes accessed | tf_op | source)
XLA Modules:
  0.0 38.6 jit_solution(13451603997946149053)
XLA Ops:
  0.0 1.0 %cut.1 = (bf16[64,768]{1,0:T(8,128)(2,1)S(1)}, bf16[64,1280]{1,0:T(8,128)(2,1)S(1)}) custom-call(bf16[512,2048]{1,0:T(8,128)(2,1)} %refs_1_.3), custom_call_target="tpu_custom_call" | custom-call | tf_op jit(solution)/shard_map/cut/pallas_call | solution.py:181
  1.0 1.3 %collective-permute-start = (bf16[64,768]{1,0:T(8,128)(2,1)S(1)}, bf16[64,768]{1,0:T(8,128)(2,1)S(1)}, u32[]{:S(2)}, u32[]{:S(2)}) collective-permute-start(bf16[64,768]{1,0:T(8,128)(2,1)S(1)} %get-tuple-element.25), channel_id=1, source_target_pairs={{4,0},{8,4},{12,8},{5,1},{9,5},{13,9},{6,2},{10,6},{14,10},{7,3},{... | collective-permute-start | bytes 294920 | tf_op jit(solution)/shard_map/ppermute | solution.py:328
  2.3 1.3 %collective-permute-start.3 = (bf16[64,1280]{1,0:T(8,128)(2,1)S(1)}, bf16[64,1280]{1,0:T(8,128)(2,1)S(1)}, u32[]{:S(2)}, u32[]{:S(2)}) collective-permute-start(bf16[64,1280]{1,0:T(8,128)(2,1)S(1)} %get-tuple-element.30), channel_id=1, source_target_pairs={{4,0},{8,4},{12,8},{5,1},{9,5},{13,9},{6,2},{10,6},{14,10},{7,3},{... | collective-permute-start | bytes 491528 | tf_op jit(solution)/shard_map/ppermute | solution.py:328
  3.6 2.3 %stage.1 = (bf16[4,512,768]{2,1,0:T(8,128)(2,1)S(1)}, bf16[512,768]{1,0:T(8,128)(2,1)S(1)}, f32[1,2048]{1,0:T(1,128)S(1)}, bf16[192,192]{1,0:T(8,128)(2,1)S(1)}, bf16[4,64,192]{2,1,0:T(8,128)(2,1)S(1)}) custom-call(s32[1]{0:T(128)} %bitcast.meta, bf16[4,512,2048]{2,1,0:T(8,128)(2,1)} %refs_0_.3, bf16[512,2048]{1,0:T(8,128)(2,1)} %refs_1_.3, ...), custom_call_target="tpu_custom_call" | custom-call | tf_op jit(solution)/shard_map/stage/pallas_call | solution.py:196
  5.9 3.0 %collective-permute-done.rim = bf16[64,768]{1,0:T(8,128)(2,1)S(1)} collective-permute-done((bf16[64,768]{1,0:T(8,128)(2,1)S(1)}, bf16[64,768]{1,0:T(8,128)(2,1)S(1)}, u32[]{:S(2)}, u32[]{:S(2)}) %collective-permute-start) | collective-permute-done | bytes 98336 | tf_op jit(solution)/shard_map/ppermute | solution.py:328
  8.9 3.0 %conv_chunk.3 = (f32[4,32,768]{2,1,0:T(8,128)S(1)}, bf16[4,32,768]{2,1,0:T(8,128)(2,1)S(1)}, bf16[4,512,1280]{2,1,0:T(8,128)(2,1)S(1)}, bf16[512,1280]{1,0:T(8,128)(2,1)S(1)}) custom-call(s32[1]{0:T(128)} %bitcast.meta, bf16[4,512,768]{2,1,0:T(8,128)(2,1)S(1)} %get-tuple-element.20.hist, bf16[512,768]{1,0:T(8,128)(2,1)S(1)} %get-tuple-element.21.taps, ...), custom_call_target="tpu_custom_call" | custom-call | flops 754974720 | bytes 3932160 | tf_op jit(solution)/shard_map/conv_chunk/pallas_call | solution.py:240
  11.9 2.0 %collective-permute-start.1 = (bf16[4,32,768]{2,1,0:T(8,128)(2,1)S(1)}, bf16[4,32,768]{2,1,0:T(8,128)(2,1)S(1)}, u32[]{:S(2)}, u32[]{:S(2)}) collective-permute-start(bf16[4,32,768]{2,1,0:T(8,128)(2,1)S(1)} %get-tuple-element.27), channel_id=1, source_target_pairs={{0,4},{4,0},{8,12},{12,8},{1,5},{5,1},{9,13},{13,9},{2,6},{6,2},{1... | collective-permute-start | bytes 589832 | tf_op jit(solution)/shard_map/ppermute | solution.py:301
  13.9 0.0 collective-permute-done.3.rim
  13.9 1.9 %conv_chunk.5 = (f32[4,32,512]{2,1,0:T(8,128)S(1)}, bf16[4,32,512]{2,1,0:T(8,128)(2,1)S(1)}) custom-call(s32[1]{0:T(128)} %bitcast.meta, bf16[4,512,1280]{2,1,0:T(8,128)(2,1)S(1)} %get-tuple-element.28.hist, bf16[512,1280]{1,0:T(8,128)(2,1)S(1)} %get-tuple-element.29.taps, f32[1,2048]{1,0:T(1,128)S(1)} %get-tuple-element.22.gain, ...), custom_call_target="tpu_custom_call" | custom-call | flops 503316480 | bytes 2621440 | tf_op jit(solution)/shard_map/conv_chunk/pallas_call | solution.py:240
  15.8 0.2 collective-permute-start.6
  16.0 2.8 %conv_chunk.4 = (f32[4,32,768]{2,1,0:T(8,128)S(1)}, bf16[4,32,768]{2,1,0:T(8,128)(2,1)S(1)}) custom-call(s32[1]{0:T(128)} %bitcast.meta, bf16[4,512,1280]{2,1,0:T(8,128)(2,1)S(1)} %get-tuple-element.28.hist, bf16[512,1280]{1,0:T(8,128)(2,1)S(1)} %get-tuple-element.29.taps, f32[1,2048]{1,0:T(1,128)S(1)} %get-tuple-element.22.gain, ...), custom_call_target="tpu_custom_call" | custom-call | flops 754974720 | bytes 3932160 | tf_op jit(solution)/shard_map/conv_chunk/pallas_call | solution.py:240
  18.8 0.0 copy-start
  18.8 1.9 %collective-permute-start.4 = (bf16[4,32,768]{2,1,0:T(8,128)(2,1)S(1)}, bf16[4,32,768]{2,1,0:T(8,128)(2,1)S(1)}, u32[]{:S(2)}, u32[]{:S(2)}) collective-permute-start(bf16[4,32,768]{2,1,0:T(8,128)(2,1)S(1)} %get-tuple-element.32), channel_id=1, source_target_pairs={{0,4},{4,0},{8,12},{12,8},{1,5},{5,1},{9,13},{13,9},{2,6},{6,2},{1... | collective-permute-start | bytes 589832 | tf_op jit(solution)/shard_map/ppermute | solution.py:301
  20.8 0.0 collective-permute-done.1
  20.8 3.0 %collective-permute-start.2 = (bf16[4,16,768]{2,1,0:T(8,128)(2,1)S(1)}, bf16[4,16,768]{2,1,0:T(8,128)(2,1)S(1)}, u32[]{:S(2)}, u32[]{:S(2)}) collective-permute-start(bf16[4,16,768]{2,1,0:T(8,128)(2,1)S(1)} %slice.37), channel_id=1, source_target_pairs={{0,8},{4,12},{8,0},{12,4},{1,9},{5,13},{9,1},{13,5},{2,10},{6,14},... | collective-permute-start | bytes 294920 | tf_op jit(solution)/shard_map/ppermute | solution.py:301
  23.8 3.5 %collective-permute-done.4 = bf16[4,32,768]{2,1,0:T(8,128)(2,1)S(1)} collective-permute-done((bf16[4,32,768]{2,1,0:T(8,128)(2,1)S(1)}, bf16[4,32,768]{2,1,0:T(8,128)(2,1)S(1)}, u32[]{:S(2)}, u32[]{:S(2)}) %collective-permute-start.4) | collective-permute-done | bytes 196640 | tf_op jit(solution)/shard_map/ppermute | solution.py:301
  27.4 2.2 %collective-permute-start.5 = (bf16[4,16,768]{2,1,0:T(8,128)(2,1)S(1)}, bf16[4,16,768]{2,1,0:T(8,128)(2,1)S(1)}, u32[]{:S(2)}, u32[]{:S(2)}) collective-permute-start(bf16[4,16,768]{2,1,0:T(8,128)(2,1)S(1)} %slice.36), channel_id=1, source_target_pairs={{0,8},{4,12},{8,0},{12,4},{1,9},{5,13},{9,1},{13,5},{2,10},{6,14},... | collective-permute-start | bytes 294920 | tf_op jit(solution)/shard_map/ppermute | solution.py:301
  29.6 0.0 collective-permute-done.6
  29.7 0.8 %collective-permute-start.7 = (bf16[4,16,512]{2,1,0:T(8,128)(2,1)S(1)}, bf16[4,16,512]{2,1,0:T(8,128)(2,1)S(1)}, u32[]{:S(2)}, u32[]{:S(2)}) collective-permute-start(bf16[4,16,512]{2,1,0:T(8,128)(2,1)S(1)} %slice.38), channel_id=1, source_target_pairs={{0,8},{4,12},{8,0},{12,4},{1,9},{5,13},{9,1},{13,5},{2,10},{6,14},... | collective-permute-start | bytes 196616 | tf_op jit(solution)/shard_map/ppermute | solution.py:301
  30.6 7.2 %collective-permute-done.7.refs_5_ = bf16[4,16,512]{2,1,0:T(8,128)(2,1)S(1)} collective-permute-done((bf16[4,16,512]{2,1,0:T(8,128)(2,1)S(1)}, bf16[4,16,512]{2,1,0:T(8,128)(2,1)S(1)}, u32[]{:S(2)}, u32[]{:S(2)}) %collective-permute-start.7) | collective-permute-done | bytes 65568 | tf_op jit(solution)/shard_map/ppermute | solution.py:301
  37.8 0.0 collective-permute-done.2.refs_1_
  37.8 0.0 collective-permute-done.5.refs_3_
  37.8 0.0 copy-done
  37.8 0.8 %gated.1 = bf16[4,16,2048]{2,1,0:T(8,128)(2,1)} custom-call(bf16[4,16,2048]{2,1,0:T(8,128)(2,1)S(1)} %copy-done, f32[4,16,768]{2,1,0:T(8,128)S(1)} %slice.27.refs_0_, bf16[4,16,768]{2,1,0:T(8,128)(2,1)S(1)} %collective-permute-done.2.refs_1_, f32[4,16,768]{2,1,0:T(8,128)S(1)} %slice.29.refs_2_, bf16[4,16,768]{2,1,0:T(8,128)(2,1)S(1)} %collective-permute-done.5.refs_3_, ...), custom_call_target="tpu_custom_call" | custom-call | tf_op jit(solution)/shard_map/gated/pallas_call | solution.py:276
  (9 shorter events, 0.2 us)
Async XLA Ops:
  1.0 7.9 %collective-permute-start = (bf16[64,768]{1,0:T(8,128)(2,1)S(1)}, bf16[64,768]{1,0:T(8,128)(2,1)S(1)}, u32[]{:S(2)}, u32[]{:S(2)}) collective-permute-start(bf16[64,768]{1,0:T(8,128)(2,1)S(1)} %get-tuple-element.25), channel_id=1, source_target_pairs={{4,0},{8,4},{12,8},{5,1},{9,5},{13,9},{6,2},{10,6},{14,10},{7,3},{... | collective-permute-start | bytes 294920 | tf_op jit(solution)/shard_map/ppermute | solution.py:328
  2.3 11.6 %collective-permute-start.3 = (bf16[64,1280]{1,0:T(8,128)(2,1)S(1)}, bf16[64,1280]{1,0:T(8,128)(2,1)S(1)}, u32[]{:S(2)}, u32[]{:S(2)}) collective-permute-start(bf16[64,1280]{1,0:T(8,128)(2,1)S(1)} %get-tuple-element.30), channel_id=1, source_target_pairs={{4,0},{8,4},{12,8},{5,1},{9,5},{13,9},{6,2},{10,6},{14,10},{7,3},{... | collective-permute-start | bytes 491528 | tf_op jit(solution)/shard_map/ppermute | solution.py:328
  11.9 8.8 %collective-permute-start.1 = (bf16[4,32,768]{2,1,0:T(8,128)(2,1)S(1)}, bf16[4,32,768]{2,1,0:T(8,128)(2,1)S(1)}, u32[]{:S(2)}, u32[]{:S(2)}) collective-permute-start(bf16[4,32,768]{2,1,0:T(8,128)(2,1)S(1)} %get-tuple-element.27), channel_id=1, source_target_pairs={{0,4},{4,0},{8,12},{12,8},{1,5},{5,1},{9,13},{13,9},{2,6},{6,2},{1... | collective-permute-start | bytes 589832 | tf_op jit(solution)/shard_map/ppermute | solution.py:301
  15.8 13.8 %collective-permute-start.6 = (bf16[4,32,512]{2,1,0:T(8,128)(2,1)S(1)}, bf16[4,32,512]{2,1,0:T(8,128)(2,1)S(1)}, u32[]{:S(2)}, u32[]{:S(2)}) collective-permute-start(bf16[4,32,512]{2,1,0:T(8,128)(2,1)S(1)} %get-tuple-element.34), channel_id=1, source_target_pairs={{0,4},{4,0},{8,12},{12,8},{1,5},{5,1},{9,13},{13,9},{2,6},{6,2},{1... | collective-permute-start | bytes 393224 | tf_op jit(solution)/shard_map/ppermute | solution.py:301
  18.8 19.0 %copy-start = (bf16[4,16,2048]{2,1,0:T(8,128)(2,1)S(1)}, bf16[4,16,2048]{2,1,0:T(8,128)(2,1)}, u32[]{:S(2)}) copy-start(bf16[4,16,2048]{2,1,0:T(8,128)(2,1)} %gate.1) | copy-start | bytes 786436
  18.8 8.5 %collective-permute-start.4 = (bf16[4,32,768]{2,1,0:T(8,128)(2,1)S(1)}, bf16[4,32,768]{2,1,0:T(8,128)(2,1)S(1)}, u32[]{:S(2)}, u32[]{:S(2)}) collective-permute-start(bf16[4,32,768]{2,1,0:T(8,128)(2,1)S(1)} %get-tuple-element.32), channel_id=1, source_target_pairs={{0,4},{4,0},{8,12},{12,8},{1,5},{5,1},{9,13},{13,9},{2,6},{6,2},{1... | collective-permute-start | bytes 589832 | tf_op jit(solution)/shard_map/ppermute | solution.py:301
  20.8 17.0 %collective-permute-start.2 = (bf16[4,16,768]{2,1,0:T(8,128)(2,1)S(1)}, bf16[4,16,768]{2,1,0:T(8,128)(2,1)S(1)}, u32[]{:S(2)}, u32[]{:S(2)}) collective-permute-start(bf16[4,16,768]{2,1,0:T(8,128)(2,1)S(1)} %slice.37), channel_id=1, source_target_pairs={{0,8},{4,12},{8,0},{12,4},{1,9},{5,13},{9,1},{13,5},{2,10},{6,14},... | collective-permute-start | bytes 294920 | tf_op jit(solution)/shard_map/ppermute | solution.py:301
  27.4 10.4 %collective-permute-start.5 = (bf16[4,16,768]{2,1,0:T(8,128)(2,1)S(1)}, bf16[4,16,768]{2,1,0:T(8,128)(2,1)S(1)}, u32[]{:S(2)}, u32[]{:S(2)}) collective-permute-start(bf16[4,16,768]{2,1,0:T(8,128)(2,1)S(1)} %slice.36), channel_id=1, source_target_pairs={{0,8},{4,12},{8,0},{12,4},{1,9},{5,13},{9,1},{13,5},{2,10},{6,14},... | collective-permute-start | bytes 294920 | tf_op jit(solution)/shard_map/ppermute | solution.py:301
  29.7 8.1 %collective-permute-start.7 = (bf16[4,16,512]{2,1,0:T(8,128)(2,1)S(1)}, bf16[4,16,512]{2,1,0:T(8,128)(2,1)S(1)}, u32[]{:S(2)}, u32[]{:S(2)}) collective-permute-start(bf16[4,16,512]{2,1,0:T(8,128)(2,1)S(1)} %slice.38), channel_id=1, source_target_pairs={{0,8},{4,12},{8,0},{12,4},{1,9},{5,13},{9,1},{13,5},{2,10},{6,14},... | collective-permute-start | bytes 196616 | tf_op jit(solution)/shard_map/ppermute | solution.py:301
